TPU v7x, 32 devices: a whole 2x2x4 slice. The times are simulated.
32 devices in a mesh: gx: 4 (over y, x), gy: 4 (over z), ma: 2 (over core).
Axes of the slice: x: 2, y: 2, z: 4, core: 2. Of those that a mesh axis runs over, the one named last changes fastest.
Arguments:
- alpha_fields: bfloat16 [80, 2, 512, 512], P('ma', None, 'gy', 'gx'), may hold values from -6 to 6
- member_perts: bfloat16 [80, 2, 512, 512], P('ma', None, 'gy', 'gx'), may hold values from -0.625 to 0.625
- band_widths: int32 [2], replicated, may hold values from 2 to 8
- lat_index: int32 [1024], P('gy'), may hold values from 0 to 510, as said below
- lat_weight: float32 [1024], P('gy'), may hold values from 0 to 1
- lon_index: int32 [1024], P('gx'), may hold values from 0 to 511, as said below
- lon_weight: float32 [1024], P('gx'), may hold values from 0 to 1
- innovation: float32 [2, 1024, 1024], P(None, 'gy', 'gx'), may hold values from -6 to 6
- obs_weight: float32 [2, 1024, 1024], P(None, 'gy', 'gx'), may hold values from 0.1 to 1
Outputs:
- increment: float32 [2, 1024, 1024], P(None, 'gy', 'gx')
- gradient: float32 [80, 2, 512, 512], P('ma', None, 'gy', 'gx')
Inputs may be any that keep to these rules, and one draw needn't show every extreme that they name: lat_index[p] is p // 2 - 1 or p // 2, clamped to 0 .. 510. lon_index[q] is q // 2 - 1 or q // 2, taken modulo 512.
All inputs are finite; a program needn't handle non-finite values.
Results may differ from a plain program's by a relative error of at most 0.0003.
Values may be sent and summed in bfloat16 or wider, within the bound.
No kernel may reach another device: no remote copies, remote signals or barrier semaphores. Data moves between devices by JAX's collectives and lax.ppermute only.
A program may use at most 128 MiB of HBM per device.

v0:
```python
import jax
import jax.numpy as jnp
from jax import lax
from jax.sharding import PartitionSpec as P

HB = 8


def padded_2(block, sides, width, periodic):
    for axis, dim in sides:
        count = lax.axis_size(axis)
        forward = [(i, i + 1) for i in range(count - 1)]
        if periodic:
            forward.append((count - 1, 0))
        backward = [(target, source) for source, target in forward]
        low = lax.ppermute(
            lax.slice_in_dim(block, block.shape[dim] - width, None, axis=dim), axis, forward
        )
        high = lax.ppermute(lax.slice_in_dim(block, 0, width, axis=dim), axis, backward)
        block = jnp.concatenate([low, block, high], axis=dim)
    return block


def tap_table(band_widths):
    tap_offsets = jnp.arange(-HB, HB + 1).astype(jnp.float32)
    spread = band_widths.astype(jnp.float32)[:, None]
    shapes = jnp.exp(-tap_offsets[None, :] ** 2 / (2.0 * spread * spread))
    return shapes / jnp.sqrt(jnp.sum(shapes * shapes, axis=1, keepdims=True))


def band_matrix(filter_taps, length):
    row_index = jnp.arange(length + 2 * HB, dtype=jnp.int32)[None, :, None]
    col_index = jnp.arange(length, dtype=jnp.int32)[None, None, :]
    tap_index = jnp.arange(2 * HB + 1, dtype=jnp.int32)[:, None, None]
    onehot = (row_index - col_index == tap_index).astype(jnp.float32)
    return jnp.einsum("ld,dkj->lkj", filter_taps, onehot, precision=lax.Precision.HIGHEST)


def lon_filter(padded, lon_matrix):
    return jnp.einsum("mlik,lkj->mlij", padded, lon_matrix, precision=lax.Precision.HIGHEST)


def lat_local(padded, lat_matrix):
    return jnp.einsum("mlkj,lki->mlij", padded, lat_matrix, precision=lax.Precision.HIGHEST)


def lat_filter(source, lat_matrix):
    padded = padded_2(source, (("gy", 2),), HB, False)
    return lat_local(padded, lat_matrix)


def stencil(relative, weight, length):
    columns = jnp.arange(length, dtype=jnp.int32)[None, :]
    near_cell = (columns == relative[:, None]).astype(jnp.float32)
    next_cell = (columns == relative[:, None] + 1).astype(jnp.float32)
    return (1.0 - weight[:, None]) * near_cell + weight[:, None] * next_cell


def fine_step(coarse, target, weights, lat_map, lon_map):
    framed = padded_2(coarse, (("gx", 2), ("gy", 1)), 1, True)
    by_lat = jnp.einsum("pa,lab->lpb", lat_map, framed, precision=lax.Precision.HIGHEST)
    increment = jnp.einsum("lpb,qb->lpq", by_lat, lon_map, precision=lax.Precision.HIGHEST)
    misfit = weights * (increment - target)
    lon_back = jnp.einsum("lpq,qb->lpb", misfit, lon_map, precision=lax.Precision.HIGHEST)
    restricted = jnp.einsum("pa,lpb->lab", lat_map, lon_back, precision=lax.Precision.HIGHEST)
    lon_edges = jnp.stack((restricted[:, :, 0], restricted[:, :, -1]), axis=2)
    received = padded_2(lon_edges, (("gx", 2),), 1, True)
    folded = restricted[:, :, 1:-1]
    folded = folded.at[:, :, 0].add(received[:, :, 0]).at[:, :, -1].add(received[:, :, 3])
    lat_edges = jnp.stack((folded[:, 0, :], folded[:, -1, :]), axis=1)
    arrived = padded_2(lat_edges, (("gy", 1),), 1, False)
    residual = folded[:, 1:-1, :]
    residual = residual.at[:, 0, :].add(arrived[:, 0, :]).at[:, -1, :].add(arrived[:, 3, :])
    return (increment, residual)


def body(
    alpha_fields,
    member_perts,
    band_widths,
    lat_index,
    lat_weight,
    lon_index,
    lon_weight,
    innovation,
    obs_weight,
):
    shard_lat = alpha_fields.shape[2]
    shard_lon = alpha_fields.shape[3]
    filter_taps = tap_table(band_widths)
    lon_matrix = band_matrix(filter_taps, shard_lon)
    lat_matrix = band_matrix(filter_taps, shard_lat)
    alpha_wide = padded_2(alpha_fields, (("gx", 3),), HB, True)
    localized = lat_filter(lon_filter(alpha_wide.astype(jnp.float32), lon_matrix), lat_matrix)
    local_sum = jnp.sum(member_perts.astype(jnp.float32) * localized, axis=0)
    lat_start = lax.axis_index("gy") * shard_lat
    lon_start = lax.axis_index("gx") * shard_lon
    lon_total = shard_lon * lax.axis_size("gx")
    lat_map = stencil(lat_index - lat_start + 1, lat_weight, shard_lat + 2)
    lon_map = stencil(
        jnp.remainder(lon_index - lon_start + 1, lon_total), lon_weight, shard_lon + 2
    )
    level_share = lax.psum_scatter(local_sum, "ma", scatter_dimension=0, tiled=True)
    levels_here = level_share.shape[0]
    first_level = lax.axis_index("ma") * levels_here
    own_target = lax.dynamic_slice_in_dim(innovation, first_level, levels_here, 0)
    own_weight = lax.dynamic_slice_in_dim(obs_weight, first_level, levels_here, 0)
    part_increment, part_residual = fine_step(level_share, own_target, own_weight, lat_map, lon_map)
    increment = lax.all_gather(part_increment, "ma", axis=0, tiled=True)
    coarse_residual = lax.all_gather(part_residual, "ma", axis=0, tiled=True)
    products = padded_2(
        member_perts.astype(jnp.float32) * coarse_residual[None], (("gx", 3),), HB, True
    )
    gradient = alpha_fields.astype(jnp.float32) + lat_filter(
        lon_filter(products, lon_matrix), lat_matrix
    )
    return (increment, gradient)


def solution(mesh):
    placed = (
        P("ma", None, "gy", "gx"),
        P("ma", None, "gy", "gx"),
        P(),
        P("gy"),
        P("gy"),
        P("gx"),
        P("gx"),
        P(None, "gy", "gx"),
        P(None, "gy", "gx"),
    )
    return jax.shard_map(
        body,
        mesh=mesh,
        in_specs=placed,
        out_specs=(P(None, "gy", "gx"), P("ma", None, "gy", "gx")),
        check_vma=False,
    )
```

profile of v0, /device:TPU:0, one launch (start us, length us, event | category | flops | bytes accessed | tf_op | source)
XLA Modules:
  0.0 171.9 jit_solution(5458942289306915994)
XLA Ops:
  7.2 3.3 %copy.24 = bf16[40,2,128,128]{2,3,0,1:T(8,128)(2,1)S(1)} copy(bf16[40,2,128,128]{3,2,1,0:T(8,128)(2,1)} %param.17) | data formatting | bytes 5242880 | tf_op args[0]
  10.6 3.0 %collective-permute-start = (bf16[40,2,128,8]{2,3,0,1:T(8,128)(2,1)S(1)}, bf16[40,2,128,8]{2,3,0,1:T(8,128)(2,1)S(1)}, u32[]{:S(2)}, u32[]{:S(2)}) collective-permute-start(bf16[40,2,128,8]{2,3,0,1:T(8,128)(2,1)S(1)} %get-tuple-element.62), channel_id=1, source_target_pairs={{0,8},{8,16},{16,24},{24,0},{1,9},{9,17},{17,25},{25,1},{2,10},{10... | collective-permute-start | bytes 491528 | tf_op jit(solution)/shard_map/ppermute | solution.py:16
  13.6 1.0 collective-permute-start.1
  15.5 4.1 %collective-permute-done = bf16[40,2,128,8]{2,3,0,1:T(8,128)(2,1)S(1)} collective-permute-done((bf16[40,2,128,8]{2,3,0,1:T(8,128)(2,1)S(1)}, bf16[40,2,128,8]{2,3,0,1:T(8,128)(2,1)S(1)}, u32[]{:S(2)}, u32[]{:S(2)}) %collective-permute-start) | collective-permute-done | bytes 163872 | tf_op jit(solution)/shard_map/ppermute | solution.py:16
  19.6 2.9 %collective-permute-done.1 = bf16[40,2,128,8]{2,3,0,1:T(8,128)(2,1)S(1)} collective-permute-done((bf16[40,2,128,8]{2,3,0,1:T(8,128)(2,1)S(1)}, bf16[40,2,128,8]{2,3,0,1:T(8,128)(2,1)S(1)}, u32[]{:S(2)}, u32[]{:S(2)}) %collective-permute-start.1) | collective-permute-done | bytes 163872 | tf_op jit(solution)/shard_map/ppermute | solution.py:19
  22.5 5.5 %fusion.25 = f32[40,2,128,128]{3,2,0,1:T(8,128)S(1)} fusion(bf16[40,2,128,8]{2,3,0,1:T(8,128)(2,1)S(1)} %collective-permute-done.1, bf16[40,2,128,128]{2,3,0,1:T(8,128)(2,1)S(1)} %copy.24, bf16[40,2,128,8]{2,3,0,1:T(8,128)(2,1)S(1)} %collective-permute-done, f32[2,144,128,1]{2,0,1,3:T(2,128)S(1)} %fusion.36), kind=kOutput, calls=%fused_computation.28 | convolution fusion | flops 2273771520 | bytes 8339456 | tf_op jit(solution)/shard_map/mlik,lkj->mlij/dot_general | solution.py:40
  28.0 2.3 %copy-done.2 = f32[40,2,128,128]{3,2,0,1:T(8,128)} copy-done((f32[40,2,128,128]{3,2,0,1:T(8,128)}, f32[40,2,128,128]{3,2,0,1:T(8,128)S(1)}, u32[]{:S(2)}) %copy-start.2) | copy-done | bytes 5242904
  30.4 3.5 %collective-permute-start.2 = (f32[40,2,8,128]{3,2,0,1:T(8,128)S(1)}, f32[40,2,8,128]{3,2,0,1:T(8,128)S(1)}, u32[]{:S(2)}, u32[]{:S(2)}) collective-permute-start(f32[40,2,8,128]{3,2,0,1:T(8,128)S(1)} %get-tuple-element.60), channel_id=1, source_target_pairs={{0,2},{2,4},{4,6},{1,3},{3,5},{5,7},{8,10},{10,12},{12,14},{9,11},... | collective-permute-start | bytes 983048 | tf_op jit(solution)/shard_map/ppermute | solution.py:16
  33.9 1.5 collective-permute-start.3
  35.4 4.5 %collective-permute-done.2 = f32[40,2,8,128]{3,2,0,1:T(8,128)S(1)} collective-permute-done((f32[40,2,8,128]{3,2,0,1:T(8,128)S(1)}, f32[40,2,8,128]{3,2,0,1:T(8,128)S(1)}, u32[]{:S(2)}, u32[]{:S(2)}) %collective-permute-start.2) | collective-permute-done | bytes 327712 | tf_op jit(solution)/shard_map/ppermute | solution.py:16
  40.0 4.1 %collective-permute-done.3 = f32[40,2,8,128]{3,2,0,1:T(8,128)S(1)} collective-permute-done((f32[40,2,8,128]{3,2,0,1:T(8,128)S(1)}, f32[40,2,8,128]{3,2,0,1:T(8,128)S(1)}, u32[]{:S(2)}, u32[]{:S(2)}) %collective-permute-start.3) | collective-permute-done | bytes 327712 | tf_op jit(solution)/shard_map/ppermute | solution.py:19
  44.1 9.6 %fusion.18 = f32[2,128,128]{2,1,0:T(8,128)} fusion(f32[40,2,8,128]{3,2,0,1:T(8,128)S(1)} %collective-permute-done.3, f32[40,2,128,128]{3,2,0,1:T(8,128)} %copy-done.2, f32[40,2,8,128]{3,2,0,1:T(8,128)S(1)} %collective-permute-done.2, bf16[40,2,128,128]{3,2,1,0:T(8,128)(2,1)} %param.18, f32[2,144,128,1]{2,0,1,3:T(2,128)S(1)} %fusion.36), kind=kOutput, calls=%fused_computation.20 | convolution fusion | flops 2271772672 | bytes 8798208 | tf_op jit(solution)/shard_map/mlkj,lki->mlij/dot_general | solution.py:44
  53.8 6.9 %reduce-scatter.2.cloned.1.call-done = f32[1,128,128]{2,1,0:T(8,128)} async-done(((f32[2,128,128]{2,1,0:T(8,128)}), f32[1,128,128]{2,1,0:T(8,128)}) %reduce-scatter.2.cloned.1.call-update) | async-done | bytes 65552 | tf_op jit(solution)/shard_map/reduce_scatter | solution.py:103
  60.7 1.0 fusion.97
  61.7 1.7 %collective-permute-start.4 = (f32[1,128,1]{2,1,0:T(8,128)S(1)}, f32[1,128,1]{2,1,0:T(8,128)S(1)}, u32[]{:S(2)}, u32[]{:S(2)}) collective-permute-start(f32[1,128,1]{2,1,0:T(8,128)S(1)} %get-tuple-element.70), channel_id=1, source_target_pairs={{0,8},{8,16},{16,24},{24,0},{1,9},{9,17},{17,25},{25,1},{2,10},{10... | collective-permute-start | bytes 1544 | tf_op jit(solution)/shard_map/ppermute | solution.py:16
  63.5 1.2 collective-permute-start.5
  64.7 2.3 %collective-permute-done.4 = f32[1,128,1]{2,1,0:T(8,128)S(1)} collective-permute-done((f32[1,128,1]{2,1,0:T(8,128)S(1)}, f32[1,128,1]{2,1,0:T(8,128)S(1)}, u32[]{:S(2)}, u32[]{:S(2)}) %collective-permute-start.4) | collective-permute-done | bytes 544 | tf_op jit(solution)/shard_map/ppermute | solution.py:16
  67.0 1.7 collective-permute-done.5
  69.4 1.5 collective-permute-start.6
  70.9 2.3 %collective-permute-start.7 = (f32[1,1,130]{2,1,0:T(1,128)S(1)}, f32[1,1,130]{2,1,0:T(1,128)S(1)}, u32[]{:S(2)}, u32[]{:S(2)}) collective-permute-start(f32[1,1,130]{2,1,0:T(1,128)S(1)} %get-tuple-element.65), channel_id=1, source_target_pairs={{2,0},{4,2},{6,4},{0,6},{3,1},{5,3},{7,5},{1,7},{10,8},{12,10},{14... | collective-permute-start | bytes 1568 | tf_op jit(solution)/shard_map/ppermute | solution.py:19
  73.2 1.5 collective-permute-done.6
  74.8 1.5 convolution_bitcast_fusion.1
  76.3 0.8 fusion.44
  77.1 1.6 fusion.38
  79.5 1.5 collective-permute-start.8
  81.0 1.5 collective-permute-start.9
  82.5 1.5 collective-permute-done.8
  84.7 3.1 %collective-permute-start.10 = (f32[1,1,128]{1,2,0:T(8,128)S(1)}, f32[1,1,128]{1,2,0:T(8,128)S(1)}, u32[]{:S(2)}, u32[]{:S(2)}) collective-permute-start(f32[1,1,128]{1,2,0:T(8,128)S(1)} %get-tuple-element.69), channel_id=1, source_target_pairs={{0,2},{2,4},{4,6},{1,3},{3,5},{5,7},{8,10},{10,12},{12,14},{9,11},... | collective-permute-start | bytes 1544 | tf_op jit(solution)/shard_map/ppermute | solution.py:16
  87.9 1.3 collective-permute-start.11
  90.1 4.0 %collective-permute-done.11 = f32[1,1,128]{1,2,0:T(8,128)S(1)} collective-permute-done((f32[1,1,128]{1,2,0:T(8,128)S(1)}, f32[1,1,128]{1,2,0:T(8,128)S(1)}, u32[]{:S(2)}, u32[]{:S(2)}) %collective-permute-start.11) | collective-permute-done | bytes 544 | tf_op jit(solution)/shard_map/ppermute | solution.py:19
  94.6 2.1 %all_gather.7 = f32[2,128,128]{2,1,0:T(8,128)S(1)} all-gather(f32[1,128,128]{2,1,0:T(8,128)S(1)} %copy.30), channel_id=1, replica_groups=mesh['gx'=4,'gy'=4,'ma'=2] {'ma'}, dimensions={0}, use_global_device_ids=true | all-gather | bytes 196608 | tf_op jit(solution)/shard_map/all_gather | solution.py:110
  97.5 5.8 %fusion.92 = (f32[40,2,128,8]{3,2,0,1:T(8,128)}, f32[40,2,128,8]{3,2,0,1:T(8,128)}) fusion(f32[40,2,128,128]{3,2,0,1:T(8,128)S(1)} %convert_multiply_fusion), kind=kLoop, calls=%fused_computation.117 | loop fusion | bytes 1310720 | tf_op jit(solution)/shard_map/slice | solution.py:17
  103.3 3.2 %copy.31 = f32[40,2,128,8]{2,3,1,0:T(8,128)S(1)} copy(f32[40,2,128,8]{3,2,0,1:T(8,128)} %get-tuple-element.58) | data formatting | bytes 655360 | tf_op jit(solution)/shard_map/slice | solution.py:17
  106.5 1.6 collective-permute-start.12
  108.1 3.2 %copy.32 = f32[40,2,128,8]{2,3,1,0:T(8,128)S(1)} copy(f32[40,2,128,8]{3,2,0,1:T(8,128)} %get-tuple-element.59) | data formatting | bytes 655360 | tf_op jit(solution)/shard_map/slice | solution.py:19
  111.3 1.4 collective-permute-start.13
  112.8 5.3 %collective-permute-done.12 = f32[40,2,128,8]{2,3,1,0:T(8,128)S(1)} collective-permute-done((f32[40,2,128,8]{2,3,1,0:T(8,128)S(1)}, f32[40,2,128,8]{2,3,1,0:T(8,128)S(1)}, u32[]{:S(2)}, u32[]{:S(2)}) %collective-permute-start.12) | collective-permute-done | bytes 327712 | tf_op jit(solution)/shard_map/ppermute | solution.py:16
  118.0 3.1 %copy.33 = f32[40,2,128,8]{3,2,0,1:T(8,128)} copy(f32[40,2,128,8]{2,3,1,0:T(8,128)S(1)} %collective-permute-done.12) | data formatting | bytes 655360 | tf_op jit(solution)/shard_map/ppermute | solution.py:16
  121.2 2.1 %collective-permute-done.13 = f32[40,2,128,8]{2,3,1,0:T(8,128)S(1)} collective-permute-done((f32[40,2,128,8]{2,3,1,0:T(8,128)S(1)}, f32[40,2,128,8]{2,3,1,0:T(8,128)S(1)}, u32[]{:S(2)}, u32[]{:S(2)}) %collective-permute-start.13) | collective-permute-done | bytes 327712 | tf_op jit(solution)/shard_map/ppermute | solution.py:19
  123.3 3.1 %copy.34 = f32[40,2,128,8]{3,2,0,1:T(8,128)} copy(f32[40,2,128,8]{2,3,1,0:T(8,128)S(1)} %collective-permute-done.13) | data formatting | bytes 655360 | tf_op jit(solution)/shard_map/ppermute | solution.py:19
  126.5 14.3 %fusion.32 = f32[40,2,128,128]{3,2,0,1:T(8,128)S(1)} fusion(f32[40,2,128,8]{3,2,0,1:T(8,128)} %copy.34, f32[40,2,128,128]{3,2,0,1:T(8,128)} %copy-done, f32[40,2,128,8]{3,2,0,1:T(8,128)} %copy.33, f32[2,144,128,1]{2,0,1,3:T(2,128)S(1)} %fusion.36), kind=kOutput, calls=%fused_computation.29 | convolution fusion | flops 2267873280 | bytes 11288576 | tf_op jit(solution)/shard_map/mlik,lkj->mlij/dot_general | solution.py:40
  140.9 3.7 %collective-permute-start.14 = (f32[40,2,8,128]{3,2,0,1:T(8,128)S(1)}, f32[40,2,8,128]{3,2,0,1:T(8,128)S(1)}, u32[]{:S(2)}, u32[]{:S(2)}) collective-permute-start(f32[40,2,8,128]{3,2,0,1:T(8,128)S(1)} %get-tuple-element.56), channel_id=1, source_target_pairs={{0,2},{2,4},{4,6},{1,3},{3,5},{5,7},{8,10},{10,12},{12,14},{9,11},... | collective-permute-start | bytes 983048 | tf_op jit(solution)/shard_map/ppermute | solution.py:16
  144.6 1.3 collective-permute-start.15
  145.9 2.4 %all-gather = f32[512,256]{1,0:T(8,128)S(1)} all-gather(f32[256,256]{1,0:T(8,128)S(1)} %fusion.44), channel_id=2, replica_groups=mesh['gx'=4,'gy'=4,'ma'=2] {'ma'}, dimensions={0}, use_global_device_ids=true | all-gather | bytes 786432 | tf_op jit(solution)/shard_map/all_gather | solution.py:109
  148.3 2.7 %collective-permute-done.14 = f32[40,2,8,128]{3,2,0,1:T(8,128)S(1)} collective-permute-done((f32[40,2,8,128]{3,2,0,1:T(8,128)S(1)}, f32[40,2,8,128]{3,2,0,1:T(8,128)S(1)}, u32[]{:S(2)}, u32[]{:S(2)}) %collective-permute-start.14) | collective-permute-done | bytes 327712 | tf_op jit(solution)/shard_map/ppermute | solution.py:16
  151.0 4.4 %collective-permute-done.15 = f32[40,2,8,128]{3,2,0,1:T(8,128)S(1)} collective-permute-done((f32[40,2,8,128]{3,2,0,1:T(8,128)S(1)}, f32[40,2,8,128]{3,2,0,1:T(8,128)S(1)}, u32[]{:S(2)}, u32[]{:S(2)}) %collective-permute-start.15) | collective-permute-done | bytes 327712 | tf_op jit(solution)/shard_map/ppermute | solution.py:19
  155.4 5.9 %bitcast_add_fusion = f32[40,2,128,128]{3,2,0,1:T(8,128)S(1)} fusion(bf16[40,2,128,128]{3,2,1,0:T(8,128)(2,1)S(1)} %copy-done.1, f32[40,2,8,128]{3,2,0,1:T(8,128)S(1)} %collective-permute-done.15, f32[40,2,128,128]{3,2,0,1:T(8,128)S(1)} %fusion.32, f32[40,2,8,128]{3,2,0,1:T(8,128)S(1)} %collective-permute-done.14, f32[2,144,128,1]{2,0,1,3:T(2,128)S(1)} %fusion.36), kind=kOutput, calls=%fused_computation.21 | convolution fusion | flops 2270494720 | bytes 13910016 | tf_op jit(solution)/shard_map/mlkj,lki->mlij/dot_general | solution.py:44
  161.3 3.0 %copy.38 = f32[40,2,128,128]{3,2,1,0:T(8,128)} copy(f32[40,2,128,128]{3,2,0,1:T(8,128)S(1)} %bitcast_add_fusion) | data formatting | bytes 10485760
  (52 shorter events, 6.4 us)
Async XLA Ops:
  7.2 7.5 %copy-start.8 = (s32[2]{0:T(128)S(1)}, s32[2]{0:T(128)}, u32[]{:S(2)}) copy-start(s32[2]{0:T(128)} %param.19) | copy-start | bytes 28
  7.2 53.5 %reduce-scatter.2.cloned.1.call-start = ((), (), s32[]{:S(2)}) async-start(), calls=%async_computation.1 | async-start | bytes 196608 | tf_op jit(solution)/shard_map/reduce_scatter | solution.py:103
  10.6 9.0 %collective-permute-start = (bf16[40,2,128,8]{2,3,0,1:T(8,128)(2,1)S(1)}, bf16[40,2,128,8]{2,3,0,1:T(8,128)(2,1)S(1)}, u32[]{:S(2)}, u32[]{:S(2)}) collective-permute-start(bf16[40,2,128,8]{2,3,0,1:T(8,128)(2,1)S(1)} %get-tuple-element.62), channel_id=1, source_target_pairs={{0,8},{8,16},{16,24},{24,0},{1,9},{9,17},{17,25},{25,1},{2,10},{10... | collective-permute-start | bytes 491528 | tf_op jit(solution)/shard_map/ppermute | solution.py:16
  13.6 8.9 %collective-permute-start.1 = (bf16[40,2,128,8]{2,3,0,1:T(8,128)(2,1)S(1)}, bf16[40,2,128,8]{2,3,0,1:T(8,128)(2,1)S(1)}, u32[]{:S(2)}, u32[]{:S(2)}) collective-permute-start(bf16[40,2,128,8]{2,3,0,1:T(8,128)(2,1)S(1)} %get-tuple-element.63), channel_id=1, source_target_pairs={{8,0},{16,8},{24,16},{0,24},{9,1},{17,9},{25,17},{1,25},{10,2},{18... | collective-permute-start | bytes 491528 | tf_op jit(solution)/shard_map/ppermute | solution.py:19
  28.0 2.4 %copy-start.2 = (f32[40,2,128,128]{3,2,0,1:T(8,128)}, f32[40,2,128,128]{3,2,0,1:T(8,128)S(1)}, u32[]{:S(2)}) copy-start(f32[40,2,128,128]{3,2,0,1:T(8,128)S(1)} %fusion.25) | copy-start | bytes 15728644
  30.4 9.6 %collective-permute-start.2 = (f32[40,2,8,128]{3,2,0,1:T(8,128)S(1)}, f32[40,2,8,128]{3,2,0,1:T(8,128)S(1)}, u32[]{:S(2)}, u32[]{:S(2)}) collective-permute-start(f32[40,2,8,128]{3,2,0,1:T(8,128)S(1)} %get-tuple-element.60), channel_id=1, source_target_pairs={{0,2},{2,4},{4,6},{1,3},{3,5},{5,7},{8,10},{10,12},{12,14},{9,11},... | collective-permute-start | bytes 983048 | tf_op jit(solution)/shard_map/ppermute | solution.py:16
  33.9 10.2 %collective-permute-start.3 = (f32[40,2,8,128]{3,2,0,1:T(8,128)S(1)}, f32[40,2,8,128]{3,2,0,1:T(8,128)S(1)}, u32[]{:S(2)}, u32[]{:S(2)}) collective-permute-start(f32[40,2,8,128]{3,2,0,1:T(8,128)S(1)} %get-tuple-element.61), channel_id=1, source_target_pairs={{2,0},{4,2},{6,4},{3,1},{5,3},{7,5},{10,8},{12,10},{14,12},{11,9},... | collective-permute-start | bytes 983048 | tf_op jit(solution)/shard_map/ppermute | solution.py:19
  35.4 18.3 %copy-start.5 = (s32[256]{0:T(256)S(1)}, s32[256]{0:T(256)}, u32[]{:S(2)}) copy-start(s32[256]{0:T(256)} %param.20) | copy-start | bytes 3076
  35.4 18.4 %copy-start.6 = (s32[256]{0:T(256)S(1)}, s32[256]{0:T(256)}, u32[]{:S(2)}) copy-start(s32[256]{0:T(256)} %param.22) | copy-start | bytes 3076
  35.4 29.3 %copy-start.7 = (f32[256]{0:T(256)S(1)}, f32[256]{0:T(256)}, u32[]{:S(2)}) copy-start(f32[256]{0:T(256)} %param.21) | copy-start | bytes 3076
  35.4 37.8 %copy-start.4 = (f32[256]{0:T(256)S(1)}, f32[256]{0:T(256)}, u32[]{:S(2)}) copy-start(f32[256]{0:T(256)} %param.23) | copy-start | bytes 3076
  53.7 43.0 %copy-start.3 = (bf16[40,2,128,128]{3,2,1,0:T(8,128)(2,1)S(1)}, bf16[40,2,128,128]{3,2,1,0:T(8,128)(2,1)}, u32[]{:S(2)}) copy-start(bf16[40,2,128,128]{3,2,1,0:T(8,128)(2,1)} %param.18) | copy-start | bytes 7864324
  61.7 5.3 %collective-permute-start.4 = (f32[1,128,1]{2,1,0:T(8,128)S(1)}, f32[1,128,1]{2,1,0:T(8,128)S(1)}, u32[]{:S(2)}, u32[]{:S(2)}) collective-permute-start(f32[1,128,1]{2,1,0:T(8,128)S(1)} %get-tuple-element.70), channel_id=1, source_target_pairs={{0,8},{8,16},{16,24},{24,0},{1,9},{9,17},{17,25},{25,1},{2,10},{10... | collective-permute-start | bytes 1544 | tf_op jit(solution)/shard_map/ppermute | solution.py:16
  63.5 5.2 %collective-permute-start.5 = (f32[1,128,1]{2,1,0:T(8,128)S(1)}, f32[1,128,1]{2,1,0:T(8,128)S(1)}, u32[]{:S(2)}, u32[]{:S(2)}) collective-permute-start(f32[1,128,1]{2,1,0:T(8,128)S(1)} %get-tuple-element.71), channel_id=1, source_target_pairs={{8,0},{16,8},{24,16},{0,24},{9,1},{17,9},{25,17},{1,25},{10,2},{18... | collective-permute-start | bytes 1544 | tf_op jit(solution)/shard_map/ppermute | solution.py:19
  69.4 5.4 %collective-permute-start.6 = (f32[1,1,130]{2,1,0:T(1,128)S(1)}, f32[1,1,130]{2,1,0:T(1,128)S(1)}, u32[]{:S(2)}, u32[]{:S(2)}) collective-permute-start(f32[1,1,130]{2,1,0:T(1,128)S(1)} %get-tuple-element.64), channel_id=1, source_target_pairs={{0,2},{2,4},{4,6},{6,0},{1,3},{3,5},{5,7},{7,1},{8,10},{10,12},{12... | collective-permute-start | bytes 1568 | tf_op jit(solution)/shard_map/ppermute | solution.py:16
  70.9 3.9 %collective-permute-start.7 = (f32[1,1,130]{2,1,0:T(1,128)S(1)}, f32[1,1,130]{2,1,0:T(1,128)S(1)}, u32[]{:S(2)}, u32[]{:S(2)}) collective-permute-start(f32[1,1,130]{2,1,0:T(1,128)S(1)} %get-tuple-element.65), channel_id=1, source_target_pairs={{2,0},{4,2},{6,4},{0,6},{3,1},{5,3},{7,5},{1,7},{10,8},{12,10},{14... | collective-permute-start | bytes 1568 | tf_op jit(solution)/shard_map/ppermute | solution.py:19
  79.5 4.5 %collective-permute-start.8 = (f32[1,130,1]{1,2,0:T(1,128)S(1)}, f32[1,130,1]{1,2,0:T(1,128)S(1)}, u32[]{:S(2)}, u32[]{:S(2)}) collective-permute-start(f32[1,130,1]{1,2,0:T(1,128)S(1)} %get-tuple-element.67), channel_id=1, source_target_pairs={{0,8},{8,16},{16,24},{24,0},{1,9},{9,17},{17,25},{25,1},{2,10},{10... | collective-permute-start | bytes 1568 | tf_op jit(solution)/shard_map/ppermute | solution.py:16
  81.0 3.6 %collective-permute-start.9 = (f32[1,130,1]{1,2,0:T(1,128)S(1)}, f32[1,130,1]{1,2,0:T(1,128)S(1)}, u32[]{:S(2)}, u32[]{:S(2)}) collective-permute-start(f32[1,130,1]{1,2,0:T(1,128)S(1)} %get-tuple-element.66), channel_id=1, source_target_pairs={{8,0},{16,8},{24,16},{0,24},{9,1},{17,9},{25,17},{1,25},{10,2},{18... | collective-permute-start | bytes 1568 | tf_op jit(solution)/shard_map/ppermute | solution.py:19
  84.7 5.0 %collective-permute-start.10 = (f32[1,1,128]{1,2,0:T(8,128)S(1)}, f32[1,1,128]{1,2,0:T(8,128)S(1)}, u32[]{:S(2)}, u32[]{:S(2)}) collective-permute-start(f32[1,1,128]{1,2,0:T(8,128)S(1)} %get-tuple-element.69), channel_id=1, source_target_pairs={{0,2},{2,4},{4,6},{1,3},{3,5},{5,7},{8,10},{10,12},{12,14},{9,11},... | collective-permute-start | bytes 1544 | tf_op jit(solution)/shard_map/ppermute | solution.py:16
  87.9 6.2 %collective-permute-start.11 = (f32[1,1,128]{1,2,0:T(8,128)S(1)}, f32[1,1,128]{1,2,0:T(8,128)S(1)}, u32[]{:S(2)}, u32[]{:S(2)}) collective-permute-start(f32[1,1,128]{1,2,0:T(8,128)S(1)} %get-tuple-element.68), channel_id=1, source_target_pairs={{2,0},{4,2},{6,4},{3,1},{5,3},{7,5},{10,8},{12,10},{14,12},{11,9},... | collective-permute-start | bytes 1544 | tf_op jit(solution)/shard_map/ppermute | solution.py:19
  97.4 5.8 %copy-start = (f32[40,2,128,128]{3,2,0,1:T(8,128)}, f32[40,2,128,128]{3,2,0,1:T(8,128)S(1)}, u32[]{:S(2)}) copy-start(f32[40,2,128,128]{3,2,0,1:T(8,128)S(1)} %convert_multiply_fusion) | copy-start | bytes 15728644
  106.5 11.5 %collective-permute-start.12 = (f32[40,2,128,8]{2,3,1,0:T(8,128)S(1)}, f32[40,2,128,8]{2,3,1,0:T(8,128)S(1)}, u32[]{:S(2)}, u32[]{:S(2)}) collective-permute-start(f32[40,2,128,8]{2,3,1,0:T(8,128)S(1)} %copy.31), channel_id=1, source_target_pairs={{0,8},{8,16},{16,24},{24,0},{1,9},{9,17},{17,25},{25,1},{2,10},{10... | collective-permute-start | bytes 983048 | tf_op jit(solution)/shard_map/ppermute | solution.py:16
  111.3 12.0 %collective-permute-start.13 = (f32[40,2,128,8]{2,3,1,0:T(8,128)S(1)}, f32[40,2,128,8]{2,3,1,0:T(8,128)S(1)}, u32[]{:S(2)}, u32[]{:S(2)}) collective-permute-start(f32[40,2,128,8]{2,3,1,0:T(8,128)S(1)} %copy.32), channel_id=1, source_target_pairs={{8,0},{16,8},{24,16},{0,24},{9,1},{17,9},{25,17},{1,25},{10,2},{18... | collective-permute-start | bytes 983048 | tf_op jit(solution)/shard_map/ppermute | solution.py:19
  126.5 28.9 %copy-start.1 = (bf16[40,2,128,128]{3,2,1,0:T(8,128)(2,1)S(1)}, bf16[40,2,128,128]{3,2,1,0:T(8,128)(2,1)}, u32[]{:S(2)}) copy-start(bf16[40,2,128,128]{3,2,1,0:T(8,128)(2,1)} %param.17) | copy-start | bytes 7864324
  140.9 10.1 %collective-permute-start.14 = (f32[40,2,8,128]{3,2,0,1:T(8,128)S(1)}, f32[40,2,8,128]{3,2,0,1:T(8,128)S(1)}, u32[]{:S(2)}, u32[]{:S(2)}) collective-permute-start(f32[40,2,8,128]{3,2,0,1:T(8,128)S(1)} %get-tuple-element.56), channel_id=1, source_target_pairs={{0,2},{2,4},{4,6},{1,3},{3,5},{5,7},{8,10},{10,12},{12,14},{9,11},... | collective-permute-start | bytes 983048 | tf_op jit(solution)/shard_map/ppermute | solution.py:16
  144.6 10.8 %collective-permute-start.15 = (f32[40,2,8,128]{3,2,0,1:T(8,128)S(1)}, f32[40,2,8,128]{3,2,0,1:T(8,128)S(1)}, u32[]{:S(2)}, u32[]{:S(2)}) collective-permute-start(f32[40,2,8,128]{3,2,0,1:T(8,128)S(1)} %get-tuple-element.57), channel_id=1, source_target_pairs={{2,0},{4,2},{6,4},{3,1},{5,3},{7,5},{10,8},{12,10},{14,12},{11,9},... | collective-permute-start | bytes 983048 | tf_op jit(solution)/shard_map/ppermute | solution.py:19
Sparse Core Ops, SparseCore 0:
  53.8 6.8 reduce-scatter.1
where the time goes:
time: 172 us
  waiting for transfers between devices  49.1 us (29%)
  matrix products  40.7 us (24%)
  starting transfers between devices  31.2 us (18%)
  local copies, waits for them, and re-layouts  30.1 us (18%)
  between operations  14.4 us (8%)
  blocking collectives  4.56 us (3%)
  other arithmetic  1.89 us (1%)
    ppermute x8, waiting for transfers between devices, padded_2(): lax.ppermute(lax.slice_in_dim(block, block.shape[dim] - width, None, axis...  22.3 us
    ppermute x8, waiting for transfers between devices, padded_2(): lax.ppermute(lax.slice_in_dim(block, 0, width, axis=dim), axis, backward)  19.8 us
    dot_general x2, matrix products, lon_filter(): jnp.einsum('mlik,lkj->mlij', padded, lon_matrix, precision=lax.Precision....  19.8 us
    ppermute x8, starting transfers between devices, padded_2(): lax.ppermute(lax.slice_in_dim(block, block.shape[dim] - width, None, axis...  19.6 us
    dot_general x2, matrix products, lat_local(): jnp.einsum('mlkj,lki->mlij', padded, lat_matrix, precision=lax.Precision....  15.5 us
    ppermute x8, starting transfers between devices, padded_2(): lax.ppermute(lax.slice_in_dim(block, 0, width, axis=dim), axis, backward)  11.6 us
    slice x6, local copies, waits for them, and re-layouts, padded_2(): lax.slice_in_dim(block, block.shape[dim] - width, None, axis=dim)  10.2 us
    unnamed x21, local copies, waits for them, and re-layouts  9.41 us
  transfers between devices with their start and end apart: 17, of which 16 were waited for; matrix products, arithmetic and copies ran while one was open for 5% of the time, Pallas kernels for 0%

commit v1 on v0

v1 whole, which is shorter than its diff:
```python
import functools

import jax
import jax.numpy as jnp
from jax import lax
from jax.experimental import pallas as pl
from jax.experimental.pallas import tpu as pltpu
from jax.sharding import PartitionSpec as P

HB = 8
GROUP = 16
MEMBERS = 8
LANES = 128
HIGHEST = lax.Precision.HIGHEST
F32 = jnp.float32
BF16 = jnp.bfloat16


def rounded(size, step):
    return -(-size // step) * step


def iota(shape, axis):
    return lax.broadcasted_iota(jnp.int32, shape, axis)


def split(value):
    high = value.astype(BF16)
    return high, (value - high.astype(F32)).astype(BF16)


def dot(left, right, precision=None):
    return lax.dot_general(
        left, right, (((1,), (0,)), ((), ())), precision=precision, preferred_element_type=F32
    )


def row_of(index, height):
    above = index - height - HB
    return jnp.where(index < height, index, jnp.where(index < height + HB, above, index - HB))


def packed_column(lane, level, width):
    west = (lane < LANES // 2) if level == 0 else (lane >= LANES // 2)
    cell = lane % HB
    return jnp.where(west, cell - HB, width + cell)


def packed_member(lane):
    return (lane % (LANES // 2)) // HB


def taps(offset, spread):
    lane = iota((8, LANES), 1)
    distance = (lane - HB).astype(F32)
    scale = jnp.full((8, LANES), 1.0, F32) * (0.5 / (spread * spread))
    shape = jnp.where(lane <= 2 * HB, jnp.exp(-(distance * distance) * scale), 0.0)
    norm = lax.rsqrt(jnp.sum(shape * shape, axis=1, keepdims=True))[:1, :1]
    far = offset.astype(F32)
    value = jnp.exp(-(far * far) * scale[:1, :1]) * norm
    return jnp.where(jnp.abs(offset) <= HB, value, 0.0)


def pack_kernel(perts_ref, halo_ref, east_ref, west_ref):
    rows = east_ref.shape[1]
    width = perts_ref.shape[2]
    lane = iota((rows, LANES), 1)
    east = jnp.zeros((rows, LANES), F32)
    west = jnp.zeros((rows, LANES), F32)
    for k in range(GROUP):
        t, level = k // 2, k % 2
        own = perts_ref[k]
        halo = halo_ref[k]
        last = jnp.concatenate([own[:, width - LANES :], halo[:, width - LANES :]], 0).astype(F32)
        first = jnp.concatenate([own[:, :LANES], halo[:, :LANES]], 0).astype(F32)
        slot = level * (LANES // 2) + t * HB
        other = (1 - level) * (LANES // 2) + t * HB
        last = pltpu.roll(last, (slot + HB) % LANES, 1)
        first = first if other == 0 else pltpu.roll(first, other, 1)
        east = jnp.where(lane // HB == slot // HB, last, east)
        west = jnp.where(lane // HB == other // HB, first, west)
    east_ref[0] = east.astype(BF16)
    west_ref[0] = west.astype(BF16)


def local_kernel(
    width_ref, alpha_ref, perts_ref, sum_ref, rows_ref, cols_ref, lon_ref, lat_ref, stack_ref
):
    height, width = alpha_ref.shape[1], alpha_ref.shape[2]
    ext = height + 2 * HB

    @pl.when(pl.program_id(0) == 0)
    def _():
        sum_ref[...] = jnp.zeros_like(sum_ref)
        for level in range(2):
            spread = width_ref[level].astype(F32)
            source = iota((width, width), 0)
            high, low = split(taps(source - iota((width, width), 1), spread))
            source = iota((width, LANES), 0)
            lane = iota((width, LANES), 1)
            edge = taps(source - packed_column(lane, level, width), spread)
            for t in range(MEMBERS):
                part_high, part_low = split(jnp.where(packed_member(lane) == t, edge, 0.0))
                lon_ref[level, t, :width, :width] = high
                lon_ref[level, t, width:, :width] = low
                lon_ref[level, t, :width, width:] = part_high
                lon_ref[level, t, width:, width:] = part_low
            target = row_of(iota((ext, height), 0), height)
            high, low = split(taps(target - iota((ext, height), 1), spread))
            lat_ref[level, :, :height] = high
            lat_ref[level, :, height : 2 * height] = low
            lat_ref[level, :, 2 * height :] = high

    for level in range(2):
        packed = jnp.zeros((height, LANES), F32)
        for t in range(MEMBERS):
            field = alpha_ref[2 * t + level]
            both = dot(jnp.concatenate([field, field], 1), lon_ref[level, t])
            high, low = split(both[:, :width])
            stack_ref[:height, t * width : (t + 1) * width] = high
            stack_ref[height : 2 * height, t * width : (t + 1) * width] = high
            stack_ref[2 * height :, t * width : (t + 1) * width] = low
            packed = packed + both[:, width:]
        high, low = split(packed)
        stack_ref[:height, MEMBERS * width :] = high
        stack_ref[height : 2 * height, MEMBERS * width :] = high
        stack_ref[2 * height :, MEMBERS * width :] = low
        total = sum_ref[level]
        for pair in range(MEMBERS // 2):
            base = 2 * pair * width
            wide = dot(lat_ref[level], stack_ref[:, base : base + 2 * width])
            for side in range(2):
                k = 2 * (2 * pair + side) + level
                field = wide[:, side * width : (side + 1) * width]
                total = total + perts_ref[k].astype(F32) * field[:height]
                rows_ref[k] = field[height:]
        sum_ref[level] = total
        cols_ref[0, level] = dot(lat_ref[level], stack_ref[:, MEMBERS * width :])


def frame_kernel(sum_ref, rows_ref, cols_ref, halo_ref, west_ref, east_ref, out_ref):
    height, width = sum_ref.shape[1], sum_ref.shape[2]
    ext = height + 2 * HB
    groups = west_ref.shape[0]
    lane = iota((ext, LANES), 1)
    out = out_ref.shape[2]
    for level in range(2):
        edge = jnp.zeros((2 * HB, width), F32)
        packed = jnp.zeros((ext, LANES), F32)
        for group in range(groups):
            for t in range(MEMBERS):
                k = group * GROUP + 2 * t + level
                edge = edge + halo_ref[k].astype(F32) * rows_ref[k]
            west = west_ref[group].astype(F32)
            east = east_ref[group].astype(F32)
            half = lane < LANES // 2
            cell = jnp.where(half, west, east) if level == 0 else jnp.where(half, east, west)
            packed = packed + cell * cols_ref[group, level]
        own = jnp.concatenate([edge[:HB], sum_ref[level], edge[HB:]], 0)
        packed = jnp.concatenate(
            [packed[height : height + HB], packed[:height], packed[height + HB :]], 0
        )
        place = (iota((width, out), 0) + HB == iota((width, out), 1)).astype(F32)
        column = packed_column(iota((LANES, out), 0), level, width)
        gather = (column + HB == iota((LANES, out), 1)).astype(F32)
        out_ref[level] = dot(own, place, HIGHEST) + dot(packed, gather, HIGHEST)


def fine_kernel(
    margin,
    coarse_ref,
    target_ref,
    weight_ref,
    lat_col_ref,
    lat_row_ref,
    lon_col_ref,
    lon_row_ref,
    inc_ref,
    own_ref,
    edge_ref,
):
    height, width = own_ref.shape[1] - 2 * HB, own_ref.shape[2]
    ext = height + 2 * HB
    fine_rows, fine_cols = target_ref.shape[1], target_ref.shape[2]
    coarse_rows, coarse_cols = coarse_ref.shape[1], coarse_ref.shape[2]
    tall = lat_row_ref.shape[1]
    skirt = 2 * margin - 2

    def interpolate(cell, index, weight):
        near = jnp.where(cell == index, 1.0 - weight, 0.0)
        return near + jnp.where(cell == index + 1, weight, 0.0)

    lat_index = lat_col_ref[:, 0:1].astype(jnp.int32)
    lat_map = interpolate(iota((fine_rows, coarse_rows), 1), lat_index, lat_col_ref[:, 1:2])
    lon_index = lon_row_ref[0:1, :].astype(jnp.int32)
    lon_map = interpolate(iota((coarse_cols, fine_cols), 0), lon_index, lon_row_ref[1:2, :])
    row = row_of(iota((ext, tall), 0), height) + margin
    lat_index = lat_row_ref[0:1, :].astype(jnp.int32)
    lat_back = interpolate(row, lat_index, lat_row_ref[1:2, :])
    back_index = lon_col_ref[:, 0:1].astype(jnp.int32)
    back_weight = lon_col_ref[:, 1:2]
    own_back = interpolate(iota((fine_cols, width), 1) + margin, back_index, back_weight)
    for level in range(2):
        by_lat = dot(lat_map, coarse_ref[level], HIGHEST)
        increment = dot(by_lat, lon_map, HIGHEST)
        rows, cols = inc_ref.shape[1], inc_ref.shape[2]
        inc_ref[level] = increment[skirt : skirt + rows, skirt : skirt + cols]
        misfit = weight_ref[level] * (increment - target_ref[level])
        column = packed_column(iota((fine_cols, LANES), 1), level, width) + margin
        edge_back = interpolate(column, back_index, back_weight)
        lon_back = dot(misfit, jnp.concatenate([own_back, edge_back], 1), HIGHEST)
        if tall > fine_rows:
            blank = jnp.zeros((tall - fine_rows, width + LANES), F32)
            lon_back = jnp.concatenate([lon_back, blank], 0)
        residual = dot(lat_back, lon_back, HIGHEST)
        own_ref[level] = residual[:, :width]
        edge_ref[level] = residual[:, width:]


def gradient_kernel(
    width_ref, alpha_ref, perts_ref, halo_ref, west_ref, east_ref, own_ref, edge_ref, out_ref,
    lon_ref, lat_ref, stack_ref,
):
    height, width = alpha_ref.shape[1], alpha_ref.shape[2]
    ext = height + 2 * HB

    @pl.when(pl.program_id(0) == 0)
    def _():
        for level in range(2):
            spread = width_ref[level].astype(F32)
            source = iota((width, width), 0)
            high, low = split(taps(source - iota((width, width), 1), spread))
            lane = iota((LANES, width), 0)
            edge = taps(packed_column(lane, level, width) - iota((LANES, width), 1), spread)
            for t in range(MEMBERS):
                part_high, part_low = split(jnp.where(packed_member(lane) == t, edge, 0.0))
                lon_ref[level, t, :width, :width] = high
                lon_ref[level, t, :width, width:] = low
                lon_ref[level, t, width:, :width] = part_high
                lon_ref[level, t, width:, width:] = part_low
            source = row_of(iota((height, ext), 1), height)
            high, low = split(taps(source - iota((height, ext), 0), spread))
            lat_ref[level, :, :ext] = high
            lat_ref[level, :, ext : 2 * ext] = low
            lat_ref[level, :, 2 * ext :] = high

    half = iota((ext, LANES), 1) < LANES // 2
    west = west_ref[0].astype(F32)
    east = east_ref[0].astype(F32)

    def stack(value, start, size):
        high, low = split(value)
        stack_ref[:ext, start : start + size] = high
        stack_ref[ext : 2 * ext, start : start + size] = high
        stack_ref[2 * ext :, start : start + size] = low

    for level in range(2):
        cell = jnp.where(half, west, east) if level == 0 else jnp.where(half, east, west)
        stack(cell * edge_ref[level], MEMBERS * width, LANES)
        for t in range(MEMBERS):
            k = 2 * t + level
            field = jnp.concatenate([perts_ref[k], halo_ref[k]], 0).astype(F32)
            stack(field * own_ref[level], t * width, width)
        edge_high, edge_low = split(dot(lat_ref[level], stack_ref[:, MEMBERS * width :]))
        for pair in range(MEMBERS // 2):
            base = 2 * pair * width
            wide = dot(lat_ref[level], stack_ref[:, base : base + 2 * width])
            for side in range(2):
                t = 2 * pair + side
                k = 2 * t + level
                high, low = split(wide[:, side * width : (side + 1) * width])
                main = dot(jnp.concatenate([high, edge_high], 1), lon_ref[level, t])
                rest = dot(jnp.concatenate([low, edge_low], 1), lon_ref[level, t, :, :width])
                total = main[:, :width] + main[:, width:] + rest
                out_ref[k] = alpha_ref[k].astype(F32) + total


def ring(axis, periodic):
    count = lax.axis_size(axis)
    forward = [(i, i + 1) for i in range(count - 1)]
    if periodic:
        forward.append((count - 1, 0))
    return forward, [(target, source) for source, target in forward]


def exchange(to_next, to_previous, axis, periodic):
    forward, backward = ring(axis, periodic)
    return lax.ppermute(to_next, axis, forward), lax.ppermute(to_previous, axis, backward)


def vmem(*shape):
    return pl.BlockSpec(shape, lambda s: (0,) * len(shape))


def grouped(*shape):
    return pl.BlockSpec(shape, lambda s: (s,) + (0,) * (len(shape) - 1))


def params(*semantics):
    return pltpu.CompilerParams(dimension_semantics=semantics, vmem_limit_bytes=60 * 1024 * 1024)


def body(
    alpha_fields,
    member_perts,
    band_widths,
    lat_index,
    lat_weight,
    lon_index,
    lon_weight,
    innovation,
    obs_weight,
):
    members, levels, height, width = alpha_fields.shape
    fields = members * levels
    groups = fields // GROUP
    ext = height + 2 * HB
    margin = HB + 2
    skirt = 2 * margin - 2
    strip = margin + HB
    fine_h, fine_w = innovation.shape[1], innovation.shape[2]
    alpha = alpha_fields.reshape(fields, height, width)
    perts = member_perts.reshape(fields, height, width)
    smem = pl.BlockSpec(memory_space=pltpu.SMEM)

    above, below = exchange(perts[:, height - HB :], perts[:, :HB], "gy", False)
    halo = jnp.concatenate([above, below], axis=1)
    east_send, west_send = pl.pallas_call(
        pack_kernel,
        grid=(groups,),
        in_specs=[grouped(GROUP, height, width), grouped(GROUP, 2 * HB, width)],
        out_specs=[grouped(1, ext, LANES)] * 2,
        out_shape=[jax.ShapeDtypeStruct((groups, ext, LANES), BF16)] * 2,
        compiler_params=params("arbitrary"),
        name="pack",
    )(perts, halo)
    west, east = exchange(east_send, west_send, "gx", True)

    lane = jnp.arange(fine_w)[None, :]
    table = jnp.where(
        lane == 0,
        lat_index.astype(F32)[:, None],
        jnp.where(lane == 1, lat_weight[:, None], 0.0),
    )[None]

    def rows_of(cut):
        return jnp.concatenate([innovation[:, cut], obs_weight[:, cut], table[:, cut]], 0)

    top, bottom = exchange(
        rows_of(slice(fine_h - skirt, None)), rows_of(slice(0, skirt)), "gy", False
    )
    target = jnp.concatenate([top[:2], innovation, bottom[:2]], 1)
    weight = jnp.concatenate([top[2:4], obs_weight, bottom[2:4]], 1)
    lat_table = jnp.concatenate([top[4, :, :2], table[0, :, :2], bottom[4, :, :2]], 0)
    tall = fine_h + 2 * skirt
    row = jnp.arange(tall)[:, None]

    def cols_of(cut):
        lon = jnp.where(
            row == 0, lon_index.astype(F32)[None, cut], jnp.where(row == 1, lon_weight[None, cut], 0.0)
        )[None]
        return jnp.concatenate([target[:, :, cut], weight[:, :, cut], lon], 0)

    left, right = exchange(
        cols_of(slice(fine_w - skirt, None)), cols_of(slice(0, skirt)), "gx", True
    )
    pad_rows = rounded(tall, 8) - tall
    pad_cols = rounded(fine_w + 2 * skirt, LANES) - fine_w - 2 * skirt
    pads = ((0, 0), (0, pad_rows), (0, pad_cols))
    target = jnp.pad(jnp.concatenate([left[:2], target, right[:2]], 2), pads)
    weight = jnp.pad(jnp.concatenate([left[2:4], weight, right[2:4]], 2), pads)
    lon_table = jnp.concatenate(
        [left[4, :2], jnp.stack([lon_index.astype(F32), lon_weight]), right[4, :2]], 1
    )
    lat_start = lax.axis_index("gy") * height
    lon_start = lax.axis_index("gx") * width
    lon_total = width * lax.axis_size("gx")
    lat_rel = lat_table[:, 0] - (lat_start - margin).astype(F32)
    lon_rel = jnp.remainder(
        lon_table[0].astype(jnp.int32) - lon_start + margin, lon_total
    ).astype(F32)

    def padded(index, values, size):
        short = size - index.shape[0]
        index = jnp.pad(index, (0, short), constant_values=-9.0)
        return jnp.stack([index, jnp.pad(values, (0, short))])

    lat_col = padded(lat_rel, lat_table[:, 1], tall + pad_rows).T
    lat_row = padded(lat_rel, lat_table[:, 1], rounded(tall, LANES))
    lon_row = padded(lon_rel, lon_table[1], fine_w + 2 * skirt + pad_cols)
    lon_col = lon_row.T

    partial, edge_rows, edge_cols = pl.pallas_call(
        local_kernel,
        grid=(groups,),
        in_specs=[smem, grouped(GROUP, height, width), grouped(GROUP, height, width)],
        out_specs=[
            vmem(2, height, width),
            grouped(GROUP, 2 * HB, width),
            grouped(1, 2, ext, LANES),
        ],
        out_shape=[
            jax.ShapeDtypeStruct((2, height, width), F32),
            jax.ShapeDtypeStruct((fields, 2 * HB, width), F32),
            jax.ShapeDtypeStruct((groups, 2, ext, LANES), F32),
        ],
        scratch_shapes=[
            pltpu.VMEM((2, MEMBERS, 2 * width, width + LANES), BF16),
            pltpu.VMEM((2, ext, 3 * height), BF16),
            pltpu.VMEM((3 * height, MEMBERS * width + LANES), BF16),
        ],
        compiler_params=params("arbitrary"),
        name="local",
        cost_estimate=pl.CostEstimate(flops=10**10, bytes_accessed=10**7, transcendentals=0),
    )(band_widths, alpha, perts)

    framed = pl.pallas_call(
        frame_kernel,
        out_shape=jax.ShapeDtypeStruct((2, ext, width + 2 * HB), F32),
        compiler_params=params(),
        name="frame",
    )(partial, edge_rows, edge_cols, halo, west, east)
    count = lax.axis_size("ma")
    swap = [(i, (i + 1) % count) for i in range(count)]
    framed = framed + lax.ppermute(framed, "ma", swap)
    above, below = exchange(framed[:, ext - strip :], framed[:, :strip], "gy", False)
    gap = ext + 4 - strip
    framed = (
        jnp.pad(framed, ((0, 0), (2, 2), (0, 0)))
        + jnp.pad(above, ((0, 0), (0, gap), (0, 0)))
        + jnp.pad(below, ((0, 0), (gap, 0), (0, 0)))
    )
    wide = framed.shape[2]
    before, after = exchange(framed[:, :, wide - strip :], framed[:, :, :strip], "gx", True)
    rows = rounded(ext + 4, LANES)
    cols = rounded(wide + 4, LANES)
    gap = wide + 4 - strip

    def place(value, start):
        return jnp.pad(
            value,
            ((0, 0), (0, rows - value.shape[1]), (start, cols - start - value.shape[2])),
        )

    coarse = place(framed, 2) + place(before, 0) + place(after, gap)
    increment, own, edge = pl.pallas_call(
        functools.partial(fine_kernel, margin),
        out_shape=[
            jax.ShapeDtypeStruct((2, fine_h, fine_w), F32),
            jax.ShapeDtypeStruct((2, ext, width), F32),
            jax.ShapeDtypeStruct((2, ext, LANES), F32),
        ],
        compiler_params=params(),
        name="fine",
    )(coarse, target, weight, lat_col, lat_row, lon_col, lon_row)

    gradient = pl.pallas_call(
        gradient_kernel,
        grid=(groups,),
        in_specs=[
            smem,
            grouped(GROUP, height, width),
            grouped(GROUP, height, width),
            grouped(GROUP, 2 * HB, width),
            grouped(1, ext, LANES),
            grouped(1, ext, LANES),
            vmem(2, ext, width),
            vmem(2, ext, LANES),
        ],
        out_specs=grouped(GROUP, height, width),
        out_shape=jax.ShapeDtypeStruct((fields, height, width), F32),
        scratch_shapes=[
            pltpu.VMEM((2, MEMBERS, width + LANES, 2 * width), BF16),
            pltpu.VMEM((2, height, 3 * ext), BF16),
            pltpu.VMEM((3 * ext, MEMBERS * width + LANES), BF16),
        ],
        compiler_params=params("arbitrary"),
        name="gradient",
    )(band_widths, alpha, perts, halo, west, east, own, edge)
    return increment, gradient.reshape(alpha_fields.shape)


def solution(mesh):
    placed = (
        P("ma", None, "gy", "gx"),
        P("ma", None, "gy", "gx"),
        P(),
        P("gy"),
        P("gy"),
        P("gx"),
        P("gx"),
        P(None, "gy", "gx"),
        P(None, "gy", "gx"),
    )
    return jax.shard_map(
        body,
        mesh=mesh,
        in_specs=placed,
        out_specs=(P(None, "gy", "gx"), P("ma", None, "gy", "gx")),
        check_vma=False,
    )
```

time: 172 us -> 96.8 us (0.56)
  matrix products: 40.7 us -> 0 us
  Pallas kernels: 0 us -> 38.5 us
  waiting for transfers between devices: 49.1 us -> 13.4 us
  local copies, waits for them, and re-layouts: 30.1 us -> 8.1 us
  between operations: 14.4 us -> 1.02 us
  other arithmetic: 1.89 us -> 8.58 us
  starting transfers between devices: 31.2 us -> 26.4 us
  blocking collectives: 4.56 us -> 0 us
    dot_general x9 -> x0, matrix products: 40.7 us -> none  [the longest x2 19.8 us: lon_filter(): jnp.einsum('mlik,lkj->mlij', padded, lon_matrix, precision=lax.Precision....]
    pallas_call x0 -> x5, Pallas kernels: none -> 38.5 us  [the longest x1 14.2 us: body(): pl.pallas_call(gradient_kernel, grid=(groups,), in_specs=[smem, grouped(G...]
    ppermute x16 -> x13, waiting for transfers between devices: 42.2 us -> 13.4 us  [the longest x6 6.99 us: exchange(): lax.ppermute(to_previous, axis, backward)]
    slice x11 -> x25, local copies, waits for them, and re-layouts: 13.6 us -> 4.22 us  [the longest x1 1.02 us: body(): above, below = exchange(perts[:, height - HB:], perts[:, :HB], 'gy', False)]
    unnamed x21 -> x17, local copies, waits for them, and re-layouts: 9.41 us -> 2.06 us
    reduce_scatter x1 -> x0, waiting for transfers between devices: 6.93 us -> none  [body(): lax.psum_scatter(local_sum, 'ma', scatter_dimension=0, tiled=True)]
    ppermute x2 -> x0, local copies, waits for them, and re-layouts: 6.29 us -> none  [the longest x1 3.15 us: padded_2(): lax.ppermute(lax.slice_in_dim(block, block.shape[dim] - width, None, axis...]
    ppermute x16 -> x13, starting transfers between devices: 31.2 us -> 26.4 us  [the longest x6 18.1 us: exchange(): lax.ppermute(to_next, axis, forward)]
  transfers between devices with their start and end apart: 17 -> 13, of which waited for: 16 -> 7; matrix products, arithmetic and copies ran while one was open for 5% -> 11% of each run, Pallas kernels for 0% -> 14%
where the time goes in v1:
time: 96.8 us; the launch traced here: 96 us
  Pallas kernels  38.5 us (40%)
  starting transfers between devices  26.4 us (27%)
  waiting for transfers between devices  13.4 us (14%)
  other arithmetic  8.58 us (9%)
  local copies, waits for them, and re-layouts  8.1 us (8%)
  between operations  1.02 us (1%)
    ppermute x6, starting transfers between devices, exchange(): lax.ppermute(to_next, axis, forward)  18.1 us
    pallas_call x1, Pallas kernels, body(): pl.pallas_call(gradient_kernel, grid=(groups,), in_specs=[smem, grouped(G...  14.2 us
    pallas_call x1, Pallas kernels, body(): pl.pallas_call(local_kernel, grid=(groups,), in_specs=[smem, grouped(GROU...  8.37 us
    ppermute x6, starting transfers between devices, exchange(): lax.ppermute(to_previous, axis, backward)  8.35 us
    pallas_call x1, Pallas kernels, body(): pl.pallas_call(functools.partial(fine_kernel, margin), out_shape=[jax.Sha...  8.02 us
    ppermute x6, waiting for transfers between devices, exchange(): lax.ppermute(to_previous, axis, backward)  6.99 us
    ppermute x6, waiting for transfers between devices, exchange(): lax.ppermute(to_next, axis, forward)  5.97 us
    pallas_call x1, Pallas kernels, body(): pl.pallas_call(pack_kernel, grid=(groups,), in_specs=[grouped(GROUP, heig...  4.9 us
  transfers between devices with their start and end apart: 13, of which 7 were waited for; matrix products, arithmetic and copies ran while one was open for 11% of the time, Pallas kernels for 14%

profile of v1, /device:TPU:0, one launch (start us, length us, event | category | flops | bytes accessed | tf_op | source)
XLA Modules:
  0.0 96.0 jit_solution(3701313714969931230)
XLA Ops:
  0.6 0.7 convert_element_type.38
  1.3 0.8 select_select_fusion
  2.2 0.9 fusion.19
  3.1 1.3 %collective-permute-start.10 = (f32[5,18,256]{2,1,0:T(8,128)S(1)}, f32[5,18,256]{2,1,0:T(8,128)S(1)}, u32[]{:S(2)}, u32[]{:S(2)}) collective-permute-start(f32[5,18,256]{2,1,0:T(8,128)S(1)} %pad_maximum_fusion.5), channel_id=1, source_target_pairs={{2,0},{4,2},{6,4},{3,1},{5,3},{7,5},{10,8},{12,10},{14,12},{11,9},... | collective-permute-start | bytes 276488 | tf_op jit(solution)/shard_map/ppermute | solution.py:288
  4.4 5.6 %collective-permute-start.9 = (f32[5,18,256]{2,1,0:T(8,128)S(1)}, f32[5,18,256]{2,1,0:T(8,128)S(1)}, u32[]{:S(2)}, u32[]{:S(2)}) collective-permute-start(f32[5,18,256]{2,1,0:T(8,128)S(1)} %pad_maximum_fusion.4), channel_id=1, source_target_pairs={{0,2},{2,4},{4,6},{1,3},{3,5},{5,7},{8,10},{10,12},{12,14},{9,11},... | collective-permute-start | bytes 276488 | tf_op jit(solution)/shard_map/ppermute | solution.py:288
  10.0 1.0 %fusion.16 = (bf16[80,8,128]{2,1,0:T(8,128)(2,1)S(1)}, bf16[80,8,128]{2,1,0:T(8,128)(2,1)S(1)}) fusion(bf16[80,128,128]{2,1,0:T(8,128)(2,1)} %bitcast.14), kind=kLoop, calls=%fused_computation.54 | loop fusion | bytes 655360 | tf_op jit(solution)/shard_map/slice | solution.py:326
  11.0 1.3 %collective-permute-start.1 = (bf16[80,8,128]{2,1,0:T(8,128)(2,1)S(1)}, bf16[80,8,128]{2,1,0:T(8,128)(2,1)S(1)}, u32[]{:S(2)}, u32[]{:S(2)}) collective-permute-start(bf16[80,8,128]{2,1,0:T(8,128)(2,1)S(1)} %get-tuple-element.20), channel_id=1, source_target_pairs={{2,0},{4,2},{6,4},{3,1},{5,3},{7,5},{10,8},{12,10},{14,12},{11,9},... | collective-permute-start | bytes 491528 | tf_op jit(solution)/shard_map/ppermute | solution.py:288
  12.3 4.6 %collective-permute-start = (bf16[80,8,128]{2,1,0:T(8,128)(2,1)S(1)}, bf16[80,8,128]{2,1,0:T(8,128)(2,1)S(1)}, u32[]{:S(2)}, u32[]{:S(2)}) collective-permute-start(bf16[80,8,128]{2,1,0:T(8,128)(2,1)S(1)} %get-tuple-element.21), channel_id=1, source_target_pairs={{0,2},{2,4},{4,6},{1,3},{3,5},{5,7},{8,10},{10,12},{12,14},{9,11},... | collective-permute-start | bytes 491528 | tf_op jit(solution)/shard_map/ppermute | solution.py:288
  16.9 0.7 convert_element_type.39
  17.6 0.8 fusion.28
  18.4 8.4 %local.1 = (f32[2,128,128]{2,1,0:T(8,128)}, f32[80,16,128]{2,1,0:T(8,128)}, f32[5,2,144,128]{3,2,1,0:T(8,128)}) custom-call(s32[2]{0:T(128)} %width_ref.3, bf16[80,128,128]{2,1,0:T(8,128)(2,1)} %bitcast.19, bf16[80,128,128]{2,1,0:T(8,128)(2,1)} %bitcast.15), custom_call_target="tpu_custom_call" | custom-call | flops 10000000000 | bytes 10000000 | tf_op jit(solution)/shard_map/local/pallas_call | solution.py:393
  27.4 0.1 fusion.17
  27.6 0.2 copy.23
  27.7 0.2 copy.26
  28.1 0.2 copy.24
  28.3 0.2 copy.27
  28.5 2.9 %collective-permute-start.12 = (f32[5,292,18]{1,2,0:T(8,128)S(1)}, f32[5,292,18]{1,2,0:T(8,128)S(1)}, u32[]{:S(2)}, u32[]{:S(2)}) collective-permute-start(f32[5,292,18]{1,2,0:T(8,128)S(1)} %pad_maximum_fusion.3), channel_id=1, source_target_pairs={{8,0},{16,8},{24,16},{0,24},{9,1},{17,9},{25,17},{1,25},{10,2},{18... | collective-permute-start | bytes 315368 | tf_op jit(solution)/shard_map/ppermute | solution.py:288
  31.5 0.6 pad_maximum_fusion.8.lat_row_ref
  32.1 0.8 copy.34
  33.0 0.7 copy-done
  33.8 4.9 %pack.1 = (bf16[5,144,128]{2,1,0:T(8,128)(2,1)}, bf16[5,144,128]{2,1,0:T(8,128)(2,1)}) custom-call(bf16[80,128,128]{2,1,0:T(8,128)(2,1)} %bitcast.16, bf16[80,16,128]{2,1,0:T(8,128)(2,1)} %copy-done), custom_call_target="tpu_custom_call" | custom-call | tf_op jit(solution)/shard_map/pack/pallas_call | solution.py:328
  38.7 2.0 %collective-permute-start.2 = (bf16[5,144,128]{2,1,0:T(8,128)(2,1)}, bf16[5,144,128]{2,1,0:T(8,128)(2,1)S(1)}, u32[]{:S(2)}, u32[]{:S(2)}) collective-permute-start(bf16[5,144,128]{2,1,0:T(8,128)(2,1)} %get-tuple-element.13), channel_id=1, source_target_pairs={{0,8},{8,16},{16,24},{24,0},{1,9},{9,17},{17,25},{25,1},{2,10},{10... | collective-permute-start | bytes 552968 | tf_op jit(solution)/shard_map/ppermute | solution.py:288
  40.6 1.0 %collective-permute-start.3 = (bf16[5,144,128]{2,1,0:T(8,128)(2,1)}, bf16[5,144,128]{2,1,0:T(8,128)(2,1)S(1)}, u32[]{:S(2)}, u32[]{:S(2)}) collective-permute-start(bf16[5,144,128]{2,1,0:T(8,128)(2,1)} %get-tuple-element.14), channel_id=1, source_target_pairs={{8,0},{16,8},{24,16},{0,24},{9,1},{17,9},{25,17},{1,25},{10,2},{18... | collective-permute-start | bytes 552968 | tf_op jit(solution)/shard_map/ppermute | solution.py:288
  42.0 0.2 copy.40
  42.1 0.2 copy.41
  42.3 0.2 copy.38
  42.4 0.2 copy.39
  42.6 1.4 %select_maximum_fusion.weight_ref = f32[2,296,384]{2,1,0:T(8,128)} fusion(f32[2,292,18]{2,1,0:T(8,128)S(1)} %copy.41, f32[2,292,18]{2,1,0:T(8,128)S(1)} %copy.40, f32[2,18,256]{2,1,0:T(8,128)S(1)} %get-tuple-element.43, f32[2,256,256]{2,1,0:T(8,128)S(1)} %copy-done.1, f32[2,18,256]{2,1,0:T(8,128)S(1)} %get-tuple-element.41), kind=kLoop, calls=%fused_computation | loop fusion | flops 3864576 | bytes 1591424 | tf_op jit(solution)/shard_map/concatenate | solution.py:371
  44.0 2.7 %collective-permute-done.2.west_ref = bf16[5,144,128]{2,1,0:T(8,128)(2,1)S(1)} collective-permute-done((bf16[5,144,128]{2,1,0:T(8,128)(2,1)}, bf16[5,144,128]{2,1,0:T(8,128)(2,1)S(1)}, u32[]{:S(2)}, u32[]{:S(2)}) %collective-permute-start.2) | collective-permute-done | bytes 184352 | tf_op jit(solution)/shard_map/ppermute | solution.py:288
  46.7 1.3 %collective-permute-done.3.east_ref = bf16[5,144,128]{2,1,0:T(8,128)(2,1)S(1)} collective-permute-done((bf16[5,144,128]{2,1,0:T(8,128)(2,1)}, bf16[5,144,128]{2,1,0:T(8,128)(2,1)S(1)}, u32[]{:S(2)}, u32[]{:S(2)}) %collective-permute-start.3) | collective-permute-done | bytes 184352 | tf_op jit(solution)/shard_map/ppermute | solution.py:288
  48.0 0.7 copy-done.4
  48.7 3.0 %frame.1 = f32[2,144,144]{2,1,0:T(8,128)} custom-call(f32[2,128,128]{2,1,0:T(8,128)} %get-tuple-element.10.sum_ref, f32[80,16,128]{2,1,0:T(8,128)} %get-tuple-element.11.rows_ref, f32[5,2,144,128]{3,2,1,0:T(8,128)} %get-tuple-element.12.cols_ref, bf16[80,16,128]{2,1,0:T(8,128)(2,1)} %copy-done, bf16[5,144,128]{2,1,0:T(8,128)(2,1)} %copy-done.3, ...), custom_call_target="tpu_custom_call" | custom-call | tf_op jit(solution)/shard_map/frame/pallas_call | solution.py:417
  51.7 1.3 %select_maximum_fusion.4.target_ref = f32[2,296,384]{2,1,0:T(8,128)} fusion(f32[2,292,18]{2,1,0:T(8,128)S(1)} %copy.39, f32[2,292,18]{2,1,0:T(8,128)S(1)} %copy.38, f32[2,18,256]{2,1,0:T(8,128)S(1)} %get-tuple-element.42, f32[2,256,256]{2,1,0:T(8,128)S(1)} %copy-done.2, f32[2,18,256]{2,1,0:T(8,128)S(1)} %get-tuple-element.40), kind=kLoop, calls=%fused_computation.4 | loop fusion | flops 3864576 | bytes 1591424 | tf_op jit(solution)/shard_map/concatenate | solution.py:370
  53.0 0.5 collective-permute-done.4
  53.5 1.0 %add.59 = f32[2,144,144]{2,1,0:T(8,128)S(1)} add(f32[2,144,144]{2,1,0:T(8,128)} %frame.1, f32[2,144,144]{2,1,0:T(8,128)S(1)} %collective-permute-done.4) | non-fusion elementwise | flops 41472 | bytes 497664 | tf_op jit(solution)/shard_map/add | solution.py:425
  54.5 3.5 %collective-permute-start.5 = (f32[2,18,144]{2,1,0:T(8,128)S(1)}, f32[2,18,144]{2,1,0:T(8,128)S(1)}, u32[]{:S(2)}, u32[]{:S(2)}) collective-permute-start(f32[2,18,144]{2,1,0:T(8,128)S(1)} %get-tuple-element.32), channel_id=1, source_target_pairs={{0,2},{2,4},{4,6},{1,3},{3,5},{5,7},{8,10},{10,12},{12,14},{9,11},... | collective-permute-start | bytes 62216 | tf_op jit(solution)/shard_map/ppermute | solution.py:288
  58.0 1.3 %collective-permute-start.6 = (f32[2,18,144]{2,1,0:T(8,128)S(1)}, f32[2,18,144]{2,1,0:T(8,128)S(1)}, u32[]{:S(2)}, u32[]{:S(2)}) collective-permute-start(f32[2,18,144]{2,1,0:T(8,128)S(1)} %get-tuple-element.33), channel_id=1, source_target_pairs={{2,0},{4,2},{6,4},{3,1},{5,3},{7,5},{10,8},{12,10},{14,12},{11,9},... | collective-permute-start | bytes 62216 | tf_op jit(solution)/shard_map/ppermute | solution.py:288
  59.4 0.4 collective-permute-done.5
  59.7 4.3 %collective-permute-done.6 = f32[2,18,144]{2,1,0:T(8,128)S(1)} collective-permute-done((f32[2,18,144]{2,1,0:T(8,128)S(1)}, f32[2,18,144]{2,1,0:T(8,128)S(1)}, u32[]{:S(2)}, u32[]{:S(2)}) %collective-permute-start.6) | collective-permute-done | bytes 20768 | tf_op jit(solution)/shard_map/ppermute | solution.py:288
  64.1 2.4 %collective-permute-start.7 = (f32[2,148,18]{2,1,0:T(8,128)S(1)}, f32[2,148,18]{2,1,0:T(8,128)S(1)}, u32[]{:S(2)}, u32[]{:S(2)}) collective-permute-start(f32[2,148,18]{2,1,0:T(8,128)S(1)} %get-tuple-element.30), channel_id=1, source_target_pairs={{0,8},{8,16},{16,24},{24,0},{1,9},{9,17},{17,25},{25,1},{2,10},{10... | collective-permute-start | bytes 63944 | tf_op jit(solution)/shard_map/ppermute | solution.py:288
  66.6 0.5 collective-permute-start.8
  67.1 0.6 pad_maximum_fusion.10
  67.7 0.8 copy.37.lon_col_ref
  68.5 2.9 %collective-permute-done.7 = f32[2,148,18]{2,1,0:T(8,128)S(1)} collective-permute-done((f32[2,148,18]{2,1,0:T(8,128)S(1)}, f32[2,148,18]{2,1,0:T(8,128)S(1)}, u32[]{:S(2)}, u32[]{:S(2)}) %collective-permute-start.7) | collective-permute-done | bytes 21344 | tf_op jit(solution)/shard_map/ppermute | solution.py:288
  71.4 1.4 %collective-permute-done.8 = f32[2,148,18]{2,1,0:T(8,128)S(1)} collective-permute-done((f32[2,148,18]{2,1,0:T(8,128)S(1)}, f32[2,148,18]{2,1,0:T(8,128)S(1)}, u32[]{:S(2)}, u32[]{:S(2)}) %collective-permute-start.8) | collective-permute-done | bytes 21344 | tf_op jit(solution)/shard_map/ppermute | solution.py:288
  72.8 1.0 %pad_add_fusion.coarse_ref = f32[2,256,256]{2,1,0:T(8,128)} fusion(f32[2,148,18]{2,1,0:T(8,128)S(1)} %collective-permute-done.8, f32[2,148,18]{2,1,0:T(8,128)S(1)} %collective-permute-done.7, f32[2,148,144]{2,1,0:T(8,128)S(1)} %pad_add_fusion.1), kind=kLoop, calls=%fused_computation.19 | loop fusion | flops 262144 | bytes 737408 | tf_op jit(solution)/shard_map/add | solution.py:445
  73.8 8.0 %fine.1 = (f32[2,256,256]{2,1,0:T(8,128)}, f32[2,144,128]{2,1,0:T(8,128)}, f32[2,144,128]{2,1,0:T(8,128)}) custom-call(f32[2,256,256]{2,1,0:T(8,128)} %pad_add_fusion.coarse_ref, f32[2,296,384]{2,1,0:T(8,128)} %select_maximum_fusion.4.target_ref, f32[2,296,384]{2,1,0:T(8,128)} %select_maximum_fusion.weight_ref, f32[296,2]{1,0:T(8,128)} %bitcast.21, ...), custom_call_target="tpu_custom_call" | custom-call | tf_op jit(solution)/shard_map/fine/pallas_call | solution.py:446
  81.8 14.2 %gradient.1 = f32[80,128,128]{2,1,0:T(8,128)} custom-call(s32[2]{0:T(128)} %width_ref.3, bf16[80,128,128]{2,1,0:T(8,128)(2,1)} %bitcast.20, bf16[80,128,128]{2,1,0:T(8,128)(2,1)} %bitcast.17, bf16[80,16,128]{2,1,0:T(8,128)(2,1)} %copy-done, bf16[5,144,128]{2,1,0:T(8,128)(2,1)} %copy-done.3, bf16[5,144,128]{2,1,0:T(8,128)(2,1)} %copy-done.4, ...), custom_call_target="tpu_custom_call" | custom-call | tf_op jit(solution)/shard_map/gradient/pallas_call | solution.py:457
  (67 shorter events, 1.5 us)
Async XLA Ops:
  3.1 23.9 %collective-permute-start.10 = (f32[5,18,256]{2,1,0:T(8,128)S(1)}, f32[5,18,256]{2,1,0:T(8,128)S(1)}, u32[]{:S(2)}, u32[]{:S(2)}) collective-permute-start(f32[5,18,256]{2,1,0:T(8,128)S(1)} %pad_maximum_fusion.5), channel_id=1, source_target_pairs={{2,0},{4,2},{6,4},{3,1},{5,3},{7,5},{10,8},{12,10},{14,12},{11,9},... | collective-permute-start | bytes 276488 | tf_op jit(solution)/shard_map/ppermute | solution.py:288
  4.4 22.7 %collective-permute-start.9 = (f32[5,18,256]{2,1,0:T(8,128)S(1)}, f32[5,18,256]{2,1,0:T(8,128)S(1)}, u32[]{:S(2)}, u32[]{:S(2)}) collective-permute-start(f32[5,18,256]{2,1,0:T(8,128)S(1)} %pad_maximum_fusion.4), channel_id=1, source_target_pairs={{0,2},{2,4},{4,6},{1,3},{3,5},{5,7},{8,10},{10,12},{12,14},{9,11},... | collective-permute-start | bytes 276488 | tf_op jit(solution)/shard_map/ppermute | solution.py:288
  11.0 21.9 %collective-permute-start.1 = (bf16[80,8,128]{2,1,0:T(8,128)(2,1)S(1)}, bf16[80,8,128]{2,1,0:T(8,128)(2,1)S(1)}, u32[]{:S(2)}, u32[]{:S(2)}) collective-permute-start(bf16[80,8,128]{2,1,0:T(8,128)(2,1)S(1)} %get-tuple-element.20), channel_id=1, source_target_pairs={{2,0},{4,2},{6,4},{3,1},{5,3},{7,5},{10,8},{12,10},{14,12},{11,9},... | collective-permute-start | bytes 491528 | tf_op jit(solution)/shard_map/ppermute | solution.py:288
  12.3 20.6 %collective-permute-start = (bf16[80,8,128]{2,1,0:T(8,128)(2,1)S(1)}, bf16[80,8,128]{2,1,0:T(8,128)(2,1)S(1)}, u32[]{:S(2)}, u32[]{:S(2)}) collective-permute-start(bf16[80,8,128]{2,1,0:T(8,128)(2,1)S(1)} %get-tuple-element.21), channel_id=1, source_target_pairs={{0,2},{2,4},{4,6},{1,3},{3,5},{5,7},{8,10},{10,12},{12,14},{9,11},... | collective-permute-start | bytes 491528 | tf_op jit(solution)/shard_map/ppermute | solution.py:288
  18.4 8.9 %copy-start.2 = (f32[2,256,256]{2,1,0:T(8,128)S(1)}, f32[2,256,256]{2,1,0:T(8,128)}, u32[]{:S(2)}) copy-start(f32[2,256,256]{2,1,0:T(8,128)} %param.16) | copy-start | bytes 1572868
  26.8 1.1 %copy-start.1 = (f32[2,256,256]{2,1,0:T(8,128)S(1)}, f32[2,256,256]{2,1,0:T(8,128)}, u32[]{:S(2)}) copy-start(f32[2,256,256]{2,1,0:T(8,128)} %param.17) | copy-start | bytes 1572868
  28.1 13.7 %copy-start.5 = (f32[256]{0:T(256)S(1)}, f32[256]{0:T(256)}, u32[]{:S(2)}) copy-start(f32[256]{0:T(256)} %param.15) | copy-start | bytes 3076
  28.5 13.2 %collective-permute-start.12 = (f32[5,292,18]{1,2,0:T(8,128)S(1)}, f32[5,292,18]{1,2,0:T(8,128)S(1)}, u32[]{:S(2)}, u32[]{:S(2)}) collective-permute-start(f32[5,292,18]{1,2,0:T(8,128)S(1)} %pad_maximum_fusion.3), channel_id=1, source_target_pairs={{8,0},{16,8},{24,16},{0,24},{9,1},{17,9},{25,17},{1,25},{10,2},{18... | collective-permute-start | bytes 315368 | tf_op jit(solution)/shard_map/ppermute | solution.py:288
  31.4 10.3 %collective-permute-start.11 = (f32[5,292,18]{1,2,0:T(8,128)S(1)}, f32[5,292,18]{1,2,0:T(8,128)S(1)}, u32[]{:S(2)}, u32[]{:S(2)}) collective-permute-start(f32[5,292,18]{1,2,0:T(8,128)S(1)} %pad_maximum_fusion.2), channel_id=1, source_target_pairs={{0,8},{8,16},{16,24},{24,0},{1,9},{9,17},{17,25},{25,1},{2,10},{10... | collective-permute-start | bytes 315368 | tf_op jit(solution)/shard_map/ppermute | solution.py:288
  33.0 0.7 copy-start
  38.7 8.1 %collective-permute-start.2 = (bf16[5,144,128]{2,1,0:T(8,128)(2,1)}, bf16[5,144,128]{2,1,0:T(8,128)(2,1)S(1)}, u32[]{:S(2)}, u32[]{:S(2)}) collective-permute-start(bf16[5,144,128]{2,1,0:T(8,128)(2,1)} %get-tuple-element.13), channel_id=1, source_target_pairs={{0,8},{8,16},{16,24},{24,0},{1,9},{9,17},{17,25},{25,1},{2,10},{10... | collective-permute-start | bytes 552968 | tf_op jit(solution)/shard_map/ppermute | solution.py:288
  40.6 7.4 %collective-permute-start.3 = (bf16[5,144,128]{2,1,0:T(8,128)(2,1)}, bf16[5,144,128]{2,1,0:T(8,128)(2,1)S(1)}, u32[]{:S(2)}, u32[]{:S(2)}) collective-permute-start(bf16[5,144,128]{2,1,0:T(8,128)(2,1)} %get-tuple-element.14), channel_id=1, source_target_pairs={{8,0},{16,8},{24,16},{0,24},{9,1},{17,9},{25,17},{1,25},{10,2},{18... | collective-permute-start | bytes 552968 | tf_op jit(solution)/shard_map/ppermute | solution.py:288
  46.7 1.3 %copy-start.3 = (bf16[5,144,128]{2,1,0:T(8,128)(2,1)}, bf16[5,144,128]{2,1,0:T(8,128)(2,1)S(1)}, u32[]{:S(2)}) copy-start(bf16[5,144,128]{2,1,0:T(8,128)(2,1)S(1)} %collective-permute-done.2.west_ref) | copy-start | bytes 552964
  48.0 0.7 copy-start.4
  51.7 1.8 %collective-permute-start.4 = (f32[2,144,144]{2,1,0:T(8,128)}, f32[2,144,144]{2,1,0:T(8,128)S(1)}, u32[]{:S(2)}, u32[]{:S(2)}) collective-permute-start(f32[2,144,144]{2,1,0:T(8,128)} %frame.1), channel_id=1, source_target_pairs={{0,1},{1,0},{2,3},{3,2},{4,5},{5,4},{6,7},{7,6},{8,9},{9,8},{10,11... | collective-permute-start | bytes 497672 | tf_op jit(solution)/shard_map/ppermute | solution.py:425
  54.5 5.2 %collective-permute-start.5 = (f32[2,18,144]{2,1,0:T(8,128)S(1)}, f32[2,18,144]{2,1,0:T(8,128)S(1)}, u32[]{:S(2)}, u32[]{:S(2)}) collective-permute-start(f32[2,18,144]{2,1,0:T(8,128)S(1)} %get-tuple-element.32), channel_id=1, source_target_pairs={{0,2},{2,4},{4,6},{1,3},{3,5},{5,7},{8,10},{10,12},{12,14},{9,11},... | collective-permute-start | bytes 62216 | tf_op jit(solution)/shard_map/ppermute | solution.py:288
  58.0 6.0 %collective-permute-start.6 = (f32[2,18,144]{2,1,0:T(8,128)S(1)}, f32[2,18,144]{2,1,0:T(8,128)S(1)}, u32[]{:S(2)}, u32[]{:S(2)}) collective-permute-start(f32[2,18,144]{2,1,0:T(8,128)S(1)} %get-tuple-element.33), channel_id=1, source_target_pairs={{2,0},{4,2},{6,4},{3,1},{5,3},{7,5},{10,8},{12,10},{14,12},{11,9},... | collective-permute-start | bytes 62216 | tf_op jit(solution)/shard_map/ppermute | solution.py:288
  64.1 7.3 %collective-permute-start.7 = (f32[2,148,18]{2,1,0:T(8,128)S(1)}, f32[2,148,18]{2,1,0:T(8,128)S(1)}, u32[]{:S(2)}, u32[]{:S(2)}) collective-permute-start(f32[2,148,18]{2,1,0:T(8,128)S(1)} %get-tuple-element.30), channel_id=1, source_target_pairs={{0,8},{8,16},{16,24},{24,0},{1,9},{9,17},{17,25},{25,1},{2,10},{10... | collective-permute-start | bytes 63944 | tf_op jit(solution)/shard_map/ppermute | solution.py:288
  66.6 6.2 %collective-permute-start.8 = (f32[2,148,18]{2,1,0:T(8,128)S(1)}, f32[2,148,18]{2,1,0:T(8,128)S(1)}, u32[]{:S(2)}, u32[]{:S(2)}) collective-permute-start(f32[2,148,18]{2,1,0:T(8,128)S(1)} %get-tuple-element.31), channel_id=1, source_target_pairs={{8,0},{16,8},{24,16},{0,24},{9,1},{17,9},{25,17},{1,25},{10,2},{18... | collective-permute-start | bytes 63944 | tf_op jit(solution)/shard_map/ppermute | solution.py:288

commit v2 on v1

v2 whole, which is shorter than its diff:
```python
import functools

import jax
import jax.numpy as jnp
from jax import lax
from jax.experimental import pallas as pl
from jax.experimental.pallas import tpu as pltpu
from jax.sharding import PartitionSpec as P

HB = 8
GROUP = 16
MEMBERS = 8
SKIRT = 24
STRIP = 24
NOWHERE = -9999
LANES = 128
F32 = jnp.float32
BF16 = jnp.bfloat16


def rounded(size, step):
    return -(-size // step) * step


def iota(shape, axis):
    return lax.broadcasted_iota(jnp.int32, shape, axis)


def split(value):
    high = value.astype(BF16)
    return high, (value - high.astype(F32)).astype(BF16)


def dot(left, right, dims=(1, 0)):
    return lax.dot_general(
        left, right, (((dims[0],), (dims[1],)), ((), ())), preferred_element_type=F32
    )


def dot3(left, right, dims=(1, 0)):
    left_high, left_low = split(left)
    right_high, right_low = split(right)
    total = dot(left_high, right_low, dims) + dot(left_low, right_high, dims)
    return total + dot(left_high, right_high, dims)


def row_of(index, height):
    above = index - height - HB
    return jnp.where(index < height, index, jnp.where(index < height + HB, above, index - HB))


def packed_column(lane, level, width):
    west = (lane < LANES // 2) if level == 0 else (lane >= LANES // 2)
    cell = lane & (HB - 1)
    return jnp.where(west, cell - HB, width + cell)


def packed_member(lane):
    return (lane & (LANES // 2 - 1)) >> 3


def taps(offset, spread):
    lane = iota((8, LANES), 1)
    distance = (lane - HB).astype(F32)
    scale = jnp.full((8, LANES), 1.0, F32) * (0.5 / (spread * spread))
    shape = jnp.where(lane <= 2 * HB, jnp.exp(-(distance * distance) * scale), 0.0)
    norm = lax.rsqrt(jnp.sum(shape * shape, axis=1, keepdims=True))[:1, :1]
    far = offset.astype(F32)
    value = jnp.exp(-(far * far) * scale[:1, :1]) * norm
    return jnp.where(jnp.abs(offset) <= HB, value, 0.0)


def pack_kernel(perts_ref, above_ref, below_ref, east_ref, west_ref):
    rows = east_ref.shape[1]
    width = perts_ref.shape[2]
    lane = iota((rows, LANES), 1)
    east = jnp.zeros((rows, LANES), F32)
    west = jnp.zeros((rows, LANES), F32)
    for k in range(GROUP):
        t, level = k // 2, k % 2
        own = perts_ref[k]
        whole = jnp.concatenate(
            [own.astype(F32), above_ref[k].astype(F32), below_ref[k].astype(F32)], 0
        )
        last = whole[:, width - LANES :]
        first = whole[:, :LANES]
        slot = level * (LANES // 2) + t * HB
        other = (1 - level) * (LANES // 2) + t * HB
        last = pltpu.roll(last, (slot + HB) % LANES, 1)
        first = first if other == 0 else pltpu.roll(first, other, 1)
        east = jnp.where(lane >> 3 == slot // HB, last, east)
        west = jnp.where(lane >> 3 == other // HB, first, west)
    east_ref[0] = east.astype(BF16)
    west_ref[0] = west.astype(BF16)


def local_kernel(
    width_ref, alpha_ref, perts_ref, token_ref, sum_ref, rows_ref, cols_ref, lon_ref, lat_ref, stack_ref
):
    height, width = alpha_ref.shape[1], alpha_ref.shape[2]
    ext = height + 2 * HB

    @pl.when(pl.program_id(0) == 0)
    def _():
        sum_ref[...] = jnp.zeros_like(sum_ref)
        for level in range(2):
            spread = width_ref[level].astype(F32)
            source = iota((width, width), 0)
            high, low = split(taps(source - iota((width, width), 1), spread))
            source = iota((width, LANES), 0)
            lane = iota((width, LANES), 1)
            edge = taps(source - packed_column(lane, level, width), spread)
            for t in range(MEMBERS):
                part_high, part_low = split(jnp.where(packed_member(lane) == t, edge, 0.0))
                lon_ref[level, t, :width, :width] = high
                lon_ref[level, t, width:, :width] = low
                lon_ref[level, t, :width, width:] = part_high
                lon_ref[level, t, width:, width:] = part_low
            target = row_of(iota((ext, height), 0), height)
            high, low = split(taps(target - iota((ext, height), 1), spread))
            lat_ref[level, :, :height] = high
            lat_ref[level, :, height : 2 * height] = low
            lat_ref[level, :, 2 * height :] = high

    for level in range(2):
        packed = jnp.zeros((height, LANES), F32)
        for t in range(MEMBERS):
            field = alpha_ref[2 * t + level]
            both = dot(jnp.concatenate([field, field], 1), lon_ref[level, t])
            high, low = split(both[:, :width])
            stack_ref[:height, t * width : (t + 1) * width] = high
            stack_ref[height : 2 * height, t * width : (t + 1) * width] = high
            stack_ref[2 * height :, t * width : (t + 1) * width] = low
            packed = packed + both[:, width:]
        high, low = split(packed)
        stack_ref[:height, MEMBERS * width :] = high
        stack_ref[height : 2 * height, MEMBERS * width :] = high
        stack_ref[2 * height :, MEMBERS * width :] = low
        total = sum_ref[level]
        for pair in range(MEMBERS // 2):
            base = 2 * pair * width
            wide = dot(lat_ref[level], stack_ref[:, base : base + 2 * width])
            for side in range(2):
                k = 2 * (2 * pair + side) + level
                field = wide[:, side * width : (side + 1) * width]
                total = total + perts_ref[k].astype(F32) * field[:height]
                rows_ref[k] = field[height:]
        sum_ref[level] = total
        cols_ref[0, level] = dot(lat_ref[level], stack_ref[:, MEMBERS * width :])


def stacked_cell(index, size, base):
    cell = row_of(index, size)
    low = index - base
    cell = jnp.where(index < size + 2 * HB, cell, NOWHERE)
    cell = jnp.where((low >= 0) & (low < STRIP), low - 2 * HB, cell)
    return jnp.where((low >= STRIP) & (low < 2 * STRIP), low - STRIP + size - HB, cell)


def interpolate(cell, index, weight):
    near = jnp.where(cell == index, 1.0 - weight, 0.0)
    return near + jnp.where(cell == index + 1, weight, 0.0)


def rows_kernel(last_ref, first_ref, next_ref, previous_ref):
    next_ref[...] = last_ref[...]
    previous_ref[...] = first_ref[...]


def table(index, weight):
    size = index.shape[-1]
    row = iota((8, size), 0)
    return jnp.where(
        row == 0, index.astype(F32).reshape(1, size), jnp.where(row == 1, weight.reshape(1, size), 0.0)
    )


def fine_cols_kernel(target_ref, weight_ref, index_ref, share_ref, east_ref, west_ref):
    cols = target_ref.shape[2]
    for a, ref in enumerate((target_ref, weight_ref)):
        for level in range(2):
            start = (2 * a + level) * SKIRT
            east_ref[start : start + SKIRT] = ref[level, :, cols - LANES :].T[LANES - SKIRT :]
            west_ref[start : start + SKIRT] = ref[level, :, :LANES].T[:SKIRT]
    lon = table(index_ref[...], share_ref[...])
    east_ref[4 * SKIRT :, :LANES] = lon[:, cols - LANES :]
    west_ref[4 * SKIRT :, :LANES] = lon[:, :LANES]


def fine_rows_kernel(
    target_ref, weight_ref, index_ref, share_ref, west_ref, east_ref, next_ref, previous_ref, token_ref
):
    rows = target_ref.shape[1]
    for a, ref in enumerate((target_ref, weight_ref)):
        for level in range(2):
            start = (2 * a + level) * SKIRT
            next_ref[start : start + SKIRT] = ref[level, rows - SKIRT :]
            previous_ref[start : start + SKIRT] = ref[level, :SKIRT]
    lat = table(index_ref[...], share_ref[...])
    for side, ref in enumerate((west_ref, east_ref)):
        lanes = slice(side * LANES, (side + 1) * LANES)
        next_ref[4 * SKIRT : 8 * SKIRT, lanes] = ref[: 4 * SKIRT, rows - LANES :]
        previous_ref[4 * SKIRT : 8 * SKIRT, lanes] = ref[: 4 * SKIRT, :LANES]
    next_ref[8 * SKIRT :, :LANES] = lat[:, rows - LANES :]
    previous_ref[8 * SKIRT :, :LANES] = lat[:, :LANES]
    token_ref[...] = lat[:, :LANES]


def frame_kernel(sum_ref, rows_ref, cols_ref, above_ref, below_ref, west_ref, east_ref, out_ref):
    height, width = sum_ref.shape[1], sum_ref.shape[2]
    ext = height + 2 * HB
    groups = west_ref.shape[0]
    half = iota((ext, LANES), 1) < LANES // 2
    for level in range(2):
        edge = jnp.zeros((2 * HB, width), F32)
        packed = jnp.zeros((ext, LANES), F32)
        for group in range(groups):
            for t in range(MEMBERS):
                k = group * GROUP + 2 * t + level
                halo = jnp.concatenate([above_ref[k].astype(F32), below_ref[k].astype(F32)], 0)
                edge = edge + halo * rows_ref[k]
            west = west_ref[group].astype(F32)
            east = east_ref[group].astype(F32)
            cell = jnp.where(half, west, east) if level == 0 else jnp.where(half, east, west)
            packed = packed + cell * cols_ref[group, level]
        column = packed_column(iota((LANES, LANES), 0), level, width)
        slot = iota((LANES, LANES), 1)
        target = jnp.where(slot < HB, slot - HB, jnp.where(slot < 2 * HB, slot - HB + width, NOWHERE))
        gather = (column == target).astype(BF16)
        high, low = split(packed)
        out_ref[level, :height, :width] = sum_ref[level]
        out_ref[level, height:, :width] = edge
        out_ref[level, :, width:] = dot(high, gather) + dot(low, gather)


def total_kernel(mine_ref, other_ref, total_ref, next_ref, previous_ref):
    total = mine_ref[...] + other_ref[...]
    height = total.shape[1] - 2 * HB
    total_ref[...] = total
    next_ref[:, : 2 * HB] = total[:, height - 2 * HB : height]
    next_ref[:, 2 * HB :] = total[:, height + HB :]
    previous_ref[:, :HB] = total[:, height : height + HB]
    previous_ref[:, HB:] = total[:, : 2 * HB]


def strips_kernel(width, total_ref, above_ref, below_ref, stack_ref, east_ref, west_ref):
    ext, lanes = total_ref.shape[1], total_ref.shape[2]
    rows = stack_ref.shape[1]
    column = stacked_cell(iota((STRIP, lanes), 1), width, lanes)
    number = iota((STRIP, lanes), 0)
    pick_east = (column == number + width - 2 * HB).astype(BF16)
    pick_west = (column == number - HB).astype(BF16)
    for level in range(2):
        stack_ref[level, :ext] = total_ref[level]
        stack_ref[level, ext : ext + STRIP] = above_ref[level]
        stack_ref[level, ext + STRIP : ext + 2 * STRIP] = below_ref[level]
        stack_ref[level, ext + 2 * STRIP :] = jnp.zeros((rows - ext - 2 * STRIP, lanes), F32)
        high, low = split(stack_ref[level])
        part = slice(level * STRIP, (level + 1) * STRIP)
        east_ref[part] = dot(pick_east, high, (1, 1)) + dot(pick_east, low, (1, 1))
        west_ref[part] = dot(pick_west, high, (1, 1)) + dot(pick_west, low, (1, 1))


def fine_kernel(
    lon_total,
    start_ref,
    stack_ref,
    strip_west_ref,
    strip_east_ref,
    target_ref,
    weight_ref,
    lat_index_ref,
    lat_share_ref,
    lon_index_ref,
    lon_share_ref,
    west_ref,
    east_ref,
    above_ref,
    below_ref,
    inc_ref,
    own_ref,
    edge_ref,
    wide_ref,
    miss_ref,
):
    ext, width = own_ref.shape[1], own_ref.shape[2]
    height = ext - 2 * HB
    rows, cols = target_ref.shape[1], target_ref.shape[2]
    lanes = stack_ref.shape[2]
    span = rows + LANES
    lane = iota((8, LANES), 1)
    first = iota((8, LANES), 0) == 0

    def side(low, high):
        low = pltpu.roll(low, SKIRT, 1)
        high = pltpu.roll(high, SKIRT, 1)
        blank = jnp.where(first, 1.0e6, 0.0)
        return jnp.where(lane < SKIRT, low, jnp.where(lane < 2 * SKIRT, high, blank))

    def corner(low, high):
        spot = iota(low.shape, 1)
        low = pltpu.roll(low, SKIRT, 1)
        high = pltpu.roll(high, SKIRT, 1)
        return jnp.where(spot < SKIRT, low, jnp.where(spot < 2 * SKIRT, high, 0.0))

    lat_side = side(above_ref[8 * SKIRT :, :LANES], below_ref[8 * SKIRT :, :LANES])
    lat = jnp.concatenate([table(lat_index_ref[...], lat_share_ref[...]), lat_side], 1)
    lon_side = side(west_ref[4 * SKIRT :, :LANES], east_ref[4 * SKIRT :, :LANES])
    lon = jnp.concatenate([table(lon_index_ref[...], lon_share_ref[...]), lon_side], 1)
    lat_cell = lat[0:1].astype(jnp.int32) - start_ref[0]
    lat_share = lat[1:2]
    lon_cell = lon[0:1].astype(jnp.int32) - start_ref[1]
    lon_cell = jnp.where(lon_cell < -(lon_total // 2), lon_cell + lon_total, lon_cell)
    wrap = (lon_cell >= lon_total // 2) & (lon_cell < lon_total)
    lon_cell = jnp.where(wrap, lon_cell - lon_total, lon_cell)
    lon_share = lon[1:2]
    upright = jnp.concatenate([lat_cell.astype(F32), lat_share, jnp.zeros((6, span), F32)], 0).T
    lat_cell_up, lat_share_up = upright[:, 0:1].astype(jnp.int32), upright[:, 1:2]
    upright = jnp.concatenate(
        [lon_cell.astype(F32), lon_share, jnp.zeros((6, cols + LANES), F32)], 0
    ).T
    lon_cell_up, lon_share_up = upright[:, 0:1].astype(jnp.int32), upright[:, 1:2]
    beside = slice(cols, cols + 2 * SKIRT)

    tall = stack_ref.shape[1]
    lat_map = interpolate(
        stacked_cell(iota((span, tall), 1), height, ext), lat_cell_up, lat_share_up
    )
    broad = lanes + LANES
    lon_map = interpolate(
        stacked_cell(iota((broad, cols), 0), width, lanes), lon_cell[:, :cols], lon_share[:, :cols]
    )
    side_map = interpolate(
        stacked_cell(iota((2 * SKIRT, broad), 1), width, lanes),
        lon_cell_up[beside],
        lon_share_up[beside],
    )
    lat_back = interpolate(row_of(iota((ext, span), 0), height), lat_cell, lat_share)
    lat_high, lat_low = split(lat_map)
    wide_ref[:, lanes:] = jnp.zeros((span, LANES), F32)
    miss_ref[rows + 2 * SKIRT :] = jnp.zeros((span - rows - 2 * SKIRT, cols), F32)

    for level in range(2):
        wide_ref[:, :lanes] = dot3(lat_map, stack_ref[level])
        part = slice(level * STRIP, (level + 1) * STRIP)
        strips = jnp.concatenate([strip_west_ref[part], strip_east_ref[part]], 0)
        wide_ref[:, lanes : lanes + 2 * STRIP] = dot3(lat_map, strips, (1, 1))
        increment = dot3(wide_ref[...], lon_map)
        inc_ref[level] = increment[:rows]
        miss_ref[:rows] = weight_ref[level] * (increment[:rows] - target_ref[level])
        target_rows = slice(level * SKIRT, (level + 1) * SKIRT)
        weight_rows = slice((2 + level) * SKIRT, (3 + level) * SKIRT)
        for number, ref in enumerate((above_ref, below_ref)):
            start = rows + number * SKIRT
            part = increment[start : start + SKIRT] - ref[target_rows]
            miss_ref[start : start + SKIRT] = ref[weight_rows] * part
        beyond = dot3(side_map, wide_ref[...], (1, 1))
        pieces = []
        for number, ref in enumerate((west_ref, east_ref)):
            tile = slice(number * LANES, (number + 1) * LANES)

            def extended(at):
                start = 4 * SKIRT + at.start
                stop = 4 * SKIRT + at.stop
                last = corner(above_ref[start:stop, tile], below_ref[start:stop, tile])
                return jnp.concatenate([ref[at], last], 1)

            part = beyond[number * SKIRT : (number + 1) * SKIRT]
            pieces.append(extended(weight_rows) * (part - extended(target_rows)))
        beyond = jnp.concatenate(pieces, 0)
        lane_wide = iota((1, width + LANES), 1)
        column = jnp.where(
            lane_wide < width, lane_wide, packed_column(lane_wide - width, level, width)
        )
        back = interpolate(column, lon_cell_up[:cols], lon_share_up[:cols])
        side_back = interpolate(column, lon_cell_up[beside], lon_share_up[beside])
        by_lon = dot3(miss_ref[...], back) + dot3(beyond, side_back, (0, 0))
        residual = dot3(lat_back, by_lon)
        own_ref[level] = residual[:, :width]
        edge_ref[level] = residual[:, width:]


def gradient_kernel(
    width_ref, alpha_ref, perts_ref, above_ref, below_ref, west_ref, east_ref, own_ref, edge_ref, out_ref,
    lon_ref, lat_ref, stack_ref,
):
    height, width = alpha_ref.shape[1], alpha_ref.shape[2]
    ext = height + 2 * HB

    @pl.when(pl.program_id(0) == 0)
    def _():
        for level in range(2):
            spread = width_ref[level].astype(F32)
            source = iota((width, width), 0)
            high, low = split(taps(source - iota((width, width), 1), spread))
            lane = iota((LANES, width), 0)
            edge = taps(packed_column(lane, level, width) - iota((LANES, width), 1), spread)
            for t in range(MEMBERS):
                part_high, part_low = split(jnp.where(packed_member(lane) == t, edge, 0.0))
                lon_ref[level, t, :width, :width] = high
                lon_ref[level, t, :width, width:] = low
                lon_ref[level, t, width:, :width] = part_high
                lon_ref[level, t, width:, width:] = part_low
            source = row_of(iota((height, ext), 1), height)
            high, low = split(taps(source - iota((height, ext), 0), spread))
            lat_ref[level, :, :ext] = high
            lat_ref[level, :, ext : 2 * ext] = low
            lat_ref[level, :, 2 * ext :] = high

    half = iota((ext, LANES), 1) < LANES // 2
    west = west_ref[0].astype(F32)
    east = east_ref[0].astype(F32)

    def stack(value, start, size):
        high, low = split(value)
        stack_ref[:ext, start : start + size] = high
        stack_ref[ext : 2 * ext, start : start + size] = high
        stack_ref[2 * ext :, start : start + size] = low

    for level in range(2):
        cell = jnp.where(half, west, east) if level == 0 else jnp.where(half, east, west)
        stack(cell * edge_ref[level], MEMBERS * width, LANES)
        for t in range(MEMBERS):
            k = 2 * t + level
            field = jnp.concatenate(
                [perts_ref[k].astype(F32), above_ref[k].astype(F32), below_ref[k].astype(F32)], 0
            )
            stack(field * own_ref[level], t * width, width)
        edge_high, edge_low = split(dot(lat_ref[level], stack_ref[:, MEMBERS * width :]))
        for pair in range(MEMBERS // 2):
            base = 2 * pair * width
            wide = dot(lat_ref[level], stack_ref[:, base : base + 2 * width])
            for side in range(2):
                t = 2 * pair + side
                k = 2 * t + level
                high, low = split(wide[:, side * width : (side + 1) * width])
                main = dot(jnp.concatenate([high, edge_high], 1), lon_ref[level, t])
                rest = dot(jnp.concatenate([low, edge_low], 1), lon_ref[level, t, :, :width])
                total = main[:, :width] + main[:, width:] + rest
                out_ref[k] = alpha_ref[k].astype(F32) + total


def ring(axis, periodic):
    count = lax.axis_size(axis)
    forward = [(i, i + 1) for i in range(count - 1)]
    if periodic:
        forward.append((count - 1, 0))
    return forward, [(target, source) for source, target in forward]


def exchange(to_next, to_previous, axis, periodic):
    forward, backward = ring(axis, periodic)
    return lax.ppermute(to_next, axis, forward), lax.ppermute(to_previous, axis, backward)


def vmem(*shape):
    return pl.BlockSpec(shape, lambda s: (0,) * len(shape))


def grouped(*shape):
    return pl.BlockSpec(shape, lambda s: (s,) + (0,) * (len(shape) - 1))


def shaped(shape, dtype=F32):
    return jax.ShapeDtypeStruct(shape, dtype)


def body(
    alpha_fields,
    member_perts,
    band_widths,
    lat_index,
    lat_weight,
    lon_index,
    lon_weight,
    innovation,
    obs_weight,
):
    members, levels, height, width = alpha_fields.shape
    fields = members * levels
    groups = fields // GROUP
    ext = height + 2 * HB
    fine_h, fine_w = innovation.shape[1], innovation.shape[2]
    alpha = alpha_fields.reshape(fields, height, width)
    perts = member_perts.reshape(fields, height, width)
    smem = pl.BlockSpec(memory_space=pltpu.SMEM)
    anywhere = pl.BlockSpec(memory_space=pl.ANY)
    limit = min(60, 16 * (width // LANES)) * 1024 * 1024
    lanes = rounded(width + 2 * HB, LANES)
    tall = rounded(ext + 2 * STRIP, LANES)

    def params(*semantics):
        return pltpu.CompilerParams(dimension_semantics=semantics, vmem_limit_bytes=limit)

    def call(kernel, out_shape, name, flops=10**8, **more):
        return pl.pallas_call(
            kernel,
            out_shape=out_shape,
            compiler_params=params(*(("arbitrary",) if "grid" in more else ())),
            name=name,
            cost_estimate=pl.CostEstimate(flops=flops, bytes_accessed=10**6, transcendentals=0),
            **more,
        )

    edge = shaped((fields, HB, width), BF16)
    to_next, to_previous = call(
        rows_kernel,
        [edge, edge],
        "rows",
        in_specs=[
            pl.BlockSpec((fields, HB, width), lambda s: (0, height // HB - 1, 0)),
            pl.BlockSpec((fields, HB, width), lambda s: (0, 0, 0)),
        ],
        grid=(1,),
        out_specs=[vmem(fields, HB, width)] * 2,
    )(perts, perts)
    above, below = exchange(to_next, to_previous, "gy", False)

    side = shaped((4 * SKIRT + 8, fine_h))
    to_next, to_previous = call(fine_cols_kernel, [side, side], "fine_cols")(
        innovation, obs_weight, lon_index, lon_weight
    )
    fine_west, fine_east = exchange(to_next, to_previous, "gx", True)

    packed = shaped((groups, ext, LANES), BF16)
    to_next, to_previous = call(
        pack_kernel,
        [packed, packed],
        "pack",
        grid=(groups,),
        in_specs=[grouped(GROUP, height, width)] + [grouped(GROUP, HB, width)] * 2,
        out_specs=[grouped(1, ext, LANES)] * 2,
    )(perts, above, below)
    west, east = exchange(to_next, to_previous, "gx", True)

    strip = shaped((8 * SKIRT + 8, fine_w))
    to_next, to_previous, token = call(
        fine_rows_kernel, [strip, strip, shaped((8, LANES))], "fine_rows"
    )(innovation, obs_weight, lat_index, lat_weight, fine_west, fine_east)
    fine_above, fine_below = exchange(to_next, to_previous, "gy", False)

    partial, edge_rows, edge_cols = call(
        local_kernel,
        [
            shaped((2, height, width)),
            shaped((fields, 2 * HB, width)),
            shaped((groups, 2, ext, LANES)),
        ],
        "local",
        flops=10**10,
        grid=(groups,),
        in_specs=[
            smem,
            grouped(GROUP, height, width),
            grouped(GROUP, height, width),
            anywhere,
        ],
        out_specs=[
            vmem(2, height, width),
            grouped(GROUP, 2 * HB, width),
            grouped(1, 2, ext, LANES),
        ],
        scratch_shapes=[
            pltpu.VMEM((2, MEMBERS, 2 * width, width + LANES), BF16),
            pltpu.VMEM((2, ext, 3 * height), BF16),
            pltpu.VMEM((3 * height, MEMBERS * width + LANES), BF16),
        ],
    )(band_widths, alpha, perts, token)

    framed = call(frame_kernel, shaped((2, ext, width + LANES)), "frame")(
        partial, edge_rows, edge_cols, above, below, west, east
    )
    count = lax.axis_size("ma")
    other = lax.ppermute(framed, "ma", [(i, (i + 1) % count) for i in range(count)])
    strip = shaped((2, STRIP, lanes))
    framed, to_next, to_previous = call(
        total_kernel, [shaped((2, ext, lanes)), strip, strip], "total"
    )(framed, other)
    north, south = exchange(to_next, to_previous, "gy", False)
    strip = shaped((2 * STRIP, tall))
    stack, to_next, to_previous = call(
        functools.partial(strips_kernel, width), [shaped((2, tall, lanes)), strip, strip], "strips"
    )(framed, north, south)
    strip_west, strip_east = exchange(to_next, to_previous, "gx", True)

    starts = jnp.stack([lax.axis_index("gy") * height, lax.axis_index("gx") * width])
    lon_total = width * lax.axis_size("gx")
    everything = [pl.BlockSpec(memory_space=pltpu.VMEM)] * 13
    increment, own, edge = call(
        functools.partial(fine_kernel, lon_total),
        [shaped((2, fine_h, fine_w)), shaped((2, ext, width)), shaped((2, ext, LANES))],
        "fine",
        in_specs=[smem] + everything,
        scratch_shapes=[
            pltpu.VMEM((fine_h + LANES, lanes + LANES), F32),
            pltpu.VMEM((fine_h + LANES, fine_w), F32),
        ],
    )(
        starts,
        stack,
        strip_west,
        strip_east,
        innovation,
        obs_weight,
        lat_index,
        lat_weight,
        lon_index,
        lon_weight,
        fine_west,
        fine_east,
        fine_above,
        fine_below,
    )

    gradient = call(
        gradient_kernel,
        shaped((fields, height, width)),
        "gradient",
        grid=(groups,),
        in_specs=[
            smem,
            grouped(GROUP, height, width),
            grouped(GROUP, height, width),
            grouped(GROUP, HB, width),
            grouped(GROUP, HB, width),
            grouped(1, ext, LANES),
            grouped(1, ext, LANES),
            vmem(2, ext, width),
            vmem(2, ext, LANES),
        ],
        out_specs=grouped(GROUP, height, width),
        scratch_shapes=[
            pltpu.VMEM((2, MEMBERS, width + LANES, 2 * width), BF16),
            pltpu.VMEM((2, height, 3 * ext), BF16),
            pltpu.VMEM((3 * ext, MEMBERS * width + LANES), BF16),
        ],
    )(band_widths, alpha, perts, above, below, west, east, own, edge)
    return increment, gradient.reshape(alpha_fields.shape)


def solution(mesh):
    placed = (
        P("ma", None, "gy", "gx"),
        P("ma", None, "gy", "gx"),
        P(),
        P("gy"),
        P("gy"),
        P("gx"),
        P("gx"),
        P(None, "gy", "gx"),
        P(None, "gy", "gx"),
    )
    return jax.shard_map(
        body,
        mesh=mesh,
        in_specs=placed,
        out_specs=(P(None, "gy", "gx"), P("ma", None, "gy", "gx")),
        check_vma=False,
    )
```

time: 96.8 us -> 79.7 us (0.82)
  other arithmetic: 8.58 us -> 0.07 us
  Pallas kernels: 38.5 us -> 30.6 us
  waiting for transfers between devices: 13.4 us -> 11.7 us
  starting transfers between devices: 26.4 us -> 27.8 us
    pallas_call x5 -> x10, Pallas kernels: 38.5 us -> 30.6 us  [the longest x1 13.3 us: body(): call(gradient_kernel, shaped((fields, height, width)), 'gradient', grid=(...]
    unnamed x17 -> x44, local copies, waits for them, and re-layouts: 2.06 us -> 8.04 us
    slice x25 -> x0, local copies, waits for them, and re-layouts: 4.22 us -> none  [the longest x1 1.02 us: body(): above, below = exchange(perts[:, height - HB:], perts[:, :HB], 'gy', False)]
    concatenate x10 -> x0, other arithmetic: 3.02 us -> none  [the longest x1 1.37 us: body(): weight = jnp.pad(jnp.concatenate([left[2:4], weight, right[2:4]], 2), pads)]
    add x4 -> x0, other arithmetic: 2.06 us -> none  [the longest x1 1 us: body(): coarse = place(framed, 2) + place(before, 0) + place(after, gap)]
    ppermute x6, waiting for transfers between devices: 6.99 us -> 5.33 us  [exchange(): lax.ppermute(to_previous, axis, backward)]
    convert_element_type x3 -> x0, other arithmetic: 1.38 us -> none  [the longest x1 0.68 us: body(): lat_index.astype(F32)[:, None]]
    another operation x3 -> x1, other arithmetic: 1.18 us -> 0.07 us  [body(): jnp.stack([lax.axis_index('gy') * height, lax.axis_index('gx') * width])]
  transfers between devices with their start and end apart: 13 -> 13, of which waited for: 7 -> 5; matrix products, arithmetic and copies ran while one was open for 11% -> 0% of each run, Pallas kernels for 14% -> 12%
where the time goes in v2:
time: 79.7 us; the launch traced here: 79.2 us
  Pallas kernels  30.6 us (38%)
  starting transfers between devices  27.8 us (35%)
  waiting for transfers between devices  11.7 us (15%)
  local copies, waits for them, and re-layouts  8.04 us (10%)
  between operations  0.93 us (1%)
    ppermute x6, starting transfers between devices, exchange(): lax.ppermute(to_next, axis, forward)  18.5 us
    pallas_call x1, Pallas kernels, body(): call(gradient_kernel, shaped((fields, height, width)), 'gradient', grid=(...  13.3 us
    ppermute x6, starting transfers between devices, exchange(): lax.ppermute(to_previous, axis, backward)  9.3 us
    unnamed x44, local copies, waits for them, and re-layouts  8.04 us
    pallas_call x1, Pallas kernels, body(): call(local_kernel, [shaped((2, height, width)), shaped((fields, 2 * HB, w...  6.67 us
    ppermute x6, waiting for transfers between devices, exchange(): lax.ppermute(to_next, axis, forward)  6.38 us
    pallas_call x1, Pallas kernels, body(): call(functools.partial(fine_kernel, lon_total), [shaped((2, fine_h, fine_...  5.46 us
    ppermute x6, waiting for transfers between devices, exchange(): lax.ppermute(to_previous, axis, backward)  5.33 us
  transfers between devices with their start and end apart: 13, of which 5 were waited for; matrix products, arithmetic and copies ran while one was open for 0% of the time, Pallas kernels for 12%

profile of v2, /device:TPU:0, one launch (start us, length us, event | category | flops | bytes accessed | tf_op | source)
XLA Modules:
  0.0 79.2 jit_solution(9695471663315549159)
XLA Ops:
  0.6 1.7 %copy-done = bf16[40,2,128,128]{3,2,1,0:T(8,128)(2,1)S(1)} copy-done((bf16[40,2,128,128]{3,2,1,0:T(8,128)(2,1)S(1)}, bf16[40,2,128,128]{3,2,1,0:T(8,128)(2,1)}, u32[]{:S(2)}) %copy-start) | copy-done | bytes 2621464
  2.4 0.0 copy-start.17
  2.4 0.1 rows.1
  2.5 5.2 %collective-permute-start.2 = (bf16[80,8,128]{2,1,0:T(8,128)(2,1)S(1)}, bf16[80,8,128]{2,1,0:T(8,128)(2,1)S(1)}, u32[]{:S(2)}, u32[]{:S(2)}) collective-permute-start(bf16[80,8,128]{2,1,0:T(8,128)(2,1)S(1)} %get-tuple-element.29), channel_id=1, source_target_pairs={{0,2},{2,4},{4,6},{1,3},{3,5},{5,7},{8,10},{10,12},{12,14},{9,11},... | collective-permute-start | bytes 491528 | tf_op jit(solution)/shard_map/ppermute | solution.py:453
  7.7 0.0 copy-start.5
  7.8 0.0 copy-start.21
  7.8 1.6 %collective-permute-start.3 = (bf16[80,8,128]{2,1,0:T(8,128)(2,1)S(1)}, bf16[80,8,128]{2,1,0:T(8,128)(2,1)S(1)}, u32[]{:S(2)}, u32[]{:S(2)}) collective-permute-start(bf16[80,8,128]{2,1,0:T(8,128)(2,1)S(1)} %get-tuple-element.30), channel_id=1, source_target_pairs={{2,0},{4,2},{6,4},{3,1},{5,3},{7,5},{10,8},{12,10},{14,12},{11,9},... | collective-permute-start | bytes 491528 | tf_op jit(solution)/shard_map/ppermute | solution.py:453
  9.4 0.3 fine_cols.1
  9.7 1.5 %collective-permute-start = (f32[104,256]{1,0:T(8,128)S(1)}, f32[104,256]{1,0:T(8,128)S(1)}, u32[]{:S(2)}, u32[]{:S(2)}) collective-permute-start(f32[104,256]{1,0:T(8,128)S(1)} %get-tuple-element.23), channel_id=1, source_target_pairs={{0,8},{8,16},{16,24},{24,0},{1,9},{9,17},{17,25},{25,1},{2,10},{10... | collective-permute-start | bytes 319496 | tf_op jit(solution)/shard_map/ppermute | solution.py:453
  11.2 1.4 %collective-permute-start.1 = (f32[104,256]{1,0:T(8,128)S(1)}, f32[104,256]{1,0:T(8,128)S(1)}, u32[]{:S(2)}, u32[]{:S(2)}) collective-permute-start(f32[104,256]{1,0:T(8,128)S(1)} %get-tuple-element.24), channel_id=1, source_target_pairs={{8,0},{16,8},{24,16},{0,24},{9,1},{17,9},{25,17},{1,25},{10,2},{18... | collective-permute-start | bytes 319496 | tf_op jit(solution)/shard_map/ppermute | solution.py:453
  12.7 3.7 %collective-permute-done.west_ref = f32[104,256]{1,0:T(8,128)S(1)} collective-permute-done((f32[104,256]{1,0:T(8,128)S(1)}, f32[104,256]{1,0:T(8,128)S(1)}, u32[]{:S(2)}, u32[]{:S(2)}) %collective-permute-start) | collective-permute-done | bytes 106528 | tf_op jit(solution)/shard_map/ppermute | solution.py:453
  16.3 1.1 %collective-permute-done.1.east_ref = f32[104,256]{1,0:T(8,128)S(1)} collective-permute-done((f32[104,256]{1,0:T(8,128)S(1)}, f32[104,256]{1,0:T(8,128)S(1)}, u32[]{:S(2)}, u32[]{:S(2)}) %collective-permute-start.1) | collective-permute-done | bytes 106528 | tf_op jit(solution)/shard_map/ppermute | solution.py:453
  17.4 0.8 fine_rows.1
  18.2 0.0 collective-permute-done.2.above_ref
  18.2 0.0 collective-permute-done.3.below_ref
  18.2 1.8 %pack.1 = (bf16[5,144,128]{2,1,0:T(8,128)(2,1)S(1)}, bf16[5,144,128]{2,1,0:T(8,128)(2,1)S(1)}) custom-call(bf16[80,128,128]{2,1,0:T(8,128)(2,1)S(1)} %bitcast.7, bf16[80,8,128]{2,1,0:T(8,128)(2,1)S(1)} %collective-permute-done.2.above_ref, bf16[80,8,128]{2,1,0:T(8,128)(2,1)S(1)} %collective-permute-done.3.below_ref), custom_call_target="tpu_custom_call" | custom-call | flops 100000000 | bytes 1000000 | tf_op jit(solution)/shard_map/pack/pallas_call | solution.py:526
  20.0 1.6 %collective-permute-start.4 = (bf16[5,144,128]{2,1,0:T(8,128)(2,1)S(1)}, bf16[5,144,128]{2,1,0:T(8,128)(2,1)S(1)}, u32[]{:S(2)}, u32[]{:S(2)}) collective-permute-start(bf16[5,144,128]{2,1,0:T(8,128)(2,1)S(1)} %get-tuple-element.31), channel_id=1, source_target_pairs={{0,8},{8,16},{16,24},{24,0},{1,9},{9,17},{17,25},{25,1},{2,10},{10... | collective-permute-start | bytes 552968 | tf_op jit(solution)/shard_map/ppermute | solution.py:453
  21.6 1.4 %collective-permute-start.5 = (bf16[5,144,128]{2,1,0:T(8,128)(2,1)S(1)}, bf16[5,144,128]{2,1,0:T(8,128)(2,1)S(1)}, u32[]{:S(2)}, u32[]{:S(2)}) collective-permute-start(bf16[5,144,128]{2,1,0:T(8,128)(2,1)S(1)} %get-tuple-element.32), channel_id=1, source_target_pairs={{8,0},{16,8},{24,16},{0,24},{9,1},{17,9},{25,17},{1,25},{10,2},{18... | collective-permute-start | bytes 552968 | tf_op jit(solution)/shard_map/ppermute | solution.py:453
  23.0 6.7 %local.1 = (f32[2,128,128]{2,1,0:T(8,128)S(1)}, f32[80,16,128]{2,1,0:T(8,128)S(1)}, f32[5,2,144,128]{3,2,1,0:T(8,128)S(1)}) custom-call(s32[2]{0:T(128)S(1)} %copy-done.21, bf16[80,128,128]{2,1,0:T(8,128)(2,1)S(1)} %bitcast.10, bf16[80,128,128]{2,1,0:T(8,128)(2,1)S(1)} %bitcast.8, f32[8,128]{1,0:T(8,128)S(1)} %get-tuple-element.25.token_ref), custom_call_target="tpu_custom_call" | custom-call | flops 10000000000 | bytes 1000000 | tf_op jit(solution)/shard_map/local/pallas_call | solution.py:542
  29.7 0.0 collective-permute-done.4.west_ref
  29.7 0.0 collective-permute-done.5.east_ref
  29.8 0.4 frame.1.mine_ref
  30.1 0.1 collective-permute-start.6
  30.2 5.0 %collective-permute-start.11 = (f32[200,256]{1,0:T(8,128)}, f32[200,256]{1,0:T(8,128)}, u32[]{:S(2)}, u32[]{:S(2)}) collective-permute-start(f32[200,256]{1,0:T(8,128)} %get-tuple-element.39), channel_id=1, source_target_pairs={{0,2},{2,4},{4,6},{1,3},{3,5},{5,7},{8,10},{10,12},{12,14},{9,11},... | collective-permute-start | bytes 614408 | tf_op jit(solution)/shard_map/ppermute | solution.py:453
  35.2 1.3 %collective-permute-start.12 = (f32[200,256]{1,0:T(8,128)}, f32[200,256]{1,0:T(8,128)}, u32[]{:S(2)}, u32[]{:S(2)}) collective-permute-start(f32[200,256]{1,0:T(8,128)} %get-tuple-element.40), channel_id=1, source_target_pairs={{2,0},{4,2},{6,4},{3,1},{5,3},{7,5},{10,8},{12,10},{14,12},{11,9},... | collective-permute-start | bytes 614408 | tf_op jit(solution)/shard_map/ppermute | solution.py:453
  36.5 0.0 collective-permute-done.6.other_ref
  36.5 0.7 total.1
  37.1 0.7 copy-done.15
  37.9 4.5 %collective-permute-start.7 = (f32[2,24,256]{2,1,0:T(8,128)}, f32[2,24,256]{2,1,0:T(8,128)S(1)}, u32[]{:S(2)}, u32[]{:S(2)}) collective-permute-start(f32[2,24,256]{2,1,0:T(8,128)} %get-tuple-element.34), channel_id=1, source_target_pairs={{0,2},{2,4},{4,6},{1,3},{3,5},{5,7},{8,10},{10,12},{12,14},{9,11},... | collective-permute-start | bytes 147464 | tf_op jit(solution)/shard_map/ppermute | solution.py:453
  42.4 1.3 %collective-permute-start.8 = (f32[2,24,256]{2,1,0:T(8,128)}, f32[2,24,256]{2,1,0:T(8,128)}, u32[]{:S(2)}, u32[]{:S(2)}) collective-permute-start(f32[2,24,256]{2,1,0:T(8,128)} %get-tuple-element.35), channel_id=1, source_target_pairs={{2,0},{4,2},{6,4},{3,1},{5,3},{7,5},{10,8},{12,10},{14,12},{11,9},... | collective-permute-start | bytes 147464 | tf_op jit(solution)/shard_map/ppermute | solution.py:453
  43.7 0.7 collective-permute-done.7.above_ref
  44.5 4.3 %collective-permute-done.8.below_ref = f32[2,24,256]{2,1,0:T(8,128)} collective-permute-done((f32[2,24,256]{2,1,0:T(8,128)}, f32[2,24,256]{2,1,0:T(8,128)}, u32[]{:S(2)}, u32[]{:S(2)}) %collective-permute-start.8) | collective-permute-done | bytes 49184 | tf_op jit(solution)/shard_map/ppermute | solution.py:453
  48.7 1.0 %copy-done.16 = f32[2,144,256]{2,1,0:T(8,128)S(1)} copy-done((f32[2,144,256]{2,1,0:T(8,128)S(1)}, f32[2,144,256]{2,1,0:T(8,128)}, u32[]{:S(2)}) %copy-start.16) | copy-done | bytes 294936
  49.7 1.2 %strips.1 = (f32[2,256,256]{2,1,0:T(8,128)S(1)}, f32[48,256]{1,0:T(8,128)S(1)}, f32[48,256]{1,0:T(8,128)S(1)}) custom-call(f32[2,144,256]{2,1,0:T(8,128)S(1)} %copy-done.16, f32[2,24,256]{2,1,0:T(8,128)S(1)} %collective-permute-done.7.above_ref, f32[2,24,256]{2,1,0:T(8,128)} %collective-permute-done.8.below_ref), custom_call_target="tpu_custom_call" | custom-call | flops 100000000 | bytes 1000000 | tf_op jit(solution)/shard_map/strips/pallas_call | solution.py:581
  50.9 0.6 collective-permute-start.9
  51.5 2.3 %collective-permute-start.10 = (f32[48,256]{1,0:T(8,128)S(1)}, f32[48,256]{1,0:T(8,128)S(1)}, u32[]{:S(2)}, u32[]{:S(2)}) collective-permute-start(f32[48,256]{1,0:T(8,128)S(1)} %get-tuple-element.38), channel_id=1, source_target_pairs={{8,0},{16,8},{24,16},{0,24},{9,1},{17,9},{25,17},{1,25},{10,2},{18... | collective-permute-start | bytes 147464 | tf_op jit(solution)/shard_map/ppermute | solution.py:453
  53.8 0.1 pad_add_fusion.start_ref
  53.9 0.0 collective-permute-done.11.above_ref
  53.9 0.0 collective-permute-done.12.below_ref
  53.9 2.0 %collective-permute-done.9.strip_west_ref = f32[48,256]{1,0:T(8,128)S(1)} collective-permute-done((f32[48,256]{1,0:T(8,128)S(1)}, f32[48,256]{1,0:T(8,128)S(1)}, u32[]{:S(2)}, u32[]{:S(2)}) %collective-permute-start.9) | collective-permute-done | bytes 49184 | tf_op jit(solution)/shard_map/ppermute | solution.py:453
  55.9 0.0 collective-permute-done.10.strip_east_ref
  55.9 1.0 %copy-done.4 = f32[2,256,256]{2,1,0:T(8,128)S(1)} copy-done((f32[2,256,256]{2,1,0:T(8,128)S(1)}, f32[2,256,256]{2,1,0:T(8,128)}, u32[]{:S(2)}) %copy-start.4) | copy-done | bytes 524312
  56.9 0.9 %copy-done.12 = f32[104,256]{1,0:T(8,128)S(1)} copy-done((f32[104,256]{1,0:T(8,128)S(1)}, f32[104,256]{1,0:T(8,128)}, u32[]{:S(2)}) %copy-start.12) | copy-done | bytes 106520
  57.8 0.9 %copy-done.14 = f32[104,256]{1,0:T(8,128)S(1)} copy-done((f32[104,256]{1,0:T(8,128)S(1)}, f32[104,256]{1,0:T(8,128)}, u32[]{:S(2)}) %copy-start.14) | copy-done | bytes 106520
  58.7 5.5 %fine.1 = (f32[2,256,256]{2,1,0:T(8,128)}, f32[2,144,128]{2,1,0:T(8,128)S(1)}, f32[2,144,128]{2,1,0:T(8,128)S(1)}) custom-call(s32[2]{0:T(128)S(1)} %pad_add_fusion.start_ref, f32[2,256,256]{2,1,0:T(8,128)S(1)} %get-tuple-element.36.stack_ref, f32[48,256]{1,0:T(8,128)S(1)} %collective-permute-done.9.strip_west_ref, ...), custom_call_target="tpu_custom_call" | custom-call | flops 100000000 | bytes 1000000 | tf_op jit(solution)/shard_map/fine/pallas_call | solution.py:589
  64.2 0.0 copy-start.6
  64.2 1.7 %copy-done.6 = bf16[40,2,128,128]{3,2,1,0:T(8,128)(2,1)S(1)} copy-done((bf16[40,2,128,128]{3,2,1,0:T(8,128)(2,1)S(1)}, bf16[40,2,128,128]{3,2,1,0:T(8,128)(2,1)}, u32[]{:S(2)}) %copy-start.6) | copy-done | bytes 2621464
  66.0 13.3 %gradient.1 = f32[80,128,128]{2,1,0:T(8,128)} custom-call(s32[2]{0:T(128)S(1)} %copy-done.21, bf16[80,128,128]{2,1,0:T(8,128)(2,1)S(1)} %bitcast.11, bf16[80,128,128]{2,1,0:T(8,128)(2,1)S(1)} %bitcast.9, bf16[80,8,128]{2,1,0:T(8,128)(2,1)S(1)} %collective-permute-done.2.above_ref, bf16[80,8,128]{2,1,0:T(8,128)(2,1)S(1)} %collective-permute-done.3.below_ref, ...), custom_call_target="tpu_custom_call" | custom-call | flops 100000000 | bytes 1000000 | tf_op jit(solution)/shard_map/gradient/pallas_call | solution.py:615
  (33 shorter events, 0.1 us)
Async XLA Ops:
  0.6 1.7 %copy-start = (bf16[40,2,128,128]{3,2,1,0:T(8,128)(2,1)S(1)}, bf16[40,2,128,128]{3,2,1,0:T(8,128)(2,1)}, u32[]{:S(2)}) copy-start(bf16[40,2,128,128]{3,2,1,0:T(8,128)(2,1)} %param.10) | copy-start | bytes 7864324
  2.4 7.0 %copy-start.2 = (f32[2,256,256]{2,1,0:T(8,128)S(1)}, f32[2,256,256]{2,1,0:T(8,128)}, u32[]{:S(2)}) copy-start(f32[2,256,256]{2,1,0:T(8,128)} %target_ref.5) | copy-start | bytes 1572868
  2.4 7.0 %copy-start.3 = (f32[2,256,256]{2,1,0:T(8,128)S(1)}, f32[2,256,256]{2,1,0:T(8,128)}, u32[]{:S(2)}) copy-start(f32[2,256,256]{2,1,0:T(8,128)} %weight_ref.5) | copy-start | bytes 1572868
  2.4 7.0 %copy-start.19 = (s32[256]{0:T(256)S(1)}, s32[256]{0:T(256)}, u32[]{:S(2)}) copy-start(s32[256]{0:T(256)} %lon_index_ref.1) | copy-start | bytes 3076
  2.4 7.0 %copy-start.20 = (f32[256]{0:T(256)S(1)}, f32[256]{0:T(256)}, u32[]{:S(2)}) copy-start(f32[256]{0:T(256)} %lon_share_ref.1) | copy-start | bytes 3076
  2.4 15.0 %copy-start.17 = (s32[256]{0:T(256)S(1)}, s32[256]{0:T(256)}, u32[]{:S(2)}) copy-start(s32[256]{0:T(256)} %lat_index_ref.1) | copy-start | bytes 3076
  2.4 15.0 %copy-start.18 = (f32[256]{0:T(256)S(1)}, f32[256]{0:T(256)}, u32[]{:S(2)}) copy-start(f32[256]{0:T(256)} %lat_share_ref.1) | copy-start | bytes 3076
  2.4 15.8 %copy-start.1 = (bf16[40,2,128,128]{3,2,1,0:T(8,128)(2,1)S(1)}, bf16[40,2,128,128]{3,2,1,0:T(8,128)(2,1)}, u32[]{:S(2)}) copy-start(bf16[40,2,128,128]{3,2,1,0:T(8,128)(2,1)} %param.10) | copy-start | bytes 7864324
  2.5 15.7 %collective-permute-start.2 = (bf16[80,8,128]{2,1,0:T(8,128)(2,1)S(1)}, bf16[80,8,128]{2,1,0:T(8,128)(2,1)S(1)}, u32[]{:S(2)}, u32[]{:S(2)}) collective-permute-start(bf16[80,8,128]{2,1,0:T(8,128)(2,1)S(1)} %get-tuple-element.29), channel_id=1, source_target_pairs={{0,2},{2,4},{4,6},{1,3},{3,5},{5,7},{8,10},{10,12},{12,14},{9,11},... | collective-permute-start | bytes 491528 | tf_op jit(solution)/shard_map/ppermute | solution.py:453
  7.7 15.3 %copy-start.5 = (bf16[40,2,128,128]{3,2,1,0:T(8,128)(2,1)S(1)}, bf16[40,2,128,128]{3,2,1,0:T(8,128)(2,1)}, u32[]{:S(2)}) copy-start(bf16[40,2,128,128]{3,2,1,0:T(8,128)(2,1)} %param.9) | copy-start | bytes 7864324
  7.8 15.3 %copy-start.21 = (s32[2]{0:T(128)S(1)}, s32[2]{0:T(128)}, u32[]{:S(2)}) copy-start(s32[2]{0:T(128)} %width_ref.3) | copy-start | bytes 28
  7.8 10.4 %collective-permute-start.3 = (bf16[80,8,128]{2,1,0:T(8,128)(2,1)S(1)}, bf16[80,8,128]{2,1,0:T(8,128)(2,1)S(1)}, u32[]{:S(2)}, u32[]{:S(2)}) collective-permute-start(bf16[80,8,128]{2,1,0:T(8,128)(2,1)S(1)} %get-tuple-element.30), channel_id=1, source_target_pairs={{2,0},{4,2},{6,4},{3,1},{5,3},{7,5},{10,8},{12,10},{14,12},{11,9},... | collective-permute-start | bytes 491528 | tf_op jit(solution)/shard_map/ppermute | solution.py:453
  9.7 6.7 %collective-permute-start = (f32[104,256]{1,0:T(8,128)S(1)}, f32[104,256]{1,0:T(8,128)S(1)}, u32[]{:S(2)}, u32[]{:S(2)}) collective-permute-start(f32[104,256]{1,0:T(8,128)S(1)} %get-tuple-element.23), channel_id=1, source_target_pairs={{0,8},{8,16},{16,24},{24,0},{1,9},{9,17},{17,25},{25,1},{2,10},{10... | collective-permute-start | bytes 319496 | tf_op jit(solution)/shard_map/ppermute | solution.py:453
  11.2 6.2 %collective-permute-start.1 = (f32[104,256]{1,0:T(8,128)S(1)}, f32[104,256]{1,0:T(8,128)S(1)}, u32[]{:S(2)}, u32[]{:S(2)}) collective-permute-start(f32[104,256]{1,0:T(8,128)S(1)} %get-tuple-element.24), channel_id=1, source_target_pairs={{8,0},{16,8},{24,16},{0,24},{9,1},{17,9},{25,17},{1,25},{10,2},{18... | collective-permute-start | bytes 319496 | tf_op jit(solution)/shard_map/ppermute | solution.py:453
  16.3 6.7 %copy-start.11 = (f32[104,256]{1,0:T(8,128)}, f32[104,256]{1,0:T(8,128)S(1)}, u32[]{:S(2)}) copy-start(f32[104,256]{1,0:T(8,128)S(1)} %collective-permute-done.west_ref) | copy-start | bytes 319492
  17.4 5.6 %copy-start.13 = (f32[104,256]{1,0:T(8,128)}, f32[104,256]{1,0:T(8,128)S(1)}, u32[]{:S(2)}) copy-start(f32[104,256]{1,0:T(8,128)S(1)} %collective-permute-done.1.east_ref) | copy-start | bytes 319492
  20.0 9.7 %collective-permute-start.4 = (bf16[5,144,128]{2,1,0:T(8,128)(2,1)S(1)}, bf16[5,144,128]{2,1,0:T(8,128)(2,1)S(1)}, u32[]{:S(2)}, u32[]{:S(2)}) collective-permute-start(bf16[5,144,128]{2,1,0:T(8,128)(2,1)S(1)} %get-tuple-element.31), channel_id=1, source_target_pairs={{0,8},{8,16},{16,24},{24,0},{1,9},{9,17},{17,25},{25,1},{2,10},{10... | collective-permute-start | bytes 552968 | tf_op jit(solution)/shard_map/ppermute | solution.py:453
  21.6 8.1 %collective-permute-start.5 = (bf16[5,144,128]{2,1,0:T(8,128)(2,1)S(1)}, bf16[5,144,128]{2,1,0:T(8,128)(2,1)S(1)}, u32[]{:S(2)}, u32[]{:S(2)}) collective-permute-start(bf16[5,144,128]{2,1,0:T(8,128)(2,1)S(1)} %get-tuple-element.32), channel_id=1, source_target_pairs={{8,0},{16,8},{24,16},{0,24},{9,1},{17,9},{25,17},{1,25},{10,2},{18... | collective-permute-start | bytes 552968 | tf_op jit(solution)/shard_map/ppermute | solution.py:453
  29.7 7.4 %copy-start.7 = (bf16[5,144,128]{2,1,0:T(8,128)(2,1)}, bf16[5,144,128]{2,1,0:T(8,128)(2,1)S(1)}, u32[]{:S(2)}) copy-start(bf16[5,144,128]{2,1,0:T(8,128)(2,1)S(1)} %collective-permute-done.4.west_ref) | copy-start | bytes 552964
  29.7 8.1 %copy-start.9 = (bf16[5,144,128]{2,1,0:T(8,128)(2,1)}, bf16[5,144,128]{2,1,0:T(8,128)(2,1)S(1)}, u32[]{:S(2)}) copy-start(bf16[5,144,128]{2,1,0:T(8,128)(2,1)S(1)} %collective-permute-done.5.east_ref) | copy-start | bytes 552964
  30.1 6.3 %collective-permute-start.6 = (f32[2,144,256]{2,1,0:T(8,128)S(1)}, f32[2,144,256]{2,1,0:T(8,128)S(1)}, u32[]{:S(2)}, u32[]{:S(2)}) collective-permute-start(f32[2,144,256]{2,1,0:T(8,128)S(1)} %frame.1.mine_ref), channel_id=1, source_target_pairs={{0,1},{1,0},{2,3},{3,2},{4,5},{5,4},{6,7},{7,6},{8,9},{9,8},{10,11... | collective-permute-start | bytes 884744 | tf_op jit(solution)/shard_map/ppermute | solution.py:574
  30.2 23.7 %collective-permute-start.11 = (f32[200,256]{1,0:T(8,128)}, f32[200,256]{1,0:T(8,128)}, u32[]{:S(2)}, u32[]{:S(2)}) collective-permute-start(f32[200,256]{1,0:T(8,128)} %get-tuple-element.39), channel_id=1, source_target_pairs={{0,2},{2,4},{4,6},{1,3},{3,5},{5,7},{8,10},{10,12},{12,14},{9,11},... | collective-permute-start | bytes 614408 | tf_op jit(solution)/shard_map/ppermute | solution.py:453
  35.2 18.7 %collective-permute-start.12 = (f32[200,256]{1,0:T(8,128)}, f32[200,256]{1,0:T(8,128)}, u32[]{:S(2)}, u32[]{:S(2)}) collective-permute-start(f32[200,256]{1,0:T(8,128)} %get-tuple-element.40), channel_id=1, source_target_pairs={{2,0},{4,2},{6,4},{3,1},{5,3},{7,5},{10,8},{12,10},{14,12},{11,9},... | collective-permute-start | bytes 614408 | tf_op jit(solution)/shard_map/ppermute | solution.py:453
  37.1 0.7 copy-start.15
  37.9 6.6 %collective-permute-start.7 = (f32[2,24,256]{2,1,0:T(8,128)}, f32[2,24,256]{2,1,0:T(8,128)S(1)}, u32[]{:S(2)}, u32[]{:S(2)}) collective-permute-start(f32[2,24,256]{2,1,0:T(8,128)} %get-tuple-element.34), channel_id=1, source_target_pairs={{0,2},{2,4},{4,6},{1,3},{3,5},{5,7},{8,10},{10,12},{12,14},{9,11},... | collective-permute-start | bytes 147464 | tf_op jit(solution)/shard_map/ppermute | solution.py:453
  42.4 6.3 %collective-permute-start.8 = (f32[2,24,256]{2,1,0:T(8,128)}, f32[2,24,256]{2,1,0:T(8,128)}, u32[]{:S(2)}, u32[]{:S(2)}) collective-permute-start(f32[2,24,256]{2,1,0:T(8,128)} %get-tuple-element.35), channel_id=1, source_target_pairs={{2,0},{4,2},{6,4},{3,1},{5,3},{7,5},{10,8},{12,10},{14,12},{11,9},... | collective-permute-start | bytes 147464 | tf_op jit(solution)/shard_map/ppermute | solution.py:453
  43.7 20.5 %copy-start.8 = (bf16[5,144,128]{2,1,0:T(8,128)(2,1)S(1)}, bf16[5,144,128]{2,1,0:T(8,128)(2,1)}, u32[]{:S(2)}) copy-start(bf16[5,144,128]{2,1,0:T(8,128)(2,1)} %copy-done.7) | copy-start | bytes 552964
  43.7 20.5 %copy-start.10 = (bf16[5,144,128]{2,1,0:T(8,128)(2,1)S(1)}, bf16[5,144,128]{2,1,0:T(8,128)(2,1)}, u32[]{:S(2)}) copy-start(bf16[5,144,128]{2,1,0:T(8,128)(2,1)} %copy-done.9) | copy-start | bytes 552964
  48.7 1.0 %copy-start.16 = (f32[2,144,256]{2,1,0:T(8,128)S(1)}, f32[2,144,256]{2,1,0:T(8,128)}, u32[]{:S(2)}) copy-start(f32[2,144,256]{2,1,0:T(8,128)} %copy-done.15) | copy-start | bytes 884740
  50.9 5.0 %collective-permute-start.9 = (f32[48,256]{1,0:T(8,128)S(1)}, f32[48,256]{1,0:T(8,128)S(1)}, u32[]{:S(2)}, u32[]{:S(2)}) collective-permute-start(f32[48,256]{1,0:T(8,128)S(1)} %get-tuple-element.37), channel_id=1, source_target_pairs={{0,8},{8,16},{16,24},{24,0},{1,9},{9,17},{17,25},{25,1},{2,10},{10... | collective-permute-start | bytes 147464 | tf_op jit(solution)/shard_map/ppermute | solution.py:453
  51.5 4.4 %collective-permute-start.10 = (f32[48,256]{1,0:T(8,128)S(1)}, f32[48,256]{1,0:T(8,128)S(1)}, u32[]{:S(2)}, u32[]{:S(2)}) collective-permute-start(f32[48,256]{1,0:T(8,128)S(1)} %get-tuple-element.38), channel_id=1, source_target_pairs={{8,0},{16,8},{24,16},{0,24},{9,1},{17,9},{25,17},{1,25},{10,2},{18... | collective-permute-start | bytes 147464 | tf_op jit(solution)/shard_map/ppermute | solution.py:453
  55.9 1.0 %copy-start.4 = (f32[2,256,256]{2,1,0:T(8,128)S(1)}, f32[2,256,256]{2,1,0:T(8,128)}, u32[]{:S(2)}) copy-start(f32[2,256,256]{2,1,0:T(8,128)} %weight_ref.5) | copy-start | bytes 1572868
  56.9 0.9 %copy-start.12 = (f32[104,256]{1,0:T(8,128)S(1)}, f32[104,256]{1,0:T(8,128)}, u32[]{:S(2)}) copy-start(f32[104,256]{1,0:T(8,128)} %copy-done.11) | copy-start | bytes 319492
  57.8 0.9 %copy-start.14 = (f32[104,256]{1,0:T(8,128)S(1)}, f32[104,256]{1,0:T(8,128)}, u32[]{:S(2)}) copy-start(f32[104,256]{1,0:T(8,128)} %copy-done.13) | copy-start | bytes 319492
  64.2 1.7 %copy-start.6 = (bf16[40,2,128,128]{3,2,1,0:T(8,128)(2,1)S(1)}, bf16[40,2,128,128]{3,2,1,0:T(8,128)(2,1)}, u32[]{:S(2)}) copy-start(bf16[40,2,128,128]{3,2,1,0:T(8,128)(2,1)} %param.9) | copy-start | bytes 7864324

commit v3 on v2

--- a/solution.py
+++ b/solution.py
@@ -162,9 +162,16 @@
     return near + jnp.where(cell == index + 1, weight, 0.0)
 
 
-def rows_kernel(last_ref, first_ref, next_ref, previous_ref):
-    next_ref[...] = last_ref[...]
-    previous_ref[...] = first_ref[...]
+def rows_kernel(perts_ref, next_ref, previous_ref, sems):
+    height = perts_ref.shape[1]
+    copies = [
+        pltpu.make_async_copy(perts_ref.at[:, height - HB :], next_ref, sems.at[0]),
+        pltpu.make_async_copy(perts_ref.at[:, :HB], previous_ref, sems.at[1]),
+    ]
+    for copy in copies:
+        copy.start()
+    for copy in copies:
+        copy.wait()
 
 
 def table(index, weight):
@@ -188,7 +195,8 @@
 
 
 def fine_rows_kernel(
-    target_ref, weight_ref, index_ref, share_ref, west_ref, east_ref, next_ref, previous_ref, token_ref
+    target_ref, weight_ref, index_ref, share_ref, west_ref, east_ref, order_ref, next_ref, previous_ref,
+    token_ref,
 ):
     rows = target_ref.shape[1]
     for a, ref in enumerate((target_ref, weight_ref)):
@@ -206,7 +214,9 @@
     token_ref[...] = lat[:, :LANES]
 
 
-def frame_kernel(sum_ref, rows_ref, cols_ref, above_ref, below_ref, west_ref, east_ref, out_ref):
+def frame_kernel(
+    sum_ref, rows_ref, cols_ref, above_ref, below_ref, west_ref, east_ref, order_ref, after_ref, out_ref
+):
     height, width = sum_ref.shape[1], sum_ref.shape[2]
     ext = height + 2 * HB
     groups = west_ref.shape[0]
@@ -263,7 +273,6 @@
 
 def fine_kernel(
     lon_total,
-    start_ref,
     stack_ref,
     strip_west_ref,
     strip_east_ref,
@@ -307,9 +316,9 @@
     lat = jnp.concatenate([table(lat_index_ref[...], lat_share_ref[...]), lat_side], 1)
     lon_side = side(west_ref[4 * SKIRT :, :LANES], east_ref[4 * SKIRT :, :LANES])
     lon = jnp.concatenate([table(lon_index_ref[...], lon_share_ref[...]), lon_side], 1)
-    lat_cell = lat[0:1].astype(jnp.int32) - start_ref[0]
+    lat_cell = lat[0:1].astype(jnp.int32) - lax.axis_index("gy") * height
     lat_share = lat[1:2]
-    lon_cell = lon[0:1].astype(jnp.int32) - start_ref[1]
+    lon_cell = lon[0:1].astype(jnp.int32) - lax.axis_index("gx") * width
     lon_cell = jnp.where(lon_cell < -(lon_total // 2), lon_cell + lon_total, lon_cell)
     wrap = (lon_cell >= lon_total // 2) & (lon_cell < lon_total)
     lon_cell = jnp.where(wrap, lon_cell - lon_total, lon_cell)
@@ -408,36 +417,48 @@
             lat_ref[level, :, 2 * ext :] = high
 
     half = iota((ext, LANES), 1) < LANES // 2
-    west = west_ref[0].astype(F32)
-    east = east_ref[0].astype(F32)
-
-    def stack(value, start, size):
+
+    def stacked(value):
         high, low = split(value)
-        stack_ref[:ext, start : start + size] = high
-        stack_ref[ext : 2 * ext, start : start + size] = high
-        stack_ref[2 * ext :, start : start + size] = low
+        return jnp.concatenate([high, high, low], 0)
 
     for level in range(2):
+        west = west_ref[0].astype(F32)
+        east = east_ref[0].astype(F32)
         cell = jnp.where(half, west, east) if level == 0 else jnp.where(half, east, west)
-        stack(cell * edge_ref[level], MEMBERS * width, LANES)
-        for t in range(MEMBERS):
-            k = 2 * t + level
-            field = jnp.concatenate(
-                [perts_ref[k].astype(F32), above_ref[k].astype(F32), below_ref[k].astype(F32)], 0
-            )
-            stack(field * own_ref[level], t * width, width)
-        edge_high, edge_low = split(dot(lat_ref[level], stack_ref[:, MEMBERS * width :]))
-        for pair in range(MEMBERS // 2):
-            base = 2 * pair * width
-            wide = dot(lat_ref[level], stack_ref[:, base : base + 2 * width])
-            for side in range(2):
-                t = 2 * pair + side
-                k = 2 * t + level
-                high, low = split(wide[:, side * width : (side + 1) * width])
-                main = dot(jnp.concatenate([high, edge_high], 1), lon_ref[level, t])
-                rest = dot(jnp.concatenate([low, edge_low], 1), lon_ref[level, t, :, :width])
-                total = main[:, :width] + main[:, width:] + rest
+        side = dot(lat_ref[level], stacked(cell * edge_ref[level]))
+        side = jnp.concatenate(split(side), 0)
+        stack_ref[...] = side
+        own = own_ref[level]
+
+        def pair(p, carry):
+            columns = []
+            for number in range(2):
+                k = 4 * p + 2 * number + level
+                field = jnp.concatenate(
+                    [perts_ref[k].astype(F32), above_ref[k].astype(F32), below_ref[k].astype(F32)], 0
+                )
+                columns.append(stacked(field * own_ref[level]))
+            wide = dot(lat_ref[level], jnp.concatenate(columns, 1))
+            for number in range(2):
+                t = 2 * p + number
+                k = 4 * p + 2 * number + level
+                parts = jnp.concatenate(split(wide[:, number * width : (number + 1) * width]), 0)
+                both = dot(jnp.concatenate([parts, stack_ref[...]], 1), lon_ref[level, t])
+                total = both[:height, :width] + both[:height, width:] + both[height:, :width]
                 out_ref[k] = alpha_ref[k].astype(F32) + total
+            return carry
+
+        lax.fori_loop(0, MEMBERS // 2, pair, 0, unroll=4)
+
+
+def GRAD_SCRATCH(height, width):
+    ext = height + 2 * HB
+    return [
+        pltpu.VMEM((2, MEMBERS, width + LANES, 2 * width), BF16),
+        pltpu.VMEM((2, height, 3 * ext), BF16),
+        pltpu.VMEM((2 * height, LANES), BF16),
+    ]
 
 
 def ring(axis, periodic):
@@ -485,18 +506,18 @@
     perts = member_perts.reshape(fields, height, width)
     smem = pl.BlockSpec(memory_space=pltpu.SMEM)
     anywhere = pl.BlockSpec(memory_space=pl.ANY)
-    limit = min(60, 16 * (width // LANES)) * 1024 * 1024
+    scale = width // LANES
     lanes = rounded(width + 2 * HB, LANES)
     tall = rounded(ext + 2 * STRIP, LANES)
 
-    def params(*semantics):
-        return pltpu.CompilerParams(dimension_semantics=semantics, vmem_limit_bytes=limit)
-
-    def call(kernel, out_shape, name, flops=10**8, **more):
+    def call(kernel, out_shape, name, flops=10**8, grant=4, **more):
+        semantics = ("arbitrary",) if "grid" in more else ()
         return pl.pallas_call(
             kernel,
             out_shape=out_shape,
-            compiler_params=params(*(("arbitrary",) if "grid" in more else ())),
+            compiler_params=pltpu.CompilerParams(
+                dimension_semantics=semantics, vmem_limit_bytes=min(60, grant * scale) * 1024 * 1024
+            ),
             name=name,
             cost_estimate=pl.CostEstimate(flops=flops, bytes_accessed=10**6, transcendentals=0),
             **more,
@@ -507,13 +528,10 @@
         rows_kernel,
         [edge, edge],
         "rows",
-        in_specs=[
-            pl.BlockSpec((fields, HB, width), lambda s: (0, height // HB - 1, 0)),
-            pl.BlockSpec((fields, HB, width), lambda s: (0, 0, 0)),
-        ],
-        grid=(1,),
-        out_specs=[vmem(fields, HB, width)] * 2,
-    )(perts, perts)
+        in_specs=[pl.BlockSpec(memory_space=pltpu.HBM)],
+        out_specs=[pl.BlockSpec(memory_space=pltpu.VMEM)] * 2,
+        scratch_shapes=[pltpu.SemaphoreType.DMA((2,))],
+    )(perts)
     above, below = exchange(to_next, to_previous, "gy", False)
 
     side = shaped((4 * SKIRT + 8, fine_h))
@@ -527,6 +545,7 @@
         pack_kernel,
         [packed, packed],
         "pack",
+        grant=8,
         grid=(groups,),
         in_specs=[grouped(GROUP, height, width)] + [grouped(GROUP, HB, width)] * 2,
         out_specs=[grouped(1, ext, LANES)] * 2,
@@ -534,9 +553,13 @@
     west, east = exchange(to_next, to_previous, "gx", True)
 
     strip = shaped((8 * SKIRT + 8, fine_w))
+    whole = pl.BlockSpec(memory_space=pltpu.VMEM)
     to_next, to_previous, token = call(
-        fine_rows_kernel, [strip, strip, shaped((8, LANES))], "fine_rows"
-    )(innovation, obs_weight, lat_index, lat_weight, fine_west, fine_east)
+        fine_rows_kernel,
+        [strip, strip, shaped((8, LANES))],
+        "fine_rows",
+        in_specs=[whole] * 6 + [anywhere],
+    )(innovation, obs_weight, lat_index, lat_weight, fine_west, fine_east, to_next)
     fine_above, fine_below = exchange(to_next, to_previous, "gy", False)
 
     partial, edge_rows, edge_cols = call(
@@ -548,6 +571,7 @@
         ],
         "local",
         flops=10**10,
+        grant=16,
         grid=(groups,),
         in_specs=[
             smem,
@@ -567,9 +591,12 @@
         ],
     )(band_widths, alpha, perts, token)
 
-    framed = call(frame_kernel, shaped((2, ext, width + LANES)), "frame")(
-        partial, edge_rows, edge_cols, above, below, west, east
-    )
+    framed = call(
+        frame_kernel,
+        shaped((2, ext, width + LANES)),
+        "frame",
+        in_specs=[whole] * 7 + [anywhere] * 2,
+    )(partial, edge_rows, edge_cols, above, below, west, east, fine_above, fine_below)
     count = lax.axis_size("ma")
     other = lax.ppermute(framed, "ma", [(i, (i + 1) % count) for i in range(count)])
     strip = shaped((2, STRIP, lanes))
@@ -583,20 +610,19 @@
     )(framed, north, south)
     strip_west, strip_east = exchange(to_next, to_previous, "gx", True)
 
-    starts = jnp.stack([lax.axis_index("gy") * height, lax.axis_index("gx") * width])
     lon_total = width * lax.axis_size("gx")
     everything = [pl.BlockSpec(memory_space=pltpu.VMEM)] * 13
     increment, own, edge = call(
         functools.partial(fine_kernel, lon_total),
         [shaped((2, fine_h, fine_w)), shaped((2, ext, width)), shaped((2, ext, LANES))],
         "fine",
-        in_specs=[smem] + everything,
+        grant=16,
+        in_specs=everything,
         scratch_shapes=[
             pltpu.VMEM((fine_h + LANES, lanes + LANES), F32),
             pltpu.VMEM((fine_h + LANES, fine_w), F32),
         ],
     )(
-        starts,
         stack,
         strip_west,
         strip_east,
@@ -616,6 +642,7 @@
         gradient_kernel,
         shaped((fields, height, width)),
         "gradient",
+        grant=16,
         grid=(groups,),
         in_specs=[
             smem,
@@ -629,11 +656,7 @@
             vmem(2, ext, LANES),
         ],
         out_specs=grouped(GROUP, height, width),
-        scratch_shapes=[
-            pltpu.VMEM((2, MEMBERS, width + LANES, 2 * width), BF16),
-            pltpu.VMEM((2, height, 3 * ext), BF16),
-            pltpu.VMEM((3 * ext, MEMBERS * width + LANES), BF16),
-        ],
+        scratch_shapes=GRAD_SCRATCH(height, width),
     )(band_widths, alpha, perts, above, below, west, east, own, edge)
     return increment, gradient.reshape(alpha_fields.shape)
 

time: 79.7 us -> 68.7 us (0.86)
  local copies, waits for them, and re-layouts: 8.04 us -> 3.86 us
  Pallas kernels: 30.6 us -> 27.3 us
  waiting for transfers between devices: 11.7 us -> 9.4 us
  starting transfers between devices: 27.8 us -> 26.8 us
    unnamed x44 -> x24, local copies, waits for them, and re-layouts: 8.04 us -> 3.86 us
    ppermute x6, waiting for transfers between devices: 6.38 us -> 2.51 us  [exchange(): lax.ppermute(to_next, axis, forward)]
    ppermute x1, waiting for transfers between devices: 0.01 us -> 1.57 us  [body(): lax.ppermute(framed, 'ma', [(i, (i + 1) % count) for i in range(count)])]
    ppermute x6, starting transfers between devices: 18.5 us -> 16.9 us  [exchange(): lax.ppermute(to_next, axis, forward)]
    pallas_call x1, Pallas kernels: 5.46 us -> 4.43 us  [body(): call(functools.partial(fine_kernel, lon_total), [shaped((2, fine_h, fine_...]
    pallas_call x5, Pallas kernels: 16.3 us -> 15.4 us  [the longest x1 13.1 us: body(): call(gradient_kernel, shaped((fields, height, width)), 'gradient', grant=...]
    pallas_call x1, Pallas kernels: 1.2 us -> 0.4 us  [body(): call(functools.partial(strips_kernel, width), [shaped((2, tall, lanes)),...]
  transfers between devices with their start and end apart: 13 -> 13, of which waited for: 5 -> 6; matrix products, arithmetic and copies ran while one was open for 0% -> 0% of each run, Pallas kernels for 12% -> 13%
where the time goes in v3:
time: 68.7 us; the launch traced here: 68.3 us
  Pallas kernels  27.3 us (40%)
  starting transfers between devices  26.8 us (39%)
  waiting for transfers between devices  9.4 us (14%)
  local copies, waits for them, and re-layouts  3.86 us (6%)
  between operations  0.88 us (1%)
    ppermute x6, starting transfers between devices, exchange(): lax.ppermute(to_next, axis, forward)  16.9 us
    pallas_call x1, Pallas kernels, body(): call(gradient_kernel, shaped((fields, height, width)), 'gradient', grant=...  13.1 us
    ppermute x6, starting transfers between devices, exchange(): lax.ppermute(to_previous, axis, backward)  9.86 us
    pallas_call x1, Pallas kernels, body(): call(local_kernel, [shaped((2, height, width)), shaped((fields, 2 * HB, w...  6.71 us
    ppermute x6, waiting for transfers between devices, exchange(): lax.ppermute(to_previous, axis, backward)  5.33 us
    pallas_call x1, Pallas kernels, body(): call(functools.partial(fine_kernel, lon_total), [shaped((2, fine_h, fine_...  4.43 us
    unnamed x24, local copies, waits for them, and re-layouts  3.86 us
    ppermute x6, waiting for transfers between devices, exchange(): lax.ppermute(to_next, axis, forward)  2.51 us
  transfers between devices with their start and end apart: 13, of which 6 were waited for; matrix products, arithmetic and copies ran while one was open for 0% of the time, Pallas kernels for 13%

profile of v3, /device:TPU:0, one launch (start us, length us, event | category | flops | bytes accessed | tf_op | source)
XLA Modules:
  0.0 68.3 jit_solution(8402613298348677669)
XLA Ops:
  0.6 0.0 copy-start.9
  0.6 0.0 copy-start
  0.7 1.7 %copy-done = bf16[40,2,128,128]{3,2,1,0:T(8,128)(2,1)S(1)} copy-done((bf16[40,2,128,128]{3,2,1,0:T(8,128)(2,1)S(1)}, bf16[40,2,128,128]{3,2,1,0:T(8,128)(2,1)}, u32[]{:S(2)}) %copy-start) | copy-done | bytes 2621464
  2.4 0.1 rows.1
  2.5 0.0 copy-start.7
  2.5 0.0 copy-start.8
  2.5 5.1 %collective-permute-start.2 = (bf16[80,8,128]{2,1,0:T(8,128)(2,1)S(1)}, bf16[80,8,128]{2,1,0:T(8,128)(2,1)S(1)}, u32[]{:S(2)}, u32[]{:S(2)}) collective-permute-start(bf16[80,8,128]{2,1,0:T(8,128)(2,1)S(1)} %get-tuple-element.25), channel_id=1, source_target_pairs={{0,2},{2,4},{4,6},{1,3},{3,5},{5,7},{8,10},{10,12},{12,14},{9,11},... | collective-permute-start | bytes 491528 | tf_op jit(solution)/shard_map/ppermute | solution.py:474
  7.6 1.3 %collective-permute-start.3 = (bf16[80,8,128]{2,1,0:T(8,128)(2,1)S(1)}, bf16[80,8,128]{2,1,0:T(8,128)(2,1)S(1)}, u32[]{:S(2)}, u32[]{:S(2)}) collective-permute-start(bf16[80,8,128]{2,1,0:T(8,128)(2,1)S(1)} %get-tuple-element.26), channel_id=1, source_target_pairs={{2,0},{4,2},{6,4},{3,1},{5,3},{7,5},{10,8},{12,10},{14,12},{11,9},... | collective-permute-start | bytes 491528 | tf_op jit(solution)/shard_map/ppermute | solution.py:474
  8.9 0.0 copy-done.9
  8.9 0.0 copy-done.10
  9.0 0.0 copy-start.2
  9.0 1.0 %copy-done.2 = f32[2,256,256]{2,1,0:T(8,128)S(1)} copy-done((f32[2,256,256]{2,1,0:T(8,128)S(1)}, f32[2,256,256]{2,1,0:T(8,128)}, u32[]{:S(2)}) %copy-start.2) | copy-done | bytes 524312
  10.0 1.0 %copy-done.4 = f32[2,256,256]{2,1,0:T(8,128)S(1)} copy-done((f32[2,256,256]{2,1,0:T(8,128)S(1)}, f32[2,256,256]{2,1,0:T(8,128)}, u32[]{:S(2)}) %copy-start.4) | copy-done | bytes 524312
  11.1 0.3 fine_cols.1
  11.4 1.5 %collective-permute-start = (f32[104,256]{1,0:T(8,128)S(1)}, f32[104,256]{1,0:T(8,128)S(1)}, u32[]{:S(2)}, u32[]{:S(2)}) collective-permute-start(f32[104,256]{1,0:T(8,128)S(1)} %get-tuple-element.23), channel_id=1, source_target_pairs={{0,8},{8,16},{16,24},{24,0},{1,9},{9,17},{17,25},{25,1},{2,10},{10... | collective-permute-start | bytes 319496 | tf_op jit(solution)/shard_map/ppermute | solution.py:474
  12.9 1.4 %collective-permute-start.1 = (f32[104,256]{1,0:T(8,128)S(1)}, f32[104,256]{1,0:T(8,128)S(1)}, u32[]{:S(2)}, u32[]{:S(2)}) collective-permute-start(f32[104,256]{1,0:T(8,128)S(1)} %get-tuple-element.24), channel_id=1, source_target_pairs={{8,0},{16,8},{24,16},{0,24},{9,1},{17,9},{25,17},{1,25},{10,2},{18... | collective-permute-start | bytes 319496 | tf_op jit(solution)/shard_map/ppermute | solution.py:474
  14.3 0.0 collective-permute-done.2.above_ref
  14.3 0.8 %collective-permute-done.3.below_ref = bf16[80,8,128]{2,1,0:T(8,128)(2,1)S(1)} collective-permute-done((bf16[80,8,128]{2,1,0:T(8,128)(2,1)S(1)}, bf16[80,8,128]{2,1,0:T(8,128)(2,1)S(1)}, u32[]{:S(2)}, u32[]{:S(2)}) %collective-permute-start.3) | collective-permute-done | bytes 163872 | tf_op jit(solution)/shard_map/ppermute | solution.py:474
  15.2 0.0 copy-done.1
  15.2 1.8 %pack.1 = (bf16[5,144,128]{2,1,0:T(8,128)(2,1)S(1)}, bf16[5,144,128]{2,1,0:T(8,128)(2,1)S(1)}) custom-call(bf16[80,128,128]{2,1,0:T(8,128)(2,1)S(1)} %bitcast.4, bf16[80,8,128]{2,1,0:T(8,128)(2,1)S(1)} %collective-permute-done.2.above_ref, bf16[80,8,128]{2,1,0:T(8,128)(2,1)S(1)} %collective-permute-done.3.below_ref), custom_call_target="tpu_custom_call" | custom-call | flops 100000000 | bytes 1000000 | tf_op jit(solution)/shard_map/pack/pallas_call | solution.py:544
  17.0 2.5 %collective-permute-start.5 = (bf16[5,144,128]{2,1,0:T(8,128)(2,1)S(1)}, bf16[5,144,128]{2,1,0:T(8,128)(2,1)S(1)}, u32[]{:S(2)}, u32[]{:S(2)}) collective-permute-start(bf16[5,144,128]{2,1,0:T(8,128)(2,1)S(1)} %get-tuple-element.32), channel_id=1, source_target_pairs={{8,0},{16,8},{24,16},{0,24},{9,1},{17,9},{25,17},{1,25},{10,2},{18... | collective-permute-start | bytes 552968 | tf_op jit(solution)/shard_map/ppermute | solution.py:474
  19.5 0.0 collective-permute-start.4
  19.6 0.0 collective-permute-done.west_ref
  19.6 0.2 collective-permute-done.1.east_ref
  19.8 0.0 copy-done.7
  19.8 0.0 copy-done.8
  19.8 0.0 copy-done.5
  19.8 4.8 %collective-permute-start.6 = (f32[200,256]{1,0:T(8,128)S(1)}, f32[200,256]{1,0:T(8,128)S(1)}, u32[]{:S(2)}, u32[]{:S(2)}) collective-permute-start(f32[200,256]{1,0:T(8,128)S(1)} %get-tuple-element.33), channel_id=1, source_target_pairs={{0,2},{2,4},{4,6},{1,3},{3,5},{5,7},{8,10},{10,12},{12,14},{9,11},... | collective-permute-start | bytes 614408 | tf_op jit(solution)/shard_map/ppermute | solution.py:474
  24.7 1.3 %collective-permute-start.7 = (f32[200,256]{1,0:T(8,128)S(1)}, f32[200,256]{1,0:T(8,128)S(1)}, u32[]{:S(2)}, u32[]{:S(2)}) collective-permute-start(f32[200,256]{1,0:T(8,128)S(1)} %get-tuple-element.34), channel_id=1, source_target_pairs={{2,0},{4,2},{6,4},{3,1},{5,3},{7,5},{10,8},{12,10},{14,12},{11,9},... | collective-permute-start | bytes 614408 | tf_op jit(solution)/shard_map/ppermute | solution.py:474
  26.0 6.7 %local.1 = (f32[2,128,128]{2,1,0:T(8,128)S(1)}, f32[80,16,128]{2,1,0:T(8,128)S(1)}, f32[5,2,144,128]{3,2,1,0:T(8,128)S(1)}) custom-call(s32[2]{0:T(128)S(1)} %copy-done.11, bf16[80,128,128]{2,1,0:T(8,128)(2,1)S(1)} %bitcast.7, bf16[80,128,128]{2,1,0:T(8,128)(2,1)S(1)} %bitcast.5, f32[8,128]{1,0:T(8,128)S(1)} %get-tuple-element.28.token_ref), custom_call_target="tpu_custom_call" | custom-call | flops 10000000000 | bytes 1000000 | tf_op jit(solution)/shard_map/local/pallas_call | solution.py:565
  32.7 0.0 collective-permute-done.5.east_ref
  32.7 0.0 collective-permute-done.4.west_ref
  32.7 0.0 collective-permute-done.6.order_ref.above_ref
  32.7 0.0 collective-permute-done.7.after_ref.below_ref
  32.7 0.4 frame.1.mine_ref
  33.1 0.1 collective-permute-start.8
  33.2 1.6 %collective-permute-done.8.other_ref = f32[2,144,256]{2,1,0:T(8,128)S(1)} collective-permute-done((f32[2,144,256]{2,1,0:T(8,128)S(1)}, f32[2,144,256]{2,1,0:T(8,128)S(1)}, u32[]{:S(2)}, u32[]{:S(2)}) %collective-permute-start.8) | collective-permute-done | bytes 294944 | tf_op jit(solution)/shard_map/ppermute | solution.py:601
  34.8 4.6 %collective-permute-start.9 = (f32[2,24,256]{2,1,0:T(8,128)S(1)}, f32[2,24,256]{2,1,0:T(8,128)S(1)}, u32[]{:S(2)}, u32[]{:S(2)}) collective-permute-start(f32[2,24,256]{2,1,0:T(8,128)S(1)} %get-tuple-element.36), channel_id=1, source_target_pairs={{0,2},{2,4},{4,6},{1,3},{3,5},{5,7},{8,10},{10,12},{12,14},{9,11},... | collective-permute-start | bytes 147464 | tf_op jit(solution)/shard_map/ppermute | solution.py:474
  39.4 1.3 %collective-permute-start.10 = (f32[2,24,256]{2,1,0:T(8,128)S(1)}, f32[2,24,256]{2,1,0:T(8,128)S(1)}, u32[]{:S(2)}, u32[]{:S(2)}) collective-permute-start(f32[2,24,256]{2,1,0:T(8,128)S(1)} %get-tuple-element.37), channel_id=1, source_target_pairs={{2,0},{4,2},{6,4},{3,1},{5,3},{7,5},{10,8},{12,10},{14,12},{11,9},... | collective-permute-start | bytes 147464 | tf_op jit(solution)/shard_map/ppermute | solution.py:474
  40.7 0.4 collective-permute-done.9.above_ref
  41.1 4.3 %collective-permute-done.10.below_ref = f32[2,24,256]{2,1,0:T(8,128)S(1)} collective-permute-done((f32[2,24,256]{2,1,0:T(8,128)S(1)}, f32[2,24,256]{2,1,0:T(8,128)S(1)}, u32[]{:S(2)}, u32[]{:S(2)}) %collective-permute-start.10) | collective-permute-done | bytes 49184 | tf_op jit(solution)/shard_map/ppermute | solution.py:474
  45.4 0.4 strips.1
  45.8 0.9 %collective-permute-start.11 = (f32[48,256]{1,0:T(8,128)S(1)}, f32[48,256]{1,0:T(8,128)S(1)}, u32[]{:S(2)}, u32[]{:S(2)}) collective-permute-start(f32[48,256]{1,0:T(8,128)S(1)} %get-tuple-element.39), channel_id=1, source_target_pairs={{0,8},{8,16},{16,24},{24,0},{1,9},{9,17},{17,25},{25,1},{2,10},{10... | collective-permute-start | bytes 147464 | tf_op jit(solution)/shard_map/ppermute | solution.py:474
  46.7 2.0 %collective-permute-start.12 = (f32[48,256]{1,0:T(8,128)S(1)}, f32[48,256]{1,0:T(8,128)S(1)}, u32[]{:S(2)}, u32[]{:S(2)}) collective-permute-start(f32[48,256]{1,0:T(8,128)S(1)} %get-tuple-element.40), channel_id=1, source_target_pairs={{8,0},{16,8},{24,16},{0,24},{9,1},{17,9},{25,17},{1,25},{10,2},{18... | collective-permute-start | bytes 147464 | tf_op jit(solution)/shard_map/ppermute | solution.py:474
  48.7 2.1 %collective-permute-done.11.strip_west_ref = f32[48,256]{1,0:T(8,128)S(1)} collective-permute-done((f32[48,256]{1,0:T(8,128)S(1)}, f32[48,256]{1,0:T(8,128)S(1)}, u32[]{:S(2)}, u32[]{:S(2)}) %collective-permute-start.11) | collective-permute-done | bytes 49184 | tf_op jit(solution)/shard_map/ppermute | solution.py:474
  50.8 0.0 collective-permute-done.12.strip_east_ref
  50.8 4.4 %fine.1 = (f32[2,256,256]{2,1,0:T(8,128)}, f32[2,144,128]{2,1,0:T(8,128)S(1)}, f32[2,144,128]{2,1,0:T(8,128)S(1)}) custom-call(f32[2,256,256]{2,1,0:T(8,128)S(1)} %get-tuple-element.38.stack_ref, f32[48,256]{1,0:T(8,128)S(1)} %collective-permute-done.11.strip_west_ref, f32[48,256]{1,0:T(8,128)S(1)} %collective-permute-done.12.strip_east_ref, ...), custom_call_target="tpu_custom_call" | custom-call | flops 100000000 | bytes 1000000 | tf_op jit(solution)/shard_map/fine/pallas_call | solution.py:615
  55.2 13.1 %gradient.1 = f32[80,128,128]{2,1,0:T(8,128)} custom-call(s32[2]{0:T(128)S(1)} %copy-done.11, bf16[80,128,128]{2,1,0:T(8,128)(2,1)S(1)} %bitcast.8, bf16[80,128,128]{2,1,0:T(8,128)(2,1)S(1)} %bitcast.6, bf16[80,8,128]{2,1,0:T(8,128)(2,1)S(1)} %collective-permute-done.2.above_ref, bf16[80,8,128]{2,1,0:T(8,128)(2,1)S(1)} %collective-permute-done.3.below_ref, ...), custom_call_target="tpu_custom_call" | custom-call | flops 100000000 | bytes 1000000 | tf_op jit(solution)/shard_map/gradient/pallas_call | solution.py:641
  (12 shorter events, 0.1 us)
Async XLA Ops:
  0.6 8.3 %copy-start.9 = (s32[256]{0:T(256)S(1)}, s32[256]{0:T(256)}, u32[]{:S(2)}) copy-start(s32[256]{0:T(256)} %lon_index_ref.1) | copy-start | bytes 3076
  0.6 1.7 %copy-start = (bf16[40,2,128,128]{3,2,1,0:T(8,128)(2,1)S(1)}, bf16[40,2,128,128]{3,2,1,0:T(8,128)(2,1)}, u32[]{:S(2)}) copy-start(bf16[40,2,128,128]{3,2,1,0:T(8,128)(2,1)} %param.10) | copy-start | bytes 7864324
  2.4 6.6 %copy-start.10 = (f32[256]{0:T(256)S(1)}, f32[256]{0:T(256)}, u32[]{:S(2)}) copy-start(f32[256]{0:T(256)} %lon_share_ref.1) | copy-start | bytes 3076
  2.4 12.8 %copy-start.1 = (bf16[40,2,128,128]{3,2,1,0:T(8,128)(2,1)S(1)}, bf16[40,2,128,128]{3,2,1,0:T(8,128)(2,1)}, u32[]{:S(2)}) copy-start(bf16[40,2,128,128]{3,2,1,0:T(8,128)(2,1)} %param.10) | copy-start | bytes 7864324
  2.5 17.3 %copy-start.7 = (s32[256]{0:T(256)S(1)}, s32[256]{0:T(256)}, u32[]{:S(2)}) copy-start(s32[256]{0:T(256)} %lat_index_ref.1) | copy-start | bytes 3076
  2.5 17.3 %copy-start.8 = (f32[256]{0:T(256)S(1)}, f32[256]{0:T(256)}, u32[]{:S(2)}) copy-start(f32[256]{0:T(256)} %lat_share_ref.1) | copy-start | bytes 3076
  2.5 11.8 %collective-permute-start.2 = (bf16[80,8,128]{2,1,0:T(8,128)(2,1)S(1)}, bf16[80,8,128]{2,1,0:T(8,128)(2,1)S(1)}, u32[]{:S(2)}, u32[]{:S(2)}) collective-permute-start(bf16[80,8,128]{2,1,0:T(8,128)(2,1)S(1)} %get-tuple-element.25), channel_id=1, source_target_pairs={{0,2},{2,4},{4,6},{1,3},{3,5},{5,7},{8,10},{10,12},{12,14},{9,11},... | collective-permute-start | bytes 491528 | tf_op jit(solution)/shard_map/ppermute | solution.py:474
  7.6 7.6 %collective-permute-start.3 = (bf16[80,8,128]{2,1,0:T(8,128)(2,1)S(1)}, bf16[80,8,128]{2,1,0:T(8,128)(2,1)S(1)}, u32[]{:S(2)}, u32[]{:S(2)}) collective-permute-start(bf16[80,8,128]{2,1,0:T(8,128)(2,1)S(1)} %get-tuple-element.26), channel_id=1, source_target_pairs={{2,0},{4,2},{6,4},{3,1},{5,3},{7,5},{10,8},{12,10},{14,12},{11,9},... | collective-permute-start | bytes 491528 | tf_op jit(solution)/shard_map/ppermute | solution.py:474
  9.0 1.0 %copy-start.2 = (f32[2,256,256]{2,1,0:T(8,128)S(1)}, f32[2,256,256]{2,1,0:T(8,128)}, u32[]{:S(2)}) copy-start(f32[2,256,256]{2,1,0:T(8,128)} %target_ref.5) | copy-start | bytes 1572868
  10.0 1.0 %copy-start.4 = (f32[2,256,256]{2,1,0:T(8,128)S(1)}, f32[2,256,256]{2,1,0:T(8,128)}, u32[]{:S(2)}) copy-start(f32[2,256,256]{2,1,0:T(8,128)} %weight_ref.5) | copy-start | bytes 1572868
  11.0 8.7 %copy-start.3 = (f32[2,256,256]{2,1,0:T(8,128)S(1)}, f32[2,256,256]{2,1,0:T(8,128)}, u32[]{:S(2)}) copy-start(f32[2,256,256]{2,1,0:T(8,128)} %target_ref.5) | copy-start | bytes 1572868
  11.0 8.7 %copy-start.5 = (f32[2,256,256]{2,1,0:T(8,128)S(1)}, f32[2,256,256]{2,1,0:T(8,128)}, u32[]{:S(2)}) copy-start(f32[2,256,256]{2,1,0:T(8,128)} %weight_ref.5) | copy-start | bytes 1572868
  11.0 14.9 %copy-start.6 = (bf16[40,2,128,128]{3,2,1,0:T(8,128)(2,1)S(1)}, bf16[40,2,128,128]{3,2,1,0:T(8,128)(2,1)}, u32[]{:S(2)}) copy-start(bf16[40,2,128,128]{3,2,1,0:T(8,128)(2,1)} %param.9) | copy-start | bytes 7864324
  11.1 14.9 %copy-start.11 = (s32[2]{0:T(128)S(1)}, s32[2]{0:T(128)}, u32[]{:S(2)}) copy-start(s32[2]{0:T(128)} %width_ref.3) | copy-start | bytes 28
  11.4 8.2 %collective-permute-start = (f32[104,256]{1,0:T(8,128)S(1)}, f32[104,256]{1,0:T(8,128)S(1)}, u32[]{:S(2)}, u32[]{:S(2)}) collective-permute-start(f32[104,256]{1,0:T(8,128)S(1)} %get-tuple-element.23), channel_id=1, source_target_pairs={{0,8},{8,16},{16,24},{24,0},{1,9},{9,17},{17,25},{25,1},{2,10},{10... | collective-permute-start | bytes 319496 | tf_op jit(solution)/shard_map/ppermute | solution.py:474
  12.9 6.9 %collective-permute-start.1 = (f32[104,256]{1,0:T(8,128)S(1)}, f32[104,256]{1,0:T(8,128)S(1)}, u32[]{:S(2)}, u32[]{:S(2)}) collective-permute-start(f32[104,256]{1,0:T(8,128)S(1)} %get-tuple-element.24), channel_id=1, source_target_pairs={{8,0},{16,8},{24,16},{0,24},{9,1},{17,9},{25,17},{1,25},{10,2},{18... | collective-permute-start | bytes 319496 | tf_op jit(solution)/shard_map/ppermute | solution.py:474
  17.0 15.6 %collective-permute-start.5 = (bf16[5,144,128]{2,1,0:T(8,128)(2,1)S(1)}, bf16[5,144,128]{2,1,0:T(8,128)(2,1)S(1)}, u32[]{:S(2)}, u32[]{:S(2)}) collective-permute-start(bf16[5,144,128]{2,1,0:T(8,128)(2,1)S(1)} %get-tuple-element.32), channel_id=1, source_target_pairs={{8,0},{16,8},{24,16},{0,24},{9,1},{17,9},{25,17},{1,25},{10,2},{18... | collective-permute-start | bytes 552968 | tf_op jit(solution)/shard_map/ppermute | solution.py:474
  19.5 13.2 %collective-permute-start.4 = (bf16[5,144,128]{2,1,0:T(8,128)(2,1)S(1)}, bf16[5,144,128]{2,1,0:T(8,128)(2,1)S(1)}, u32[]{:S(2)}, u32[]{:S(2)}) collective-permute-start(bf16[5,144,128]{2,1,0:T(8,128)(2,1)S(1)} %get-tuple-element.27.order_ref), channel_id=1, source_target_pairs={{0,8},{8,16},{16,24},{24,0},{1,9},{9,17},{17,25},{25,1},{2,10},{10... | collective-permute-start | bytes 552968 | tf_op jit(solution)/shard_map/ppermute | solution.py:474
  19.8 12.9 %collective-permute-start.6 = (f32[200,256]{1,0:T(8,128)S(1)}, f32[200,256]{1,0:T(8,128)S(1)}, u32[]{:S(2)}, u32[]{:S(2)}) collective-permute-start(f32[200,256]{1,0:T(8,128)S(1)} %get-tuple-element.33), channel_id=1, source_target_pairs={{0,2},{2,4},{4,6},{1,3},{3,5},{5,7},{8,10},{10,12},{12,14},{9,11},... | collective-permute-start | bytes 614408 | tf_op jit(solution)/shard_map/ppermute | solution.py:474
  24.7 8.1 %collective-permute-start.7 = (f32[200,256]{1,0:T(8,128)S(1)}, f32[200,256]{1,0:T(8,128)S(1)}, u32[]{:S(2)}, u32[]{:S(2)}) collective-permute-start(f32[200,256]{1,0:T(8,128)S(1)} %get-tuple-element.34), channel_id=1, source_target_pairs={{2,0},{4,2},{6,4},{3,1},{5,3},{7,5},{10,8},{12,10},{14,12},{11,9},... | collective-permute-start | bytes 614408 | tf_op jit(solution)/shard_map/ppermute | solution.py:474
  33.1 1.6 %collective-permute-start.8 = (f32[2,144,256]{2,1,0:T(8,128)S(1)}, f32[2,144,256]{2,1,0:T(8,128)S(1)}, u32[]{:S(2)}, u32[]{:S(2)}) collective-permute-start(f32[2,144,256]{2,1,0:T(8,128)S(1)} %frame.1.mine_ref), channel_id=1, source_target_pairs={{0,1},{1,0},{2,3},{3,2},{4,5},{5,4},{6,7},{7,6},{8,9},{9,8},{10,11... | collective-permute-start | bytes 884744 | tf_op jit(solution)/shard_map/ppermute | solution.py:601
  34.8 6.3 %collective-permute-start.9 = (f32[2,24,256]{2,1,0:T(8,128)S(1)}, f32[2,24,256]{2,1,0:T(8,128)S(1)}, u32[]{:S(2)}, u32[]{:S(2)}) collective-permute-start(f32[2,24,256]{2,1,0:T(8,128)S(1)} %get-tuple-element.36), channel_id=1, source_target_pairs={{0,2},{2,4},{4,6},{1,3},{3,5},{5,7},{8,10},{10,12},{12,14},{9,11},... | collective-permute-start | bytes 147464 | tf_op jit(solution)/shard_map/ppermute | solution.py:474
  39.4 6.0 %collective-permute-start.10 = (f32[2,24,256]{2,1,0:T(8,128)S(1)}, f32[2,24,256]{2,1,0:T(8,128)S(1)}, u32[]{:S(2)}, u32[]{:S(2)}) collective-permute-start(f32[2,24,256]{2,1,0:T(8,128)S(1)} %get-tuple-element.37), channel_id=1, source_target_pairs={{2,0},{4,2},{6,4},{3,1},{5,3},{7,5},{10,8},{12,10},{14,12},{11,9},... | collective-permute-start | bytes 147464 | tf_op jit(solution)/shard_map/ppermute | solution.py:474
  45.8 5.0 %collective-permute-start.11 = (f32[48,256]{1,0:T(8,128)S(1)}, f32[48,256]{1,0:T(8,128)S(1)}, u32[]{:S(2)}, u32[]{:S(2)}) collective-permute-start(f32[48,256]{1,0:T(8,128)S(1)} %get-tuple-element.39), channel_id=1, source_target_pairs={{0,8},{8,16},{16,24},{24,0},{1,9},{9,17},{17,25},{25,1},{2,10},{10... | collective-permute-start | bytes 147464 | tf_op jit(solution)/shard_map/ppermute | solution.py:474
  46.7 4.1 %collective-permute-start.12 = (f32[48,256]{1,0:T(8,128)S(1)}, f32[48,256]{1,0:T(8,128)S(1)}, u32[]{:S(2)}, u32[]{:S(2)}) collective-permute-start(f32[48,256]{1,0:T(8,128)S(1)} %get-tuple-element.40), channel_id=1, source_target_pairs={{8,0},{16,8},{24,16},{0,24},{9,1},{17,9},{25,17},{1,25},{10,2},{18... | collective-permute-start | bytes 147464 | tf_op jit(solution)/shard_map/ppermute | solution.py:474

commit v4 on v3

--- a/solution.py
+++ b/solution.py
@@ -122,31 +122,33 @@
             lat_ref[level, :, height : 2 * height] = low
             lat_ref[level, :, 2 * height :] = high
 
+    def put(level, start, value):
+        high, low = split(value)
+        stop = start + value.shape[1]
+        stack_ref[level, :height, start:stop] = high
+        stack_ref[level, height : 2 * height, start:stop] = high
+        stack_ref[level, 2 * height :, start:stop] = low
+
     for level in range(2):
         packed = jnp.zeros((height, LANES), F32)
         for t in range(MEMBERS):
             field = alpha_ref[2 * t + level]
             both = dot(jnp.concatenate([field, field], 1), lon_ref[level, t])
-            high, low = split(both[:, :width])
-            stack_ref[:height, t * width : (t + 1) * width] = high
-            stack_ref[height : 2 * height, t * width : (t + 1) * width] = high
-            stack_ref[2 * height :, t * width : (t + 1) * width] = low
+            put(level, t * width, both[:, :width])
             packed = packed + both[:, width:]
-        high, low = split(packed)
-        stack_ref[:height, MEMBERS * width :] = high
-        stack_ref[height : 2 * height, MEMBERS * width :] = high
-        stack_ref[2 * height :, MEMBERS * width :] = low
+        put(level, MEMBERS * width, packed)
+    for level in range(2):
         total = sum_ref[level]
         for pair in range(MEMBERS // 2):
             base = 2 * pair * width
-            wide = dot(lat_ref[level], stack_ref[:, base : base + 2 * width])
+            wide = dot(lat_ref[level], stack_ref[level, :, base : base + 2 * width])
             for side in range(2):
                 k = 2 * (2 * pair + side) + level
                 field = wide[:, side * width : (side + 1) * width]
                 total = total + perts_ref[k].astype(F32) * field[:height]
                 rows_ref[k] = field[height:]
         sum_ref[level] = total
-        cols_ref[0, level] = dot(lat_ref[level], stack_ref[:, MEMBERS * width :])
+        cols_ref[0, level] = dot(lat_ref[level], stack_ref[level, :, MEMBERS * width :])
 
 
 def stacked_cell(index, size, base):
@@ -160,6 +162,18 @@
 def interpolate(cell, index, weight):
     near = jnp.where(cell == index, 1.0 - weight, 0.0)
     return near + jnp.where(cell == index + 1, weight, 0.0)
+
+
+def seal(axis, next_ref, previous_ref):
+    place = lax.axis_index(axis)
+
+    @pl.when(place == lax.axis_size(axis) - 1)
+    def _():
+        next_ref[...] = jnp.zeros_like(next_ref)
+
+    @pl.when(place == 0)
+    def _():
+        previous_ref[...] = jnp.zeros_like(previous_ref)
 
 
 def rows_kernel(perts_ref, next_ref, previous_ref, sems):
@@ -172,6 +186,7 @@
         copy.start()
     for copy in copies:
         copy.wait()
+    seal("gy", next_ref, previous_ref)
 
 
 def table(index, weight):
@@ -212,10 +227,11 @@
     next_ref[8 * SKIRT :, :LANES] = lat[:, rows - LANES :]
     previous_ref[8 * SKIRT :, :LANES] = lat[:, :LANES]
     token_ref[...] = lat[:, :LANES]
+    seal("gy", next_ref, previous_ref)
 
 
 def frame_kernel(
-    sum_ref, rows_ref, cols_ref, above_ref, below_ref, west_ref, east_ref, order_ref, after_ref, out_ref
+    sum_ref, rows_ref, cols_ref, above_ref, below_ref, west_ref, east_ref, out_ref
 ):
     height, width = sum_ref.shape[1], sum_ref.shape[2]
     ext = height + 2 * HB
@@ -251,6 +267,7 @@
     next_ref[:, 2 * HB :] = total[:, height + HB :]
     previous_ref[:, :HB] = total[:, height : height + HB]
     previous_ref[:, HB:] = total[:, : 2 * HB]
+    seal("gy", next_ref, previous_ref)
 
 
 def strips_kernel(width, total_ref, above_ref, below_ref, stack_ref, east_ref, west_ref):
@@ -428,28 +445,27 @@
         cell = jnp.where(half, west, east) if level == 0 else jnp.where(half, east, west)
         side = dot(lat_ref[level], stacked(cell * edge_ref[level]))
         side = jnp.concatenate(split(side), 0)
-        stack_ref[...] = side
-        own = own_ref[level]
-
-        def pair(p, carry):
+        for p in range(MEMBERS // 2):
             columns = []
-            for number in range(2):
-                k = 4 * p + 2 * number + level
+            for t in (2 * p, 2 * p + 1):
+                k = 2 * t + level
                 field = jnp.concatenate(
                     [perts_ref[k].astype(F32), above_ref[k].astype(F32), below_ref[k].astype(F32)], 0
                 )
                 columns.append(stacked(field * own_ref[level]))
-            wide = dot(lat_ref[level], jnp.concatenate(columns, 1))
+            both = dot(lat_ref[level], jnp.concatenate(columns, 1))
             for number in range(2):
-                t = 2 * p + number
-                k = 4 * p + 2 * number + level
-                parts = jnp.concatenate(split(wide[:, number * width : (number + 1) * width]), 0)
-                both = dot(jnp.concatenate([parts, stack_ref[...]], 1), lon_ref[level, t])
-                total = both[:height, :width] + both[:height, width:] + both[height:, :width]
-                out_ref[k] = alpha_ref[k].astype(F32) + total
-            return carry
-
-        lax.fori_loop(0, MEMBERS // 2, pair, 0, unroll=4)
+                k = 2 * (2 * p + number) + level
+                high, low = split(both[:, number * width : (number + 1) * width])
+                stack_ref[k, :height, :width] = high
+                stack_ref[k, height:, :width] = low
+                stack_ref[k, :, width:] = side
+    for level in range(2):
+        for t in range(MEMBERS):
+            k = 2 * t + level
+            both = dot(stack_ref[k], lon_ref[level, t])
+            total = both[:height, :width] + both[:height, width:] + both[height:, :width]
+            out_ref[k] = alpha_ref[k].astype(F32) + total
 
 
 def GRAD_SCRATCH(height, width):
@@ -457,21 +473,17 @@
     return [
         pltpu.VMEM((2, MEMBERS, width + LANES, 2 * width), BF16),
         pltpu.VMEM((2, height, 3 * ext), BF16),
-        pltpu.VMEM((2 * height, LANES), BF16),
+        pltpu.VMEM((GROUP, 2 * height, width + LANES), BF16),
     ]
 
 
-def ring(axis, periodic):
+def exchange(to_next, to_previous, axis):
     count = lax.axis_size(axis)
-    forward = [(i, i + 1) for i in range(count - 1)]
-    if periodic:
-        forward.append((count - 1, 0))
-    return forward, [(target, source) for source, target in forward]
-
-
-def exchange(to_next, to_previous, axis, periodic):
-    forward, backward = ring(axis, periodic)
-    return lax.ppermute(to_next, axis, forward), lax.ppermute(to_previous, axis, backward)
+    forward = [(i, (i + 1) % count) for i in range(count)]
+    backward = [(target, source) for source, target in forward]
+    ahead = lax.ppermute(to_next, axis, forward)
+    behind = lax.ppermute(to_previous, axis, backward)
+    return ahead, behind
 
 
 def vmem(*shape):
@@ -486,7 +498,7 @@
     return jax.ShapeDtypeStruct(shape, dtype)
 
 
-def body(
+def whole_step(
     alpha_fields,
     member_perts,
     band_widths,
@@ -510,7 +522,7 @@
     lanes = rounded(width + 2 * HB, LANES)
     tall = rounded(ext + 2 * STRIP, LANES)
 
-    def call(kernel, out_shape, name, flops=10**8, grant=4, **more):
+    def call(kernel, out_shape, flops=10**8, grant=4, **more):
         semantics = ("arbitrary",) if "grid" in more else ()
         return pl.pallas_call(
             kernel,
@@ -518,7 +530,6 @@
             compiler_params=pltpu.CompilerParams(
                 dimension_semantics=semantics, vmem_limit_bytes=min(60, grant * scale) * 1024 * 1024
             ),
-            name=name,
             cost_estimate=pl.CostEstimate(flops=flops, bytes_accessed=10**6, transcendentals=0),
             **more,
         )
@@ -527,40 +538,35 @@
     to_next, to_previous = call(
         rows_kernel,
         [edge, edge],
-        "rows",
         in_specs=[pl.BlockSpec(memory_space=pltpu.HBM)],
         out_specs=[pl.BlockSpec(memory_space=pltpu.VMEM)] * 2,
         scratch_shapes=[pltpu.SemaphoreType.DMA((2,))],
     )(perts)
-    above, below = exchange(to_next, to_previous, "gy", False)
+    above, below = exchange(to_next, to_previous, "gy")
 
     side = shaped((4 * SKIRT + 8, fine_h))
-    to_next, to_previous = call(fine_cols_kernel, [side, side], "fine_cols")(
+    to_next, to_previous = call(fine_cols_kernel, [side, side])(
         innovation, obs_weight, lon_index, lon_weight
     )
-    fine_west, fine_east = exchange(to_next, to_previous, "gx", True)
+    fine_west, fine_east = exchange(to_next, to_previous, "gx")
 
     packed = shaped((groups, ext, LANES), BF16)
     to_next, to_previous = call(
         pack_kernel,
         [packed, packed],
-        "pack",
         grant=8,
         grid=(groups,),
         in_specs=[grouped(GROUP, height, width)] + [grouped(GROUP, HB, width)] * 2,
         out_specs=[grouped(1, ext, LANES)] * 2,
     )(perts, above, below)
-    west, east = exchange(to_next, to_previous, "gx", True)
+    west, east = exchange(to_next, to_previous, "gx")
 
     strip = shaped((8 * SKIRT + 8, fine_w))
     whole = pl.BlockSpec(memory_space=pltpu.VMEM)
     to_next, to_previous, token = call(
-        fine_rows_kernel,
-        [strip, strip, shaped((8, LANES))],
-        "fine_rows",
-        in_specs=[whole] * 6 + [anywhere],
+        fine_rows_kernel, [strip, strip, shaped((8, LANES))], in_specs=[whole] * 6 + [anywhere]
     )(innovation, obs_weight, lat_index, lat_weight, fine_west, fine_east, to_next)
-    fine_above, fine_below = exchange(to_next, to_previous, "gy", False)
+    fine_above, fine_below = exchange(to_next, to_previous, "gy")
 
     partial, edge_rows, edge_cols = call(
         local_kernel,
@@ -569,7 +575,6 @@
             shaped((fields, 2 * HB, width)),
             shaped((groups, 2, ext, LANES)),
         ],
-        "local",
         flops=10**10,
         grant=16,
         grid=(groups,),
@@ -587,35 +592,31 @@
         scratch_shapes=[
             pltpu.VMEM((2, MEMBERS, 2 * width, width + LANES), BF16),
             pltpu.VMEM((2, ext, 3 * height), BF16),
-            pltpu.VMEM((3 * height, MEMBERS * width + LANES), BF16),
+            pltpu.VMEM((2, 3 * height, MEMBERS * width + LANES), BF16),
         ],
     )(band_widths, alpha, perts, token)
 
     framed = call(
-        frame_kernel,
-        shaped((2, ext, width + LANES)),
-        "frame",
-        in_specs=[whole] * 7 + [anywhere] * 2,
-    )(partial, edge_rows, edge_cols, above, below, west, east, fine_above, fine_below)
+        frame_kernel, shaped((2, ext, width + LANES)), in_specs=[whole] * 7
+    )(partial, edge_rows, edge_cols, above, below, west, east)
     count = lax.axis_size("ma")
     other = lax.ppermute(framed, "ma", [(i, (i + 1) % count) for i in range(count)])
     strip = shaped((2, STRIP, lanes))
     framed, to_next, to_previous = call(
-        total_kernel, [shaped((2, ext, lanes)), strip, strip], "total"
+        total_kernel, [shaped((2, ext, lanes)), strip, strip]
     )(framed, other)
-    north, south = exchange(to_next, to_previous, "gy", False)
+    north, south = exchange(to_next, to_previous, "gy")
     strip = shaped((2 * STRIP, tall))
     stack, to_next, to_previous = call(
-        functools.partial(strips_kernel, width), [shaped((2, tall, lanes)), strip, strip], "strips"
+        functools.partial(strips_kernel, width), [shaped((2, tall, lanes)), strip, strip]
     )(framed, north, south)
-    strip_west, strip_east = exchange(to_next, to_previous, "gx", True)
+    strip_west, strip_east = exchange(to_next, to_previous, "gx")
 
     lon_total = width * lax.axis_size("gx")
     everything = [pl.BlockSpec(memory_space=pltpu.VMEM)] * 13
     increment, own, edge = call(
         functools.partial(fine_kernel, lon_total),
         [shaped((2, fine_h, fine_w)), shaped((2, ext, width)), shaped((2, ext, LANES))],
-        "fine",
         grant=16,
         in_specs=everything,
         scratch_shapes=[
@@ -641,7 +642,6 @@
     gradient = call(
         gradient_kernel,
         shaped((fields, height, width)),
-        "gradient",
         grant=16,
         grid=(groups,),
         in_specs=[
@@ -674,7 +674,7 @@
         P(None, "gy", "gx"),
     )
     return jax.shard_map(
-        body,
+        whole_step,
         mesh=mesh,
         in_specs=placed,
         out_specs=(P(None, "gy", "gx"), P("ma", None, "gy", "gx")),

time: 68.7 us -> 62.7 us (0.913)
  Pallas kernels: 27.3 us -> 21.6 us
  starting transfers between devices: 26.8 us -> 21.4 us
  waiting for transfers between devices: 9.4 us -> 14.7 us
    pallas_call x10, Pallas kernels: 27.3 us -> 21.6 us  [the longest x1 8.48 us: whole_step(): call(gradient_kernel, shaped((fields, height, width)), grant=16, grid=(gr...]
    ppermute x13, starting transfers between devices: 26.8 us -> 21.4 us  [the longest x6 13.2 us: exchange(): behind = lax.ppermute(to_previous, axis, backward)]
    ppermute x13, waiting for transfers between devices: 9.4 us -> 14.7 us  [the longest x6 12.3 us: exchange(): ahead = lax.ppermute(to_next, axis, forward)]
where the time goes in v4:
time: 62.7 us; the launch traced here: 62.4 us
  Pallas kernels  21.6 us (34%)
  starting transfers between devices  21.4 us (34%)
  waiting for transfers between devices  14.7 us (23%)
  local copies, waits for them, and re-layouts  3.86 us (6%)
  between operations  0.82 us (1%)
    ppermute x6, starting transfers between devices, exchange(): behind = lax.ppermute(to_previous, axis, backward)  13.2 us
    ppermute x6, waiting for transfers between devices, exchange(): ahead = lax.ppermute(to_next, axis, forward)  12.3 us
    pallas_call x1, Pallas kernels, whole_step(): call(gradient_kernel, shaped((fields, height, width)), grant=16, grid=(gr...  8.48 us
    ppermute x6, starting transfers between devices, exchange(): ahead = lax.ppermute(to_next, axis, forward)  8.15 us
    pallas_call x1, Pallas kernels, whole_step(): call(local_kernel, [shaped((2, height, width)), shaped((fields, 2 * HB, w...  5.57 us
    pallas_call x1, Pallas kernels, whole_step(): call(functools.partial(fine_kernel, lon_total), [shaped((2, fine_h, fine_...  4.44 us
    unnamed x24, local copies, waits for them, and re-layouts  3.86 us
    ppermute x6, waiting for transfers between devices, exchange(): behind = lax.ppermute(to_previous, axis, backward)  2.4 us
  transfers between devices with their start and end apart: 13, of which 6 were waited for; matrix products, arithmetic and copies ran while one was open for 0% of the time, Pallas kernels for 13%

profile of v4, /device:TPU:0, one launch (start us, length us, event | category | flops | bytes accessed | tf_op | source)
XLA Modules:
  0.0 62.4 jit_solution(14752013881382484224)
XLA Ops:
  0.6 0.0 copy-start.9
  0.6 0.0 copy-start
  0.7 1.7 %copy-done = bf16[40,2,128,128]{3,2,1,0:T(8,128)(2,1)S(1)} copy-done((bf16[40,2,128,128]{3,2,1,0:T(8,128)(2,1)S(1)}, bf16[40,2,128,128]{3,2,1,0:T(8,128)(2,1)}, u32[]{:S(2)}) %copy-start) | copy-done | bytes 2621464
  2.4 0.1 shard_map.105
  2.5 0.0 copy-start.7
  2.5 0.0 copy-start.8
  2.6 3.1 %collective-permute-start.2 = (bf16[80,8,128]{2,1,0:T(8,128)(2,1)S(1)}, bf16[80,8,128]{2,1,0:T(8,128)(2,1)S(1)}, u32[]{:S(2)}, u32[]{:S(2)}) collective-permute-start(bf16[80,8,128]{2,1,0:T(8,128)(2,1)S(1)} %get-tuple-element.25), channel_id=1, source_target_pairs={{0,2},{2,4},{4,6},{6,0},{1,3},{3,5},{5,7},{7,1},{8,10},{10,12},{12... | collective-permute-start | bytes 491528 | tf_op jit(solution)/shard_map/ppermute | solution.py:484
  5.6 2.1 %collective-permute-start.3 = (bf16[80,8,128]{2,1,0:T(8,128)(2,1)S(1)}, bf16[80,8,128]{2,1,0:T(8,128)(2,1)S(1)}, u32[]{:S(2)}, u32[]{:S(2)}) collective-permute-start(bf16[80,8,128]{2,1,0:T(8,128)(2,1)S(1)} %get-tuple-element.26), channel_id=1, source_target_pairs={{2,0},{4,2},{6,4},{0,6},{3,1},{5,3},{7,5},{1,7},{10,8},{12,10},{14... | collective-permute-start | bytes 491528 | tf_op jit(solution)/shard_map/ppermute | solution.py:485
  7.8 0.0 copy-done.9
  7.8 0.0 copy-done.10
  7.8 1.0 %copy-done.2 = f32[2,256,256]{2,1,0:T(8,128)S(1)} copy-done((f32[2,256,256]{2,1,0:T(8,128)S(1)}, f32[2,256,256]{2,1,0:T(8,128)}, u32[]{:S(2)}) %copy-start.2) | copy-done | bytes 524312
  8.8 1.0 %copy-done.4 = f32[2,256,256]{2,1,0:T(8,128)S(1)} copy-done((f32[2,256,256]{2,1,0:T(8,128)S(1)}, f32[2,256,256]{2,1,0:T(8,128)}, u32[]{:S(2)}) %copy-start.4) | copy-done | bytes 524312
  9.9 0.3 shard_map.104
  10.2 1.7 %collective-permute-start = (f32[104,256]{1,0:T(8,128)S(1)}, f32[104,256]{1,0:T(8,128)S(1)}, u32[]{:S(2)}, u32[]{:S(2)}) collective-permute-start(f32[104,256]{1,0:T(8,128)S(1)} %get-tuple-element.23), channel_id=1, source_target_pairs={{0,8},{8,16},{16,24},{24,0},{1,9},{9,17},{17,25},{25,1},{2,10},{10... | collective-permute-start | bytes 319496 | tf_op jit(solution)/shard_map/ppermute | solution.py:484
  11.9 1.3 %collective-permute-start.1 = (f32[104,256]{1,0:T(8,128)S(1)}, f32[104,256]{1,0:T(8,128)S(1)}, u32[]{:S(2)}, u32[]{:S(2)}) collective-permute-start(f32[104,256]{1,0:T(8,128)S(1)} %get-tuple-element.24), channel_id=1, source_target_pairs={{8,0},{16,8},{24,16},{0,24},{9,1},{17,9},{25,17},{1,25},{10,2},{18... | collective-permute-start | bytes 319496 | tf_op jit(solution)/shard_map/ppermute | solution.py:485
  13.1 0.0 collective-permute-done.2.above_ref
  13.2 1.7 %collective-permute-done.3.below_ref = bf16[80,8,128]{2,1,0:T(8,128)(2,1)S(1)} collective-permute-done((bf16[80,8,128]{2,1,0:T(8,128)(2,1)S(1)}, bf16[80,8,128]{2,1,0:T(8,128)(2,1)S(1)}, u32[]{:S(2)}, u32[]{:S(2)}) %collective-permute-start.3) | collective-permute-done | bytes 163872 | tf_op jit(solution)/shard_map/ppermute | solution.py:485
  14.8 0.0 copy-done.1
  14.8 1.8 %shard_map.106 = (bf16[5,144,128]{2,1,0:T(8,128)(2,1)S(1)}, bf16[5,144,128]{2,1,0:T(8,128)(2,1)S(1)}) custom-call(bf16[80,128,128]{2,1,0:T(8,128)(2,1)S(1)} %bitcast.4, bf16[80,8,128]{2,1,0:T(8,128)(2,1)S(1)} %collective-permute-done.2.above_ref, bf16[80,8,128]{2,1,0:T(8,128)(2,1)S(1)} %collective-permute-done.3.below_ref), custom_call_target="tpu_custom_call" | custom-call | flops 100000000 | bytes 1000000 | tf_op jit(solution)/shard_map/pallas_call | solution.py:554
  16.7 2.5 %collective-permute-start.5 = (bf16[5,144,128]{2,1,0:T(8,128)(2,1)S(1)}, bf16[5,144,128]{2,1,0:T(8,128)(2,1)S(1)}, u32[]{:S(2)}, u32[]{:S(2)}) collective-permute-start(bf16[5,144,128]{2,1,0:T(8,128)(2,1)S(1)} %get-tuple-element.32), channel_id=1, source_target_pairs={{8,0},{16,8},{24,16},{0,24},{9,1},{17,9},{25,17},{1,25},{10,2},{18... | collective-permute-start | bytes 552968 | tf_op jit(solution)/shard_map/ppermute | solution.py:485
  19.2 0.0 collective-permute-start.4
  19.2 0.0 collective-permute-done.west_ref
  19.2 0.0 collective-permute-done.1.east_ref
  19.2 0.0 copy-done.7
  19.2 0.0 copy-done.8
  19.2 0.0 copy-done.3
  19.2 0.0 copy-done.5
  19.3 5.6 %shard_map.108 = (f32[2,128,128]{2,1,0:T(8,128)S(1)}, f32[80,16,128]{2,1,0:T(8,128)S(1)}, f32[5,2,144,128]{3,2,1,0:T(8,128)S(1)}) custom-call(s32[2]{0:T(128)S(1)} %copy-done.11, bf16[80,128,128]{2,1,0:T(8,128)(2,1)S(1)} %bitcast.7, bf16[80,128,128]{2,1,0:T(8,128)(2,1)S(1)} %bitcast.5, f32[8,128]{1,0:T(8,128)S(1)} %get-tuple-element.28.token_ref), custom_call_target="tpu_custom_call" | custom-call | flops 10000000000 | bytes 1000000 | tf_op jit(solution)/shard_map/pallas_call | solution.py:571
  24.9 0.0 collective-permute-done.5.east_ref
  24.9 2.7 %collective-permute-done.4.west_ref = bf16[5,144,128]{2,1,0:T(8,128)(2,1)S(1)} collective-permute-done((bf16[5,144,128]{2,1,0:T(8,128)(2,1)S(1)}, bf16[5,144,128]{2,1,0:T(8,128)(2,1)S(1)}, u32[]{:S(2)}, u32[]{:S(2)}) %collective-permute-start.4) | collective-permute-done | bytes 184352 | tf_op jit(solution)/shard_map/ppermute | solution.py:484
  27.6 0.4 shard_map.109.mine_ref
  28.0 0.1 collective-permute-start.6
  28.1 1.8 %collective-permute-start.11 = (f32[200,256]{1,0:T(8,128)S(1)}, f32[200,256]{1,0:T(8,128)S(1)}, u32[]{:S(2)}, u32[]{:S(2)}) collective-permute-start(f32[200,256]{1,0:T(8,128)S(1)} %get-tuple-element.39), channel_id=1, source_target_pairs={{0,2},{2,4},{4,6},{6,0},{1,3},{3,5},{5,7},{7,1},{8,10},{10,12},{12... | collective-permute-start | bytes 614408 | tf_op jit(solution)/shard_map/ppermute | solution.py:484
  29.9 2.1 %collective-permute-start.12 = (f32[200,256]{1,0:T(8,128)S(1)}, f32[200,256]{1,0:T(8,128)S(1)}, u32[]{:S(2)}, u32[]{:S(2)}) collective-permute-start(f32[200,256]{1,0:T(8,128)S(1)} %get-tuple-element.40), channel_id=1, source_target_pairs={{2,0},{4,2},{6,4},{0,6},{3,1},{5,3},{7,5},{1,7},{10,8},{12,10},{14... | collective-permute-start | bytes 614408 | tf_op jit(solution)/shard_map/ppermute | solution.py:485
  32.0 0.0 collective-permute-done.6.other_ref
  32.0 0.1 collective-permute-start.7
  32.1 3.8 %collective-permute-start.8 = (f32[2,24,256]{2,1,0:T(8,128)S(1)}, f32[2,24,256]{2,1,0:T(8,128)S(1)}, u32[]{:S(2)}, u32[]{:S(2)}) collective-permute-start(f32[2,24,256]{2,1,0:T(8,128)S(1)} %get-tuple-element.35), channel_id=1, source_target_pairs={{2,0},{4,2},{6,4},{0,6},{3,1},{5,3},{7,5},{1,7},{10,8},{12,10},{14... | collective-permute-start | bytes 147464 | tf_op jit(solution)/shard_map/ppermute | solution.py:485
  35.9 7.5 %collective-permute-done.7.above_ref = f32[2,24,256]{2,1,0:T(8,128)S(1)} collective-permute-done((f32[2,24,256]{2,1,0:T(8,128)S(1)}, f32[2,24,256]{2,1,0:T(8,128)S(1)}, u32[]{:S(2)}, u32[]{:S(2)}) %collective-permute-start.7) | collective-permute-done | bytes 49184 | tf_op jit(solution)/shard_map/ppermute | solution.py:484
  43.4 0.1 collective-permute-done.8.below_ref
  43.5 0.4 shard_map.111
  43.9 1.5 %collective-permute-start.9 = (f32[48,256]{1,0:T(8,128)S(1)}, f32[48,256]{1,0:T(8,128)S(1)}, u32[]{:S(2)}, u32[]{:S(2)}) collective-permute-start(f32[48,256]{1,0:T(8,128)S(1)} %get-tuple-element.37), channel_id=1, source_target_pairs={{0,8},{8,16},{16,24},{24,0},{1,9},{9,17},{17,25},{25,1},{2,10},{10... | collective-permute-start | bytes 147464 | tf_op jit(solution)/shard_map/ppermute | solution.py:484
  45.4 1.4 %collective-permute-start.10 = (f32[48,256]{1,0:T(8,128)S(1)}, f32[48,256]{1,0:T(8,128)S(1)}, u32[]{:S(2)}, u32[]{:S(2)}) collective-permute-start(f32[48,256]{1,0:T(8,128)S(1)} %get-tuple-element.38), channel_id=1, source_target_pairs={{8,0},{16,8},{24,16},{0,24},{9,1},{17,9},{25,17},{1,25},{10,2},{18... | collective-permute-start | bytes 147464 | tf_op jit(solution)/shard_map/ppermute | solution.py:485
  46.9 0.0 collective-permute-done.11.above_ref
  46.9 0.0 collective-permute-done.12.below_ref
  46.9 2.1 %collective-permute-done.9.strip_west_ref = f32[48,256]{1,0:T(8,128)S(1)} collective-permute-done((f32[48,256]{1,0:T(8,128)S(1)}, f32[48,256]{1,0:T(8,128)S(1)}, u32[]{:S(2)}, u32[]{:S(2)}) %collective-permute-start.9) | collective-permute-done | bytes 49184 | tf_op jit(solution)/shard_map/ppermute | solution.py:484
  48.9 0.6 collective-permute-done.10.strip_east_ref
  49.5 4.4 %shard_map.112 = (f32[2,256,256]{2,1,0:T(8,128)}, f32[2,144,128]{2,1,0:T(8,128)S(1)}, f32[2,144,128]{2,1,0:T(8,128)S(1)}) custom-call(f32[2,256,256]{2,1,0:T(8,128)S(1)} %get-tuple-element.36.stack_ref, f32[48,256]{1,0:T(8,128)S(1)} %collective-permute-done.9.strip_west_ref, f32[48,256]{1,0:T(8,128)S(1)} %collective-permute-done.10.strip_east_ref, ...), custom_call_target="tpu_custom_call" | custom-call | flops 100000000 | bytes 1000000 | tf_op jit(solution)/shard_map/pallas_call | solution.py:617
  54.0 8.5 %shard_map.113 = f32[80,128,128]{2,1,0:T(8,128)} custom-call(s32[2]{0:T(128)S(1)} %copy-done.11, bf16[80,128,128]{2,1,0:T(8,128)(2,1)S(1)} %bitcast.8, bf16[80,128,128]{2,1,0:T(8,128)(2,1)S(1)} %bitcast.6, bf16[80,8,128]{2,1,0:T(8,128)(2,1)S(1)} %collective-permute-done.2.above_ref, bf16[80,8,128]{2,1,0:T(8,128)(2,1)S(1)} %collective-permute-done.3.below_ref, ...), custom_call_target="tpu_custom_call" | custom-call | flops 100000000 | bytes 1000000 | tf_op jit(solution)/shard_map/pallas_call | solution.py:642
  (12 shorter events, 0.1 us)
Async XLA Ops:
  0.6 7.1 %copy-start.9 = (s32[256]{0:T(256)S(1)}, s32[256]{0:T(256)}, u32[]{:S(2)}) copy-start(s32[256]{0:T(256)} %lon_index_ref.1) | copy-start | bytes 3076
  0.6 1.7 %copy-start = (bf16[40,2,128,128]{3,2,1,0:T(8,128)(2,1)S(1)}, bf16[40,2,128,128]{3,2,1,0:T(8,128)(2,1)}, u32[]{:S(2)}) copy-start(bf16[40,2,128,128]{3,2,1,0:T(8,128)(2,1)} %param.10) | copy-start | bytes 7864324
  2.4 5.4 %copy-start.10 = (f32[256]{0:T(256)S(1)}, f32[256]{0:T(256)}, u32[]{:S(2)}) copy-start(f32[256]{0:T(256)} %lon_share_ref.1) | copy-start | bytes 3076
  2.4 12.4 %copy-start.1 = (bf16[40,2,128,128]{3,2,1,0:T(8,128)(2,1)S(1)}, bf16[40,2,128,128]{3,2,1,0:T(8,128)(2,1)}, u32[]{:S(2)}) copy-start(bf16[40,2,128,128]{3,2,1,0:T(8,128)(2,1)} %param.10) | copy-start | bytes 7864324
  2.5 16.7 %copy-start.7 = (s32[256]{0:T(256)S(1)}, s32[256]{0:T(256)}, u32[]{:S(2)}) copy-start(s32[256]{0:T(256)} %lat_index_ref.1) | copy-start | bytes 3076
  2.5 16.7 %copy-start.8 = (f32[256]{0:T(256)S(1)}, f32[256]{0:T(256)}, u32[]{:S(2)}) copy-start(f32[256]{0:T(256)} %lat_share_ref.1) | copy-start | bytes 3076
  2.6 10.6 %collective-permute-start.2 = (bf16[80,8,128]{2,1,0:T(8,128)(2,1)S(1)}, bf16[80,8,128]{2,1,0:T(8,128)(2,1)S(1)}, u32[]{:S(2)}, u32[]{:S(2)}) collective-permute-start(bf16[80,8,128]{2,1,0:T(8,128)(2,1)S(1)} %get-tuple-element.25), channel_id=1, source_target_pairs={{0,2},{2,4},{4,6},{6,0},{1,3},{3,5},{5,7},{7,1},{8,10},{10,12},{12... | collective-permute-start | bytes 491528 | tf_op jit(solution)/shard_map/ppermute | solution.py:484
  5.6 9.2 %collective-permute-start.3 = (bf16[80,8,128]{2,1,0:T(8,128)(2,1)S(1)}, bf16[80,8,128]{2,1,0:T(8,128)(2,1)S(1)}, u32[]{:S(2)}, u32[]{:S(2)}) collective-permute-start(bf16[80,8,128]{2,1,0:T(8,128)(2,1)S(1)} %get-tuple-element.26), channel_id=1, source_target_pairs={{2,0},{4,2},{6,4},{0,6},{3,1},{5,3},{7,5},{1,7},{10,8},{12,10},{14... | collective-permute-start | bytes 491528 | tf_op jit(solution)/shard_map/ppermute | solution.py:485
  7.8 1.0 %copy-start.2 = (f32[2,256,256]{2,1,0:T(8,128)S(1)}, f32[2,256,256]{2,1,0:T(8,128)}, u32[]{:S(2)}) copy-start(f32[2,256,256]{2,1,0:T(8,128)} %target_ref.5) | copy-start | bytes 1572868
  8.8 1.0 %copy-start.4 = (f32[2,256,256]{2,1,0:T(8,128)S(1)}, f32[2,256,256]{2,1,0:T(8,128)}, u32[]{:S(2)}) copy-start(f32[2,256,256]{2,1,0:T(8,128)} %weight_ref.5) | copy-start | bytes 1572868
  9.8 9.4 %copy-start.3 = (f32[2,256,256]{2,1,0:T(8,128)S(1)}, f32[2,256,256]{2,1,0:T(8,128)}, u32[]{:S(2)}) copy-start(f32[2,256,256]{2,1,0:T(8,128)} %target_ref.5) | copy-start | bytes 1572868
  9.9 9.4 %copy-start.5 = (f32[2,256,256]{2,1,0:T(8,128)S(1)}, f32[2,256,256]{2,1,0:T(8,128)}, u32[]{:S(2)}) copy-start(f32[2,256,256]{2,1,0:T(8,128)} %weight_ref.5) | copy-start | bytes 1572868
  9.9 9.4 %copy-start.6 = (bf16[40,2,128,128]{3,2,1,0:T(8,128)(2,1)S(1)}, bf16[40,2,128,128]{3,2,1,0:T(8,128)(2,1)}, u32[]{:S(2)}) copy-start(bf16[40,2,128,128]{3,2,1,0:T(8,128)(2,1)} %param.9) | copy-start | bytes 7864324
  9.9 9.4 %copy-start.11 = (s32[2]{0:T(128)S(1)}, s32[2]{0:T(128)}, u32[]{:S(2)}) copy-start(s32[2]{0:T(128)} %width_ref.3) | copy-start | bytes 28
  10.2 9.0 %collective-permute-start = (f32[104,256]{1,0:T(8,128)S(1)}, f32[104,256]{1,0:T(8,128)S(1)}, u32[]{:S(2)}, u32[]{:S(2)}) collective-permute-start(f32[104,256]{1,0:T(8,128)S(1)} %get-tuple-element.23), channel_id=1, source_target_pairs={{0,8},{8,16},{16,24},{24,0},{1,9},{9,17},{17,25},{25,1},{2,10},{10... | collective-permute-start | bytes 319496 | tf_op jit(solution)/shard_map/ppermute | solution.py:484
  11.9 7.3 %collective-permute-start.1 = (f32[104,256]{1,0:T(8,128)S(1)}, f32[104,256]{1,0:T(8,128)S(1)}, u32[]{:S(2)}, u32[]{:S(2)}) collective-permute-start(f32[104,256]{1,0:T(8,128)S(1)} %get-tuple-element.24), channel_id=1, source_target_pairs={{8,0},{16,8},{24,16},{0,24},{9,1},{17,9},{25,17},{1,25},{10,2},{18... | collective-permute-start | bytes 319496 | tf_op jit(solution)/shard_map/ppermute | solution.py:485
  16.7 8.2 %collective-permute-start.5 = (bf16[5,144,128]{2,1,0:T(8,128)(2,1)S(1)}, bf16[5,144,128]{2,1,0:T(8,128)(2,1)S(1)}, u32[]{:S(2)}, u32[]{:S(2)}) collective-permute-start(bf16[5,144,128]{2,1,0:T(8,128)(2,1)S(1)} %get-tuple-element.32), channel_id=1, source_target_pairs={{8,0},{16,8},{24,16},{0,24},{9,1},{17,9},{25,17},{1,25},{10,2},{18... | collective-permute-start | bytes 552968 | tf_op jit(solution)/shard_map/ppermute | solution.py:485
  19.2 8.4 %collective-permute-start.4 = (bf16[5,144,128]{2,1,0:T(8,128)(2,1)S(1)}, bf16[5,144,128]{2,1,0:T(8,128)(2,1)S(1)}, u32[]{:S(2)}, u32[]{:S(2)}) collective-permute-start(bf16[5,144,128]{2,1,0:T(8,128)(2,1)S(1)} %get-tuple-element.27.order_ref), channel_id=1, source_target_pairs={{0,8},{8,16},{16,24},{24,0},{1,9},{9,17},{17,25},{25,1},{2,10},{10... | collective-permute-start | bytes 552968 | tf_op jit(solution)/shard_map/ppermute | solution.py:484
  28.0 4.0 %collective-permute-start.6 = (f32[2,144,256]{2,1,0:T(8,128)S(1)}, f32[2,144,256]{2,1,0:T(8,128)S(1)}, u32[]{:S(2)}, u32[]{:S(2)}) collective-permute-start(f32[2,144,256]{2,1,0:T(8,128)S(1)} %shard_map.109.mine_ref), channel_id=1, source_target_pairs={{0,1},{1,0},{2,3},{3,2},{4,5},{5,4},{6,7},{7,6},{8,9},{9,8},{10,11... | collective-permute-start | bytes 884744 | tf_op jit(solution)/shard_map/ppermute | solution.py:603
  28.1 18.8 %collective-permute-start.11 = (f32[200,256]{1,0:T(8,128)S(1)}, f32[200,256]{1,0:T(8,128)S(1)}, u32[]{:S(2)}, u32[]{:S(2)}) collective-permute-start(f32[200,256]{1,0:T(8,128)S(1)} %get-tuple-element.39), channel_id=1, source_target_pairs={{0,2},{2,4},{4,6},{6,0},{1,3},{3,5},{5,7},{7,1},{8,10},{10,12},{12... | collective-permute-start | bytes 614408 | tf_op jit(solution)/shard_map/ppermute | solution.py:484
  29.9 17.0 %collective-permute-start.12 = (f32[200,256]{1,0:T(8,128)S(1)}, f32[200,256]{1,0:T(8,128)S(1)}, u32[]{:S(2)}, u32[]{:S(2)}) collective-permute-start(f32[200,256]{1,0:T(8,128)S(1)} %get-tuple-element.40), channel_id=1, source_target_pairs={{2,0},{4,2},{6,4},{0,6},{3,1},{5,3},{7,5},{1,7},{10,8},{12,10},{14... | collective-permute-start | bytes 614408 | tf_op jit(solution)/shard_map/ppermute | solution.py:485
  32.0 11.4 %collective-permute-start.7 = (f32[2,24,256]{2,1,0:T(8,128)S(1)}, f32[2,24,256]{2,1,0:T(8,128)S(1)}, u32[]{:S(2)}, u32[]{:S(2)}) collective-permute-start(f32[2,24,256]{2,1,0:T(8,128)S(1)} %get-tuple-element.34), channel_id=1, source_target_pairs={{0,2},{2,4},{4,6},{6,0},{1,3},{3,5},{5,7},{7,1},{8,10},{10,12},{12... | collective-permute-start | bytes 147464 | tf_op jit(solution)/shard_map/ppermute | solution.py:484
  32.1 11.4 %collective-permute-start.8 = (f32[2,24,256]{2,1,0:T(8,128)S(1)}, f32[2,24,256]{2,1,0:T(8,128)S(1)}, u32[]{:S(2)}, u32[]{:S(2)}) collective-permute-start(f32[2,24,256]{2,1,0:T(8,128)S(1)} %get-tuple-element.35), channel_id=1, source_target_pairs={{2,0},{4,2},{6,4},{0,6},{3,1},{5,3},{7,5},{1,7},{10,8},{12,10},{14... | collective-permute-start | bytes 147464 | tf_op jit(solution)/shard_map/ppermute | solution.py:485
  43.9 5.0 %collective-permute-start.9 = (f32[48,256]{1,0:T(8,128)S(1)}, f32[48,256]{1,0:T(8,128)S(1)}, u32[]{:S(2)}, u32[]{:S(2)}) collective-permute-start(f32[48,256]{1,0:T(8,128)S(1)} %get-tuple-element.37), channel_id=1, source_target_pairs={{0,8},{8,16},{16,24},{24,0},{1,9},{9,17},{17,25},{25,1},{2,10},{10... | collective-permute-start | bytes 147464 | tf_op jit(solution)/shard_map/ppermute | solution.py:484
  45.4 4.1 %collective-permute-start.10 = (f32[48,256]{1,0:T(8,128)S(1)}, f32[48,256]{1,0:T(8,128)S(1)}, u32[]{:S(2)}, u32[]{:S(2)}) collective-permute-start(f32[48,256]{1,0:T(8,128)S(1)} %get-tuple-element.38), channel_id=1, source_target_pairs={{8,0},{16,8},{24,16},{0,24},{9,1},{17,9},{25,17},{1,25},{10,2},{18... | collective-permute-start | bytes 147464 | tf_op jit(solution)/shard_map/ppermute | solution.py:485

commit v5 on v4

--- a/solution.py
+++ b/solution.py
@@ -38,8 +38,8 @@
 
 
 def dot3(left, right, dims=(1, 0)):
-    left_high, left_low = split(left)
-    right_high, right_low = split(right)
+    left_high, left_low = left if isinstance(left, tuple) else split(left)
+    right_high, right_low = right if isinstance(right, tuple) else split(right)
     total = dot(left_high, right_low, dims) + dot(left_low, right_high, dims)
     return total + dot(left_high, right_high, dims)
 
@@ -70,8 +70,41 @@
     return jnp.where(jnp.abs(offset) <= HB, value, 0.0)
 
 
-def pack_kernel(perts_ref, above_ref, below_ref, east_ref, west_ref):
+def tables_kernel(turned, width_ref, lon_ref, lat_ref):
+    if turned:
+        height, ext = lat_ref.shape[1], lat_ref.shape[2] // 3
+        width = lon_ref.shape[3] // 2
+    else:
+        ext, height = lat_ref.shape[1], lat_ref.shape[2] // 3
+        width = lon_ref.shape[3] - LANES
+    for level in range(2):
+        spread = width_ref[level].astype(F32)
+        high, low = split(taps(iota((width, width), 0) - iota((width, width), 1), spread))
+        shape = (LANES, width) if turned else (width, LANES)
+        lane = iota(shape, 1 - turned)
+        edge = taps(iota(shape, int(turned)) - packed_column(lane, level, width), spread)
+        for t in range(MEMBERS):
+            part_high, part_low = split(jnp.where(packed_member(lane) == t, edge, 0.0))
+            lon_ref[level, t, :width, :width] = high
+            lon_ref[level, t, width:, width:] = part_low
+            if turned:
+                lon_ref[level, t, :width, width:] = low
+                lon_ref[level, t, width:, :width] = part_high
+            else:
+                lon_ref[level, t, width:, :width] = low
+                lon_ref[level, t, :width, width:] = part_high
+        shape = (height, ext) if turned else (ext, height)
+        framed = row_of(iota(shape, int(turned)), height)
+        high, low = split(taps(framed - iota(shape, 1 - turned), spread))
+        size = shape[1]
+        lat_ref[level, :, :size] = high
+        lat_ref[level, :, size : 2 * size] = low
+        lat_ref[level, :, 2 * size :] = high
+
+
+def pack_kernel(perts_ref, even_ref, odd_ref, east_ref, west_ref, above_ref, below_ref):
     rows = east_ref.shape[1]
+    turned = lax.axis_index("gy") % 2 == 1
     width = perts_ref.shape[2]
     lane = iota((rows, LANES), 1)
     east = jnp.zeros((rows, LANES), F32)
@@ -79,9 +112,12 @@
     for k in range(GROUP):
         t, level = k // 2, k % 2
         own = perts_ref[k]
-        whole = jnp.concatenate(
-            [own.astype(F32), above_ref[k].astype(F32), below_ref[k].astype(F32)], 0
-        )
+        even, odd = even_ref[k].astype(F32), odd_ref[k].astype(F32)
+        above = jnp.where(turned, even, odd)
+        below = jnp.where(turned, odd, even)
+        above_ref[k] = above.astype(BF16)
+        below_ref[k] = below.astype(BF16)
+        whole = jnp.concatenate([own.astype(F32), above, below], 0)
         last = whole[:, width - LANES :]
         first = whole[:, :LANES]
         slot = level * (LANES // 2) + t * HB
@@ -95,32 +131,13 @@
 
 
 def local_kernel(
-    width_ref, alpha_ref, perts_ref, token_ref, sum_ref, rows_ref, cols_ref, lon_ref, lat_ref, stack_ref
+    alpha_ref, perts_ref, lon_ref, lat_ref, token_ref, sum_ref, rows_ref, cols_ref, stack_ref
 ):
     height, width = alpha_ref.shape[1], alpha_ref.shape[2]
-    ext = height + 2 * HB
 
     @pl.when(pl.program_id(0) == 0)
     def _():
         sum_ref[...] = jnp.zeros_like(sum_ref)
-        for level in range(2):
-            spread = width_ref[level].astype(F32)
-            source = iota((width, width), 0)
-            high, low = split(taps(source - iota((width, width), 1), spread))
-            source = iota((width, LANES), 0)
-            lane = iota((width, LANES), 1)
-            edge = taps(source - packed_column(lane, level, width), spread)
-            for t in range(MEMBERS):
-                part_high, part_low = split(jnp.where(packed_member(lane) == t, edge, 0.0))
-                lon_ref[level, t, :width, :width] = high
-                lon_ref[level, t, width:, :width] = low
-                lon_ref[level, t, :width, width:] = part_high
-                lon_ref[level, t, width:, width:] = part_low
-            target = row_of(iota((ext, height), 0), height)
-            high, low = split(taps(target - iota((ext, height), 1), spread))
-            lat_ref[level, :, :height] = high
-            lat_ref[level, :, height : 2 * height] = low
-            lat_ref[level, :, 2 * height :] = high
 
     def put(level, start, value):
         high, low = split(value)
@@ -176,17 +193,31 @@
         previous_ref[...] = jnp.zeros_like(previous_ref)
 
 
-def rows_kernel(perts_ref, next_ref, previous_ref, sems):
+def rows_kernel(perts_ref, even_ref, odd_ref, sems):
     height = perts_ref.shape[1]
-    copies = [
-        pltpu.make_async_copy(perts_ref.at[:, height - HB :], next_ref, sems.at[0]),
-        pltpu.make_async_copy(perts_ref.at[:, :HB], previous_ref, sems.at[1]),
-    ]
-    for copy in copies:
-        copy.start()
-    for copy in copies:
-        copy.wait()
-    seal("gy", next_ref, previous_ref)
+    place = lax.axis_index("gy")
+
+    def fill(even, odd):
+        copies = [
+            pltpu.make_async_copy(perts_ref.at[:, even : even + HB], even_ref, sems.at[0]),
+            pltpu.make_async_copy(perts_ref.at[:, odd : odd + HB], odd_ref, sems.at[1]),
+        ]
+        for copy in copies:
+            copy.start()
+        for copy in copies:
+            copy.wait()
+
+    @pl.when(place % 2 == 0)
+    def _():
+        fill(height - HB, 0)
+
+    @pl.when(place % 2 == 1)
+    def _():
+        fill(0, height - HB)
+
+    @pl.when((place == 0) | (place == lax.axis_size("gy") - 1))
+    def _():
+        odd_ref[...] = jnp.zeros_like(odd_ref)
 
 
 def table(index, weight):
@@ -288,13 +319,11 @@
         west_ref[part] = dot(pick_west, high, (1, 1)) + dot(pick_west, low, (1, 1))
 
 
-def fine_kernel(
+def fine_maps_kernel(
+    height,
+    width,
     lon_total,
     stack_ref,
-    strip_west_ref,
-    strip_east_ref,
-    target_ref,
-    weight_ref,
     lat_index_ref,
     lat_share_ref,
     lon_index_ref,
@@ -303,17 +332,20 @@
     east_ref,
     above_ref,
     below_ref,
-    inc_ref,
-    own_ref,
-    edge_ref,
-    wide_ref,
-    miss_ref,
+    part_ref,
+    beyond_ref,
+    lat_map_ref,
+    strip_map_ref,
+    side_map_ref,
+    lat_back_ref,
+    back_ref,
+    side_back_ref,
+    side_target_ref,
+    side_weight_ref,
 ):
-    ext, width = own_ref.shape[1], own_ref.shape[2]
-    height = ext - 2 * HB
-    rows, cols = target_ref.shape[1], target_ref.shape[2]
-    lanes = stack_ref.shape[2]
-    span = rows + LANES
+    ext = height + 2 * HB
+    span, cols = part_ref.shape[1], part_ref.shape[2]
+    tall, lanes = stack_ref.shape[1], stack_ref.shape[2]
     lane = iota((8, LANES), 1)
     first = iota((8, LANES), 0) == 0
 
@@ -328,6 +360,12 @@
         low = pltpu.roll(low, SKIRT, 1)
         high = pltpu.roll(high, SKIRT, 1)
         return jnp.where(spot < SKIRT, low, jnp.where(spot < 2 * SKIRT, high, 0.0))
+
+    def keep(ref, value):
+        high, low = split(value)
+        ref[0] = high
+        ref[1] = low
+        return high, low
 
     lat_side = side(above_ref[8 * SKIRT :, :LANES], below_ref[8 * SKIRT :, :LANES])
     lat = jnp.concatenate([table(lat_index_ref[...], lat_share_ref[...]), lat_side], 1)
@@ -348,90 +386,107 @@
     lon_cell_up, lon_share_up = upright[:, 0:1].astype(jnp.int32), upright[:, 1:2]
     beside = slice(cols, cols + 2 * SKIRT)
 
-    tall = stack_ref.shape[1]
-    lat_map = interpolate(
-        stacked_cell(iota((span, tall), 1), height, ext), lat_cell_up, lat_share_up
+    lat_map = keep(
+        lat_map_ref,
+        interpolate(stacked_cell(iota((span, tall), 1), height, ext), lat_cell_up, lat_share_up),
     )
     broad = lanes + LANES
     lon_map = interpolate(
         stacked_cell(iota((broad, cols), 0), width, lanes), lon_cell[:, :cols], lon_share[:, :cols]
     )
+    keep(strip_map_ref, lon_map[lanes:])
+    lon_map = split(lon_map[:lanes])
     side_map = interpolate(
         stacked_cell(iota((2 * SKIRT, broad), 1), width, lanes),
         lon_cell_up[beside],
         lon_share_up[beside],
     )
-    lat_back = interpolate(row_of(iota((ext, span), 0), height), lat_cell, lat_share)
-    lat_high, lat_low = split(lat_map)
-    wide_ref[:, lanes:] = jnp.zeros((span, LANES), F32)
-    miss_ref[rows + 2 * SKIRT :] = jnp.zeros((span - rows - 2 * SKIRT, cols), F32)
-
-    for level in range(2):
-        wide_ref[:, :lanes] = dot3(lat_map, stack_ref[level])
+    keep(side_map_ref, side_map[:, lanes:])
+    side_map = split(side_map[:, :lanes])
+    keep(lat_back_ref, interpolate(row_of(iota((ext, span), 0), height), lat_cell, lat_share))
+    for level in range(2):
+        wide = split(dot3(lat_map, stack_ref[level]))
+        part_ref[level] = dot3(wide, lon_map)
+        beyond_ref[level] = dot3(side_map, wide, (1, 1))
+        lane_wide = iota((1, width + LANES), 1)
+        column = jnp.where(
+            lane_wide < width, lane_wide, packed_column(lane_wide - width, level, width)
+        )
+        keep(back_ref.at[level], interpolate(column, lon_cell_up[:cols], lon_share_up[:cols]))
+        keep(side_back_ref.at[level], interpolate(column, lon_cell_up[beside], lon_share_up[beside]))
+        for array, out_ref in enumerate((side_target_ref, side_weight_ref)):
+            start = (2 * array + level) * SKIRT
+            for number, ref in enumerate((west_ref, east_ref)):
+                tile = slice(number * LANES, (number + 1) * LANES)
+                rows = slice(4 * SKIRT + start, 5 * SKIRT + start)
+                at = slice(number * SKIRT, (number + 1) * SKIRT)
+                out_ref[level, at, : span - LANES] = ref[start : start + SKIRT]
+                out_ref[level, at, span - LANES :] = corner(above_ref[rows, tile], below_ref[rows, tile])
+
+
+def fine_kernel(
+    strip_west_ref,
+    strip_east_ref,
+    target_ref,
+    weight_ref,
+    above_ref,
+    below_ref,
+    part_ref,
+    beyond_ref,
+    lat_map_ref,
+    strip_map_ref,
+    side_map_ref,
+    lat_back_ref,
+    back_ref,
+    side_back_ref,
+    side_target_ref,
+    side_weight_ref,
+    inc_ref,
+    own_ref,
+    edge_ref,
+    wide_ref,
+    miss_ref,
+):
+    width = own_ref.shape[2]
+    rows, cols = target_ref.shape[1], target_ref.shape[2]
+    span = part_ref.shape[1]
+    wide_ref[...] = jnp.zeros_like(wide_ref)
+    blank = jnp.zeros((span - rows - 2 * SKIRT, cols), F32)
+    miss_ref[0, rows + 2 * SKIRT :] = blank
+    miss_ref[1, rows + 2 * SKIRT :] = blank
+
+    def kept(ref):
+        return ref[0], ref[1]
+
+    for level in range(2):
         part = slice(level * STRIP, (level + 1) * STRIP)
         strips = jnp.concatenate([strip_west_ref[part], strip_east_ref[part]], 0)
-        wide_ref[:, lanes : lanes + 2 * STRIP] = dot3(lat_map, strips, (1, 1))
-        increment = dot3(wide_ref[...], lon_map)
+        wide_ref[level, :, : 2 * STRIP] = dot3(kept(lat_map_ref), strips, (1, 1))
+        wide = split(wide_ref[level])
+        increment = part_ref[level] + dot3(wide, kept(strip_map_ref))
         inc_ref[level] = increment[:rows]
-        miss_ref[:rows] = weight_ref[level] * (increment[:rows] - target_ref[level])
+        miss_ref[level, :rows] = weight_ref[level] * (increment[:rows] - target_ref[level])
         target_rows = slice(level * SKIRT, (level + 1) * SKIRT)
         weight_rows = slice((2 + level) * SKIRT, (3 + level) * SKIRT)
         for number, ref in enumerate((above_ref, below_ref)):
             start = rows + number * SKIRT
-            part = increment[start : start + SKIRT] - ref[target_rows]
-            miss_ref[start : start + SKIRT] = ref[weight_rows] * part
-        beyond = dot3(side_map, wide_ref[...], (1, 1))
-        pieces = []
-        for number, ref in enumerate((west_ref, east_ref)):
-            tile = slice(number * LANES, (number + 1) * LANES)
-
-            def extended(at):
-                start = 4 * SKIRT + at.start
-                stop = 4 * SKIRT + at.stop
-                last = corner(above_ref[start:stop, tile], below_ref[start:stop, tile])
-                return jnp.concatenate([ref[at], last], 1)
-
-            part = beyond[number * SKIRT : (number + 1) * SKIRT]
-            pieces.append(extended(weight_rows) * (part - extended(target_rows)))
-        beyond = jnp.concatenate(pieces, 0)
-        lane_wide = iota((1, width + LANES), 1)
-        column = jnp.where(
-            lane_wide < width, lane_wide, packed_column(lane_wide - width, level, width)
-        )
-        back = interpolate(column, lon_cell_up[:cols], lon_share_up[:cols])
-        side_back = interpolate(column, lon_cell_up[beside], lon_share_up[beside])
-        by_lon = dot3(miss_ref[...], back) + dot3(beyond, side_back, (0, 0))
-        residual = dot3(lat_back, by_lon)
+            difference = increment[start : start + SKIRT] - ref[target_rows]
+            miss_ref[level, start : start + SKIRT] = ref[weight_rows] * difference
+        beyond = beyond_ref[level] + dot3(kept(side_map_ref), wide, (1, 1))
+        beyond = side_weight_ref[level] * (beyond - side_target_ref[level])
+        by_lon = dot3(miss_ref[level], kept(back_ref.at[level]))
+        by_lon = by_lon + dot3(beyond, kept(side_back_ref.at[level]), (0, 0))
+        residual = dot3(kept(lat_back_ref), by_lon)
         own_ref[level] = residual[:, :width]
         edge_ref[level] = residual[:, width:]
 
 
 def gradient_kernel(
-    width_ref, alpha_ref, perts_ref, above_ref, below_ref, west_ref, east_ref, own_ref, edge_ref, out_ref,
-    lon_ref, lat_ref, stack_ref,
+    alpha_ref, perts_ref, above_ref, below_ref, west_ref, east_ref, own_ref, edge_ref, lon_ref, lat_ref,
+    out_ref, stack_ref,
 ):
     height, width = alpha_ref.shape[1], alpha_ref.shape[2]
     ext = height + 2 * HB
-
-    @pl.when(pl.program_id(0) == 0)
-    def _():
-        for level in range(2):
-            spread = width_ref[level].astype(F32)
-            source = iota((width, width), 0)
-            high, low = split(taps(source - iota((width, width), 1), spread))
-            lane = iota((LANES, width), 0)
-            edge = taps(packed_column(lane, level, width) - iota((LANES, width), 1), spread)
-            for t in range(MEMBERS):
-                part_high, part_low = split(jnp.where(packed_member(lane) == t, edge, 0.0))
-                lon_ref[level, t, :width, :width] = high
-                lon_ref[level, t, :width, width:] = low
-                lon_ref[level, t, width:, :width] = part_high
-                lon_ref[level, t, width:, width:] = part_low
-            source = row_of(iota((height, ext), 1), height)
-            high, low = split(taps(source - iota((height, ext), 0), spread))
-            lat_ref[level, :, :ext] = high
-            lat_ref[level, :, ext : 2 * ext] = low
-            lat_ref[level, :, 2 * ext :] = high
 
     half = iota((ext, LANES), 1) < LANES // 2
 
@@ -468,21 +523,21 @@
             out_ref[k] = alpha_ref[k].astype(F32) + total
 
 
-def GRAD_SCRATCH(height, width):
-    ext = height + 2 * HB
-    return [
-        pltpu.VMEM((2, MEMBERS, width + LANES, 2 * width), BF16),
-        pltpu.VMEM((2, height, 3 * ext), BF16),
-        pltpu.VMEM((GROUP, 2 * height, width + LANES), BF16),
-    ]
-
-
 def exchange(to_next, to_previous, axis):
     count = lax.axis_size(axis)
     forward = [(i, (i + 1) % count) for i in range(count)]
     backward = [(target, source) for source, target in forward]
     ahead = lax.ppermute(to_next, axis, forward)
     behind = lax.ppermute(to_previous, axis, backward)
+    return ahead, behind
+
+
+def exchange_pairs(to_even, to_odd, axis):
+    count = lax.axis_size(axis)
+    even = [(i, i ^ 1) for i in range(count)]
+    odd = [(i, min(max(i + 1 if i % 2 else i - 1, 0), count - 1)) for i in range(count)]
+    ahead = lax.ppermute(to_even, axis, even)
+    behind = lax.ppermute(to_odd, axis, odd)
     return ahead, behind
 
 
@@ -518,6 +573,7 @@
     perts = member_perts.reshape(fields, height, width)
     smem = pl.BlockSpec(memory_space=pltpu.SMEM)
     anywhere = pl.BlockSpec(memory_space=pl.ANY)
+    whole = pl.BlockSpec(memory_space=pltpu.VMEM)
     scale = width // LANES
     lanes = rounded(width + 2 * HB, LANES)
     tall = rounded(ext + 2 * STRIP, LANES)
@@ -535,14 +591,22 @@
         )
 
     edge = shaped((fields, HB, width), BF16)
-    to_next, to_previous = call(
+    to_even, to_odd = call(
         rows_kernel,
         [edge, edge],
         in_specs=[pl.BlockSpec(memory_space=pltpu.HBM)],
         out_specs=[pl.BlockSpec(memory_space=pltpu.VMEM)] * 2,
         scratch_shapes=[pltpu.SemaphoreType.DMA((2,))],
     )(perts)
-    above, below = exchange(to_next, to_previous, "gy")
+    even, odd = exchange_pairs(to_even, to_odd, "gy")
+    lon_shape, lat_shape = (2, MEMBERS, 2 * width, width + LANES), (2, ext, 3 * height)
+    lon_back_shape, lat_back_shape = (2, MEMBERS, width + LANES, 2 * width), (2, height, 3 * ext)
+    lon_table, lat_table = call(
+        functools.partial(tables_kernel, False),
+        [shaped(lon_shape, BF16), shaped(lat_shape, BF16)],
+        grant=8,
+        in_specs=[smem],
+    )(band_widths)
 
     side = shaped((4 * SKIRT + 8, fine_h))
     to_next, to_previous = call(fine_cols_kernel, [side, side])(
@@ -551,18 +615,17 @@
     fine_west, fine_east = exchange(to_next, to_previous, "gx")
 
     packed = shaped((groups, ext, LANES), BF16)
-    to_next, to_previous = call(
+    to_next, to_previous, above, below = call(
         pack_kernel,
-        [packed, packed],
+        [packed, packed, edge, edge],
         grant=8,
         grid=(groups,),
         in_specs=[grouped(GROUP, height, width)] + [grouped(GROUP, HB, width)] * 2,
-        out_specs=[grouped(1, ext, LANES)] * 2,
-    )(perts, above, below)
+        out_specs=[grouped(1, ext, LANES)] * 2 + [grouped(GROUP, HB, width)] * 2,
+    )(perts, even, odd)
     west, east = exchange(to_next, to_previous, "gx")
 
     strip = shaped((8 * SKIRT + 8, fine_w))
-    whole = pl.BlockSpec(memory_space=pltpu.VMEM)
     to_next, to_previous, token = call(
         fine_rows_kernel, [strip, strip, shaped((8, LANES))], in_specs=[whole] * 6 + [anywhere]
     )(innovation, obs_weight, lat_index, lat_weight, fine_west, fine_east, to_next)
@@ -579,9 +642,10 @@
         grant=16,
         grid=(groups,),
         in_specs=[
-            smem,
             grouped(GROUP, height, width),
             grouped(GROUP, height, width),
+            whole,
+            whole,
             anywhere,
         ],
         out_specs=[
@@ -590,11 +654,9 @@
             grouped(1, 2, ext, LANES),
         ],
         scratch_shapes=[
-            pltpu.VMEM((2, MEMBERS, 2 * width, width + LANES), BF16),
-            pltpu.VMEM((2, ext, 3 * height), BF16),
             pltpu.VMEM((2, 3 * height, MEMBERS * width + LANES), BF16),
         ],
-    )(band_widths, alpha, perts, token)
+    )(alpha, perts, lon_table, lat_table, token)
 
     framed = call(
         frame_kernel, shaped((2, ext, width + LANES)), in_specs=[whole] * 7
@@ -605,6 +667,12 @@
     framed, to_next, to_previous = call(
         total_kernel, [shaped((2, ext, lanes)), strip, strip]
     )(framed, other)
+    lon_back, lat_back = call(
+        functools.partial(tables_kernel, True),
+        [shaped(lon_back_shape, BF16), shaped(lat_back_shape, BF16)],
+        grant=8,
+        in_specs=[smem],
+    )(band_widths)
     north, south = exchange(to_next, to_previous, "gy")
     strip = shaped((2 * STRIP, tall))
     stack, to_next, to_previous = call(
@@ -613,22 +681,26 @@
     strip_west, strip_east = exchange(to_next, to_previous, "gx")
 
     lon_total = width * lax.axis_size("gx")
-    everything = [pl.BlockSpec(memory_space=pltpu.VMEM)] * 13
-    increment, own, edge = call(
-        functools.partial(fine_kernel, lon_total),
-        [shaped((2, fine_h, fine_w)), shaped((2, ext, width)), shaped((2, ext, LANES))],
+    span = fine_h + LANES
+    pair = (2, 2 * SKIRT, span)
+    maps = call(
+        functools.partial(fine_maps_kernel, height, width, lon_total),
+        [
+            shaped((2, span, fine_w)),
+            shaped(pair),
+            shaped((2, span, tall), BF16),
+            shaped((2, LANES, fine_w), BF16),
+            shaped((2, 2 * SKIRT, LANES), BF16),
+            shaped((2, ext, span), BF16),
+            shaped((2, 2, fine_w, width + LANES), BF16),
+            shaped((2, 2, 2 * SKIRT, width + LANES), BF16),
+            shaped(pair),
+            shaped(pair),
+        ],
         grant=16,
-        in_specs=everything,
-        scratch_shapes=[
-            pltpu.VMEM((fine_h + LANES, lanes + LANES), F32),
-            pltpu.VMEM((fine_h + LANES, fine_w), F32),
-        ],
+        in_specs=[whole] * 9,
     )(
         stack,
-        strip_west,
-        strip_east,
-        innovation,
-        obs_weight,
         lat_index,
         lat_weight,
         lon_index,
@@ -638,6 +710,13 @@
         fine_above,
         fine_below,
     )
+    increment, own, edge = call(
+        fine_kernel,
+        [shaped((2, fine_h, fine_w)), shaped((2, ext, width)), shaped((2, ext, LANES))],
+        grant=16,
+        in_specs=[whole] * 16,
+        scratch_shapes=[pltpu.VMEM((2, span, LANES), F32), pltpu.VMEM((2, span, fine_w), F32)],
+    )(strip_west, strip_east, innovation, obs_weight, fine_above, fine_below, *maps)
 
     gradient = call(
         gradient_kernel,
@@ -645,7 +724,6 @@
         grant=16,
         grid=(groups,),
         in_specs=[
-            smem,
             grouped(GROUP, height, width),
             grouped(GROUP, height, width),
             grouped(GROUP, HB, width),
@@ -654,10 +732,12 @@
             grouped(1, ext, LANES),
             vmem(2, ext, width),
             vmem(2, ext, LANES),
+            whole,
+            whole,
         ],
         out_specs=grouped(GROUP, height, width),
-        scratch_shapes=GRAD_SCRATCH(height, width),
-    )(band_widths, alpha, perts, above, below, west, east, own, edge)
+        scratch_shapes=[pltpu.VMEM((GROUP, 2 * height, width + LANES), BF16)],
+    )(alpha, perts, above, below, west, east, own, edge, lon_back, lat_back)
     return increment, gradient.reshape(alpha_fields.shape)
 
 

time: 62.7 us -> 59.3 us (0.946)
  waiting for transfers between devices: 14.7 us -> 11.5 us
  starting transfers between devices: 21.4 us -> 19.9 us
  Pallas kernels: 21.6 us -> 22.9 us
    ppermute x6 -> x5, starting transfers between devices: 13.2 us -> 7.17 us  [exchange(): behind = lax.ppermute(to_previous, axis, backward)]
    ppermute x0 -> x2, starting transfers between devices: none -> 3.75 us  [the longest x1 3.1 us: exchange_pairs(): ahead = lax.ppermute(to_even, axis, even)]
    pallas_call x2 -> x5, Pallas kernels: 6.28 us -> 9.9 us  [the longest x1 3.83 us: whole_step(): call(fine_kernel, [shaped((2, fine_h, fine_w)), shaped((2, ext, width)),...]
    ppermute x6 -> x5, waiting for transfers between devices: 12.3 us -> 10.1 us  [exchange(): ahead = lax.ppermute(to_next, axis, forward)]
    pallas_call x1, Pallas kernels: 8.48 us -> 7.24 us  [whole_step(): call(gradient_kernel, shaped((fields, height, width)), grant=16, grid=(gr...]
    pallas_call x1, Pallas kernels: 5.57 us -> 4.47 us  [whole_step(): call(local_kernel, [shaped((2, height, width)), shaped((fields, 2 * HB, w...]
    ppermute x6 -> x5, waiting for transfers between devices: 2.4 us -> 1.42 us  [exchange(): behind = lax.ppermute(to_previous, axis, backward)]
    ppermute x6 -> x5, starting transfers between devices: 8.15 us -> 8.89 us  [exchange(): ahead = lax.ppermute(to_next, axis, forward)]
  transfers between devices with their start and end apart: 13 -> 13, of which waited for: 6 -> 4; matrix products, arithmetic and copies ran while one was open for 0% -> 0% of each run, Pallas kernels for 13% -> 19%
where the time goes in v5:
time: 59.3 us; the launch traced here: 59.1 us
  Pallas kernels  22.9 us (39%)
  starting transfers between devices  19.9 us (34%)
  waiting for transfers between devices  11.5 us (19%)
  local copies, waits for them, and re-layouts  3.86 us (7%)
  between operations  0.89 us (2%)
    ppermute x5, waiting for transfers between devices, exchange(): ahead = lax.ppermute(to_next, axis, forward)  10.1 us
    ppermute x5, starting transfers between devices, exchange(): ahead = lax.ppermute(to_next, axis, forward)  8.89 us
    pallas_call x1, Pallas kernels, whole_step(): call(gradient_kernel, shaped((fields, height, width)), grant=16, grid=(gr...  7.24 us
    ppermute x5, starting transfers between devices, exchange(): behind = lax.ppermute(to_previous, axis, backward)  7.17 us
    pallas_call x1, Pallas kernels, whole_step(): call(local_kernel, [shaped((2, height, width)), shaped((fields, 2 * HB, w...  4.47 us
    unnamed x24, local copies, waits for them, and re-layouts  3.86 us
    pallas_call x1, Pallas kernels, whole_step(): call(fine_kernel, [shaped((2, fine_h, fine_w)), shaped((2, ext, width)),...  3.83 us
    ppermute x1, starting transfers between devices, exchange_pairs(): ahead = lax.ppermute(to_even, axis, even)  3.1 us
  transfers between devices with their start and end apart: 13, of which 4 were waited for; matrix products, arithmetic and copies ran while one was open for 0% of the time, Pallas kernels for 19%

profile of v5, /device:TPU:0, one launch (start us, length us, event | category | flops | bytes accessed | tf_op | source)
XLA Modules:
  0.0 59.1 jit_solution(4475025768620409524)
XLA Ops:
  0.6 0.0 copy-start.9
  0.6 0.0 copy-start.11
  0.7 0.0 copy-start
  0.7 1.7 %copy-done = bf16[40,2,128,128]{3,2,1,0:T(8,128)(2,1)S(1)} copy-done((bf16[40,2,128,128]{3,2,1,0:T(8,128)(2,1)S(1)}, bf16[40,2,128,128]{3,2,1,0:T(8,128)(2,1)}, u32[]{:S(2)}) %copy-start) | copy-done | bytes 2621464
  2.4 0.1 shard_map.106
  2.5 0.0 copy-start.7
  2.6 0.0 copy-start.8
  2.6 3.1 %collective-permute-start.2 = (bf16[80,8,128]{2,1,0:T(8,128)(2,1)S(1)}, bf16[80,8,128]{2,1,0:T(8,128)(2,1)S(1)}, u32[]{:S(2)}, u32[]{:S(2)}) collective-permute-start(bf16[80,8,128]{2,1,0:T(8,128)(2,1)S(1)} %get-tuple-element.43), channel_id=1, source_target_pairs={{0,2},{2,0},{4,6},{6,4},{1,3},{3,1},{5,7},{7,5},{8,10},{10,8},{12,... | collective-permute-start | bytes 491528 | tf_op jit(solution)/shard_map/ppermute | solution.py:539
  5.7 0.7 %collective-permute-start.3 = (bf16[80,8,128]{2,1,0:T(8,128)(2,1)S(1)}, bf16[80,8,128]{2,1,0:T(8,128)(2,1)S(1)}, u32[]{:S(2)}, u32[]{:S(2)}) collective-permute-start(bf16[80,8,128]{2,1,0:T(8,128)(2,1)S(1)} %get-tuple-element.44), channel_id=1, source_target_pairs={{0,0},{2,4},{4,2},{6,6},{1,1},{3,5},{5,3},{7,7},{8,8},{10,12},{12,... | collective-permute-start | bytes 491528 | tf_op jit(solution)/shard_map/ppermute | solution.py:540
  6.4 0.0 copy-start.2
  6.4 1.0 %copy-done.2 = f32[2,256,256]{2,1,0:T(8,128)S(1)} copy-done((f32[2,256,256]{2,1,0:T(8,128)S(1)}, f32[2,256,256]{2,1,0:T(8,128)}, u32[]{:S(2)}) %copy-start.2) | copy-done | bytes 524312
  7.4 1.0 %copy-done.4 = f32[2,256,256]{2,1,0:T(8,128)S(1)} copy-done((f32[2,256,256]{2,1,0:T(8,128)S(1)}, f32[2,256,256]{2,1,0:T(8,128)}, u32[]{:S(2)}) %copy-start.4) | copy-done | bytes 524312
  8.4 0.3 shard_map.105
  8.8 0.0 copy-start.6
  8.8 1.5 %collective-permute-start = (f32[104,256]{1,0:T(8,128)S(1)}, f32[104,256]{1,0:T(8,128)S(1)}, u32[]{:S(2)}, u32[]{:S(2)}) collective-permute-start(f32[104,256]{1,0:T(8,128)S(1)} %get-tuple-element.41), channel_id=1, source_target_pairs={{0,8},{8,16},{16,24},{24,0},{1,9},{9,17},{17,25},{25,1},{2,10},{10... | collective-permute-start | bytes 319496 | tf_op jit(solution)/shard_map/ppermute | solution.py:530
  10.3 1.4 %collective-permute-start.1 = (f32[104,256]{1,0:T(8,128)S(1)}, f32[104,256]{1,0:T(8,128)S(1)}, u32[]{:S(2)}, u32[]{:S(2)}) collective-permute-start(f32[104,256]{1,0:T(8,128)S(1)} %get-tuple-element.42), channel_id=1, source_target_pairs={{8,0},{16,8},{24,16},{0,24},{9,1},{17,9},{25,17},{1,25},{10,2},{18... | collective-permute-start | bytes 319496 | tf_op jit(solution)/shard_map/ppermute | solution.py:531
  11.7 1.1 %shard_map.104 = (bf16[2,8,256,256]{3,2,1,0:T(8,128)(2,1)S(1)}, bf16[2,144,384]{2,1,0:T(8,128)(2,1)S(1)}) custom-call(s32[2]{0:T(128)S(1)} %copy-done.11), custom_call_target="tpu_custom_call" | custom-call | flops 100000000 | bytes 1000000 | tf_op jit(solution)/shard_map/pallas_call | solution.py:604
  12.8 0.0 collective-permute-done.2.even_ref
  12.9 0.0 collective-permute-done.3.odd_ref
  12.9 1.9 %shard_map.107 = (bf16[5,144,128]{2,1,0:T(8,128)(2,1)S(1)}, bf16[5,144,128]{2,1,0:T(8,128)(2,1)S(1)}, bf16[80,8,128]{2,1,0:T(8,128)(2,1)S(1)}, bf16[80,8,128]{2,1,0:T(8,128)(2,1)S(1)}) custom-call(bf16[80,128,128]{2,1,0:T(8,128)(2,1)S(1)} %bitcast.4, bf16[80,8,128]{2,1,0:T(8,128)(2,1)S(1)} %collective-permute-done.2.even_ref, ...), custom_call_target="tpu_custom_call" | custom-call | flops 100000000 | bytes 1000000 | tf_op jit(solution)/shard_map/pallas_call | solution.py:618
  14.8 1.6 %collective-permute-start.5 = (bf16[5,144,128]{2,1,0:T(8,128)(2,1)S(1)}, bf16[5,144,128]{2,1,0:T(8,128)(2,1)S(1)}, u32[]{:S(2)}, u32[]{:S(2)}) collective-permute-start(bf16[5,144,128]{2,1,0:T(8,128)(2,1)S(1)} %get-tuple-element.52), channel_id=1, source_target_pairs={{8,0},{16,8},{24,16},{0,24},{9,1},{17,9},{25,17},{1,25},{10,2},{18... | collective-permute-start | bytes 552968 | tf_op jit(solution)/shard_map/ppermute | solution.py:531
  16.4 0.5 collective-permute-start.4
  16.8 0.0 collective-permute-done.west_ref
  16.8 0.0 collective-permute-done.1.east_ref
  16.9 0.0 copy-done.7
  17.0 4.5 %shard_map.109 = (f32[2,128,128]{2,1,0:T(8,128)S(1)}, f32[80,16,128]{2,1,0:T(8,128)S(1)}, f32[5,2,144,128]{3,2,1,0:T(8,128)S(1)}) custom-call(bf16[80,128,128]{2,1,0:T(8,128)(2,1)S(1)} %bitcast.7, bf16[80,128,128]{2,1,0:T(8,128)(2,1)S(1)} %bitcast.5, bf16[2,8,256,256]{3,2,1,0:T(8,128)(2,1)S(1)} %get-tuple-element.39.lon_ref, ...), custom_call_target="tpu_custom_call" | custom-call | flops 10000000000 | bytes 1000000 | tf_op jit(solution)/shard_map/pallas_call | solution.py:634
  21.4 0.9 %collective-permute-done.5.east_ref = bf16[5,144,128]{2,1,0:T(8,128)(2,1)S(1)} collective-permute-done((bf16[5,144,128]{2,1,0:T(8,128)(2,1)S(1)}, bf16[5,144,128]{2,1,0:T(8,128)(2,1)S(1)}, u32[]{:S(2)}, u32[]{:S(2)}) %collective-permute-start.5) | collective-permute-done | bytes 184352 | tf_op jit(solution)/shard_map/ppermute | solution.py:531
  22.3 2.9 %collective-permute-done.4.west_ref = bf16[5,144,128]{2,1,0:T(8,128)(2,1)S(1)} collective-permute-done((bf16[5,144,128]{2,1,0:T(8,128)(2,1)S(1)}, bf16[5,144,128]{2,1,0:T(8,128)(2,1)S(1)}, u32[]{:S(2)}, u32[]{:S(2)}) %collective-permute-start.4) | collective-permute-done | bytes 184352 | tf_op jit(solution)/shard_map/ppermute | solution.py:530
  25.3 0.4 shard_map.110.mine_ref
  25.6 0.1 collective-permute-start.6
  25.7 4.2 %collective-permute-start.11 = (f32[200,256]{1,0:T(8,128)S(1)}, f32[200,256]{1,0:T(8,128)S(1)}, u32[]{:S(2)}, u32[]{:S(2)}) collective-permute-start(f32[200,256]{1,0:T(8,128)S(1)} %get-tuple-element.58), channel_id=1, source_target_pairs={{0,2},{2,4},{4,6},{6,0},{1,3},{3,5},{5,7},{7,1},{8,10},{10,12},{12... | collective-permute-start | bytes 614408 | tf_op jit(solution)/shard_map/ppermute | solution.py:530
  29.9 0.0 collective-permute-start.12
  29.9 0.0 collective-permute-done.6.other_ref
  30.0 2.1 %collective-permute-start.7 = (f32[2,24,256]{2,1,0:T(8,128)S(1)}, f32[2,24,256]{2,1,0:T(8,128)S(1)}, u32[]{:S(2)}, u32[]{:S(2)}) collective-permute-start(f32[2,24,256]{2,1,0:T(8,128)S(1)} %get-tuple-element.54), channel_id=1, source_target_pairs={{0,2},{2,4},{4,6},{6,0},{1,3},{3,5},{5,7},{7,1},{8,10},{10,12},{12... | collective-permute-start | bytes 147464 | tf_op jit(solution)/shard_map/ppermute | solution.py:530
  32.0 1.8 %collective-permute-start.8 = (f32[2,24,256]{2,1,0:T(8,128)S(1)}, f32[2,24,256]{2,1,0:T(8,128)S(1)}, u32[]{:S(2)}, u32[]{:S(2)}) collective-permute-start(f32[2,24,256]{2,1,0:T(8,128)S(1)} %get-tuple-element.55), channel_id=1, source_target_pairs={{2,0},{4,2},{6,4},{0,6},{3,1},{5,3},{7,5},{1,7},{10,8},{12,10},{14... | collective-permute-start | bytes 147464 | tf_op jit(solution)/shard_map/ppermute | solution.py:531
  33.8 7.2 %collective-permute-done.7.above_ref = f32[2,24,256]{2,1,0:T(8,128)S(1)} collective-permute-done((f32[2,24,256]{2,1,0:T(8,128)S(1)}, f32[2,24,256]{2,1,0:T(8,128)S(1)}, u32[]{:S(2)}, u32[]{:S(2)}) %collective-permute-start.7) | collective-permute-done | bytes 49184 | tf_op jit(solution)/shard_map/ppermute | solution.py:530
  41.0 0.5 collective-permute-done.8.below_ref
  41.5 0.4 shard_map.112
  41.9 0.6 %collective-permute-start.9 = (f32[48,256]{1,0:T(8,128)S(1)}, f32[48,256]{1,0:T(8,128)S(1)}, u32[]{:S(2)}, u32[]{:S(2)}) collective-permute-start(f32[48,256]{1,0:T(8,128)S(1)} %get-tuple-element.56), channel_id=1, source_target_pairs={{0,8},{8,16},{16,24},{24,0},{1,9},{9,17},{17,25},{25,1},{2,10},{10... | collective-permute-start | bytes 147464 | tf_op jit(solution)/shard_map/ppermute | solution.py:530
  42.5 2.3 %collective-permute-start.10 = (f32[48,256]{1,0:T(8,128)S(1)}, f32[48,256]{1,0:T(8,128)S(1)}, u32[]{:S(2)}, u32[]{:S(2)}) collective-permute-start(f32[48,256]{1,0:T(8,128)S(1)} %get-tuple-element.57), channel_id=1, source_target_pairs={{8,0},{16,8},{24,16},{0,24},{9,1},{17,9},{25,17},{1,25},{10,2},{18... | collective-permute-start | bytes 147464 | tf_op jit(solution)/shard_map/ppermute | solution.py:531
  44.9 1.2 %shard_map.115 = (bf16[2,8,256,256]{3,2,1,0:T(8,128)(2,1)S(1)}, bf16[2,128,432]{2,1,0:T(8,128)(2,1)S(1)}) custom-call(s32[2]{0:T(128)S(1)} %copy-done.11), custom_call_target="tpu_custom_call" | custom-call | flops 100000000 | bytes 1000000 | tf_op jit(solution)/shard_map/pallas_call | solution.py:670
  46.1 0.0 collective-permute-done.11.above_ref
  46.1 0.0 collective-permute-done.12.below_ref
  46.1 1.9 %shard_map.113 = (f32[2,384,256]{2,1,0:T(8,128)S(1)}, f32[2,48,384]{2,1,0:T(8,128)S(1)}, bf16[2,384,256]{2,1,0:T(8,128)(2,1)S(1)}, bf16[2,128,256]{2,1,0:T(8,128...) custom-call(f32[2,256,256]{2,1,0:T(8,128)S(1)} %get-tuple-element.60, ...), custom_call_target="tpu_custom_call" | custom-call | flops 100000000 | bytes 1000000 | tf_op jit(solution)/shard_map/pallas_call | solution.py:686
  48.0 0.0 collective-permute-done.9.strip_west_ref
  48.0 0.0 collective-permute-done.10.strip_east_ref
  48.0 3.8 %shard_map.114 = (f32[2,256,256]{2,1,0:T(8,128)}, f32[2,144,128]{2,1,0:T(8,128)S(1)}, f32[2,144,128]{2,1,0:T(8,128)S(1)}) custom-call(f32[48,256]{1,0:T(8,128)S(1)} %collective-permute-done.9.strip_west_ref, f32[48,256]{1,0:T(8,128)S(1)} %collective-permute-done.10.strip_east_ref, f32[2,256,256]{2,1,0:T(8,128)S(1)} %copy-done.3, ...), custom_call_target="tpu_custom_call" | custom-call | flops 100000000 | bytes 1000000 | tf_op jit(solution)/shard_map/pallas_call | solution.py:713
  51.8 7.2 %shard_map.116 = f32[80,128,128]{2,1,0:T(8,128)} custom-call(bf16[80,128,128]{2,1,0:T(8,128)(2,1)S(1)} %bitcast.8, bf16[80,128,128]{2,1,0:T(8,128)(2,1)S(1)} %bitcast.6, bf16[80,8,128]{2,1,0:T(8,128)(2,1)S(1)} %get-tuple-element.50.above_ref, bf16[80,8,128]{2,1,0:T(8,128)(2,1)S(1)} %get-tuple-element.51.below_ref, ...), custom_call_target="tpu_custom_call" | custom-call | flops 100000000 | bytes 1000000 | tf_op jit(solution)/shard_map/pallas_call | solution.py:721
  (15 shorter events, 0.1 us)
Async XLA Ops:
  0.6 5.7 %copy-start.9 = (s32[256]{0:T(256)S(1)}, s32[256]{0:T(256)}, u32[]{:S(2)}) copy-start(s32[256]{0:T(256)} %lon_index_ref.1) | copy-start | bytes 3076
  0.6 11.1 %copy-start.11 = (s32[2]{0:T(128)S(1)}, s32[2]{0:T(128)}, u32[]{:S(2)}) copy-start(s32[2]{0:T(128)} %width_ref.3) | copy-start | bytes 28
  0.7 1.8 %copy-start = (bf16[40,2,128,128]{3,2,1,0:T(8,128)(2,1)S(1)}, bf16[40,2,128,128]{3,2,1,0:T(8,128)(2,1)}, u32[]{:S(2)}) copy-start(bf16[40,2,128,128]{3,2,1,0:T(8,128)(2,1)} %param.10) | copy-start | bytes 7864324
  2.4 3.9 %copy-start.10 = (f32[256]{0:T(256)S(1)}, f32[256]{0:T(256)}, u32[]{:S(2)}) copy-start(f32[256]{0:T(256)} %lon_share_ref.1) | copy-start | bytes 3076
  2.4 10.5 %copy-start.1 = (bf16[40,2,128,128]{3,2,1,0:T(8,128)(2,1)S(1)}, bf16[40,2,128,128]{3,2,1,0:T(8,128)(2,1)}, u32[]{:S(2)}) copy-start(bf16[40,2,128,128]{3,2,1,0:T(8,128)(2,1)} %param.10) | copy-start | bytes 7864324
  2.5 14.3 %copy-start.7 = (s32[256]{0:T(256)S(1)}, s32[256]{0:T(256)}, u32[]{:S(2)}) copy-start(s32[256]{0:T(256)} %lat_index_ref.1) | copy-start | bytes 3076
  2.6 14.3 %copy-start.8 = (f32[256]{0:T(256)S(1)}, f32[256]{0:T(256)}, u32[]{:S(2)}) copy-start(f32[256]{0:T(256)} %lat_share_ref.1) | copy-start | bytes 3076
  2.6 10.3 %collective-permute-start.2 = (bf16[80,8,128]{2,1,0:T(8,128)(2,1)S(1)}, bf16[80,8,128]{2,1,0:T(8,128)(2,1)S(1)}, u32[]{:S(2)}, u32[]{:S(2)}) collective-permute-start(bf16[80,8,128]{2,1,0:T(8,128)(2,1)S(1)} %get-tuple-element.43), channel_id=1, source_target_pairs={{0,2},{2,0},{4,6},{6,4},{1,3},{3,1},{5,7},{7,5},{8,10},{10,8},{12,... | collective-permute-start | bytes 491528 | tf_op jit(solution)/shard_map/ppermute | solution.py:539
  5.7 7.2 %collective-permute-start.3 = (bf16[80,8,128]{2,1,0:T(8,128)(2,1)S(1)}, bf16[80,8,128]{2,1,0:T(8,128)(2,1)S(1)}, u32[]{:S(2)}, u32[]{:S(2)}) collective-permute-start(bf16[80,8,128]{2,1,0:T(8,128)(2,1)S(1)} %get-tuple-element.44), channel_id=1, source_target_pairs={{0,0},{2,4},{4,2},{6,6},{1,1},{3,5},{5,3},{7,7},{8,8},{10,12},{12,... | collective-permute-start | bytes 491528 | tf_op jit(solution)/shard_map/ppermute | solution.py:540
  6.4 1.0 %copy-start.2 = (f32[2,256,256]{2,1,0:T(8,128)S(1)}, f32[2,256,256]{2,1,0:T(8,128)}, u32[]{:S(2)}) copy-start(f32[2,256,256]{2,1,0:T(8,128)} %target_ref.5) | copy-start | bytes 1572868
  7.4 1.0 %copy-start.4 = (f32[2,256,256]{2,1,0:T(8,128)S(1)}, f32[2,256,256]{2,1,0:T(8,128)}, u32[]{:S(2)}) copy-start(f32[2,256,256]{2,1,0:T(8,128)} %weight_ref.5) | copy-start | bytes 1572868
  8.4 8.4 %copy-start.3 = (f32[2,256,256]{2,1,0:T(8,128)S(1)}, f32[2,256,256]{2,1,0:T(8,128)}, u32[]{:S(2)}) copy-start(f32[2,256,256]{2,1,0:T(8,128)} %target_ref.5) | copy-start | bytes 1572868
  8.4 8.4 %copy-start.5 = (f32[2,256,256]{2,1,0:T(8,128)S(1)}, f32[2,256,256]{2,1,0:T(8,128)}, u32[]{:S(2)}) copy-start(f32[2,256,256]{2,1,0:T(8,128)} %weight_ref.5) | copy-start | bytes 1572868
  8.8 8.2 %copy-start.6 = (bf16[40,2,128,128]{3,2,1,0:T(8,128)(2,1)S(1)}, bf16[40,2,128,128]{3,2,1,0:T(8,128)(2,1)}, u32[]{:S(2)}) copy-start(bf16[40,2,128,128]{3,2,1,0:T(8,128)(2,1)} %param.9) | copy-start | bytes 7864324
  8.8 8.1 %collective-permute-start = (f32[104,256]{1,0:T(8,128)S(1)}, f32[104,256]{1,0:T(8,128)S(1)}, u32[]{:S(2)}, u32[]{:S(2)}) collective-permute-start(f32[104,256]{1,0:T(8,128)S(1)} %get-tuple-element.41), channel_id=1, source_target_pairs={{0,8},{8,16},{16,24},{24,0},{1,9},{9,17},{17,25},{25,1},{2,10},{10... | collective-permute-start | bytes 319496 | tf_op jit(solution)/shard_map/ppermute | solution.py:530
  10.3 6.5 %collective-permute-start.1 = (f32[104,256]{1,0:T(8,128)S(1)}, f32[104,256]{1,0:T(8,128)S(1)}, u32[]{:S(2)}, u32[]{:S(2)}) collective-permute-start(f32[104,256]{1,0:T(8,128)S(1)} %get-tuple-element.42), channel_id=1, source_target_pairs={{8,0},{16,8},{24,16},{0,24},{9,1},{17,9},{25,17},{1,25},{10,2},{18... | collective-permute-start | bytes 319496 | tf_op jit(solution)/shard_map/ppermute | solution.py:531
  14.8 7.6 %collective-permute-start.5 = (bf16[5,144,128]{2,1,0:T(8,128)(2,1)S(1)}, bf16[5,144,128]{2,1,0:T(8,128)(2,1)S(1)}, u32[]{:S(2)}, u32[]{:S(2)}) collective-permute-start(bf16[5,144,128]{2,1,0:T(8,128)(2,1)S(1)} %get-tuple-element.52), channel_id=1, source_target_pairs={{8,0},{16,8},{24,16},{0,24},{9,1},{17,9},{25,17},{1,25},{10,2},{18... | collective-permute-start | bytes 552968 | tf_op jit(solution)/shard_map/ppermute | solution.py:531
  16.4 8.9 %collective-permute-start.4 = (bf16[5,144,128]{2,1,0:T(8,128)(2,1)S(1)}, bf16[5,144,128]{2,1,0:T(8,128)(2,1)S(1)}, u32[]{:S(2)}, u32[]{:S(2)}) collective-permute-start(bf16[5,144,128]{2,1,0:T(8,128)(2,1)S(1)} %get-tuple-element.45.order_ref), channel_id=1, source_target_pairs={{0,8},{8,16},{16,24},{24,0},{1,9},{9,17},{17,25},{25,1},{2,10},{10... | collective-permute-start | bytes 552968 | tf_op jit(solution)/shard_map/ppermute | solution.py:530
  25.6 4.3 %collective-permute-start.6 = (f32[2,144,256]{2,1,0:T(8,128)S(1)}, f32[2,144,256]{2,1,0:T(8,128)S(1)}, u32[]{:S(2)}, u32[]{:S(2)}) collective-permute-start(f32[2,144,256]{2,1,0:T(8,128)S(1)} %shard_map.110.mine_ref), channel_id=1, source_target_pairs={{0,1},{1,0},{2,3},{3,2},{4,5},{5,4},{6,7},{7,6},{8,9},{9,8},{10,11... | collective-permute-start | bytes 884744 | tf_op jit(solution)/shard_map/ppermute | solution.py:665
  25.7 20.4 %collective-permute-start.11 = (f32[200,256]{1,0:T(8,128)S(1)}, f32[200,256]{1,0:T(8,128)S(1)}, u32[]{:S(2)}, u32[]{:S(2)}) collective-permute-start(f32[200,256]{1,0:T(8,128)S(1)} %get-tuple-element.58), channel_id=1, source_target_pairs={{0,2},{2,4},{4,6},{6,0},{1,3},{3,5},{5,7},{7,1},{8,10},{10,12},{12... | collective-permute-start | bytes 614408 | tf_op jit(solution)/shard_map/ppermute | solution.py:530
  29.9 16.2 %collective-permute-start.12 = (f32[200,256]{1,0:T(8,128)S(1)}, f32[200,256]{1,0:T(8,128)S(1)}, u32[]{:S(2)}, u32[]{:S(2)}) collective-permute-start(f32[200,256]{1,0:T(8,128)S(1)} %get-tuple-element.59), channel_id=1, source_target_pairs={{2,0},{4,2},{6,4},{0,6},{3,1},{5,3},{7,5},{1,7},{10,8},{12,10},{14... | collective-permute-start | bytes 614408 | tf_op jit(solution)/shard_map/ppermute | solution.py:531
  30.0 11.0 %collective-permute-start.7 = (f32[2,24,256]{2,1,0:T(8,128)S(1)}, f32[2,24,256]{2,1,0:T(8,128)S(1)}, u32[]{:S(2)}, u32[]{:S(2)}) collective-permute-start(f32[2,24,256]{2,1,0:T(8,128)S(1)} %get-tuple-element.54), channel_id=1, source_target_pairs={{0,2},{2,4},{4,6},{6,0},{1,3},{3,5},{5,7},{7,1},{8,10},{10,12},{12... | collective-permute-start | bytes 147464 | tf_op jit(solution)/shard_map/ppermute | solution.py:530
  32.0 9.5 %collective-permute-start.8 = (f32[2,24,256]{2,1,0:T(8,128)S(1)}, f32[2,24,256]{2,1,0:T(8,128)S(1)}, u32[]{:S(2)}, u32[]{:S(2)}) collective-permute-start(f32[2,24,256]{2,1,0:T(8,128)S(1)} %get-tuple-element.55), channel_id=1, source_target_pairs={{2,0},{4,2},{6,4},{0,6},{3,1},{5,3},{7,5},{1,7},{10,8},{12,10},{14... | collective-permute-start | bytes 147464 | tf_op jit(solution)/shard_map/ppermute | solution.py:531
  41.9 6.1 %collective-permute-start.9 = (f32[48,256]{1,0:T(8,128)S(1)}, f32[48,256]{1,0:T(8,128)S(1)}, u32[]{:S(2)}, u32[]{:S(2)}) collective-permute-start(f32[48,256]{1,0:T(8,128)S(1)} %get-tuple-element.56), channel_id=1, source_target_pairs={{0,8},{8,16},{16,24},{24,0},{1,9},{9,17},{17,25},{25,1},{2,10},{10... | collective-permute-start | bytes 147464 | tf_op jit(solution)/shard_map/ppermute | solution.py:530
  42.5 5.5 %collective-permute-start.10 = (f32[48,256]{1,0:T(8,128)S(1)}, f32[48,256]{1,0:T(8,128)S(1)}, u32[]{:S(2)}, u32[]{:S(2)}) collective-permute-start(f32[48,256]{1,0:T(8,128)S(1)} %get-tuple-element.57), channel_id=1, source_target_pairs={{8,0},{16,8},{24,16},{0,24},{9,1},{17,9},{25,17},{1,25},{10,2},{18... | collective-permute-start | bytes 147464 | tf_op jit(solution)/shard_map/ppermute | solution.py:531

commit v6 on v5

--- a/solution.py
+++ b/solution.py
@@ -446,24 +446,24 @@
     edge_ref,
     wide_ref,
     miss_ref,
+    by_lon_ref,
 ):
     width = own_ref.shape[2]
-    rows, cols = target_ref.shape[1], target_ref.shape[2]
+    rows = target_ref.shape[1]
     span = part_ref.shape[1]
     wide_ref[...] = jnp.zeros_like(wide_ref)
-    blank = jnp.zeros((span - rows - 2 * SKIRT, cols), F32)
-    miss_ref[0, rows + 2 * SKIRT :] = blank
-    miss_ref[1, rows + 2 * SKIRT :] = blank
 
     def kept(ref):
         return ref[0], ref[1]
 
+    used = rows + 2 * SKIRT
     for level in range(2):
         part = slice(level * STRIP, (level + 1) * STRIP)
         strips = jnp.concatenate([strip_west_ref[part], strip_east_ref[part]], 0)
         wide_ref[level, :, : 2 * STRIP] = dot3(kept(lat_map_ref), strips, (1, 1))
-        wide = split(wide_ref[level])
-        increment = part_ref[level] + dot3(wide, kept(strip_map_ref))
+    for level in range(2):
+        wide = split(wide_ref[level, :used])
+        increment = part_ref[level, :used] + dot3(wide, kept(strip_map_ref))
         inc_ref[level] = increment[:rows]
         miss_ref[level, :rows] = weight_ref[level] * (increment[:rows] - target_ref[level])
         target_rows = slice(level * SKIRT, (level + 1) * SKIRT)
@@ -472,11 +472,16 @@
             start = rows + number * SKIRT
             difference = increment[start : start + SKIRT] - ref[target_rows]
             miss_ref[level, start : start + SKIRT] = ref[weight_rows] * difference
+    for level in range(2):
+        wide = split(wide_ref[level])
         beyond = beyond_ref[level] + dot3(kept(side_map_ref), wide, (1, 1))
         beyond = side_weight_ref[level] * (beyond - side_target_ref[level])
-        by_lon = dot3(miss_ref[level], kept(back_ref.at[level]))
-        by_lon = by_lon + dot3(beyond, kept(side_back_ref.at[level]), (0, 0))
-        residual = dot3(kept(lat_back_ref), by_lon)
+        back_ref_level = kept(back_ref.at[level])
+        by_lon_ref[level, :used] = dot3(miss_ref[level, :used], back_ref_level)
+        by_lon_ref[level, used:] = jnp.zeros((span - used, width + LANES), F32)
+        by_lon_ref[level] += dot3(beyond, kept(side_back_ref.at[level]), (0, 0))
+    for level in range(2):
+        residual = dot3(kept(lat_back_ref), by_lon_ref[level])
         own_ref[level] = residual[:, :width]
         edge_ref[level] = residual[:, width:]
 
@@ -715,7 +720,11 @@
         [shaped((2, fine_h, fine_w)), shaped((2, ext, width)), shaped((2, ext, LANES))],
         grant=16,
         in_specs=[whole] * 16,
-        scratch_shapes=[pltpu.VMEM((2, span, LANES), F32), pltpu.VMEM((2, span, fine_w), F32)],
+        scratch_shapes=[
+            pltpu.VMEM((2, span, LANES), F32),
+            pltpu.VMEM((2, span, fine_w), F32),
+            pltpu.VMEM((2, span, width + LANES), F32),
+        ],
     )(strip_west, strip_east, innovation, obs_weight, fine_above, fine_below, *maps)
 
     gradient = call(

time: 59.3 us -> 58.3 us (0.983)
  Pallas kernels: 22.9 us -> 21.8 us
    pallas_call x1, Pallas kernels: 3.83 us -> 2.76 us  [whole_step(): call(fine_kernel, [shaped((2, fine_h, fine_w)), shaped((2, ext, width)),...]
  transfers between devices with their start and end apart: 13 -> 13, of which waited for: 4 -> 4; matrix products, arithmetic and copies ran while one was open for 0% -> 0% of each run, Pallas kernels for 19% -> 20%
where the time goes in v6:
time: 58.3 us; the launch traced here: 58 us
  Pallas kernels  21.8 us (37%)
  starting transfers between devices  19.9 us (34%)
  waiting for transfers between devices  11.5 us (20%)
  local copies, waits for them, and re-layouts  3.86 us (7%)
  between operations  0.89 us (2%)
    ppermute x5, waiting for transfers between devices, exchange(): ahead = lax.ppermute(to_next, axis, forward)  10.1 us
    ppermute x5, starting transfers between devices, exchange(): ahead = lax.ppermute(to_next, axis, forward)  8.89 us
    pallas_call x1, Pallas kernels, whole_step(): call(gradient_kernel, shaped((fields, height, width)), grant=16, grid=(gr...  7.24 us
    ppermute x5, starting transfers between devices, exchange(): behind = lax.ppermute(to_previous, axis, backward)  7.17 us
    pallas_call x1, Pallas kernels, whole_step(): call(local_kernel, [shaped((2, height, width)), shaped((fields, 2 * HB, w...  4.47 us
    unnamed x24, local copies, waits for them, and re-layouts  3.86 us
    ppermute x1, starting transfers between devices, exchange_pairs(): ahead = lax.ppermute(to_even, axis, even)  3.1 us
    pallas_call x1, Pallas kernels, whole_step(): call(fine_kernel, [shaped((2, fine_h, fine_w)), shaped((2, ext, width)),...  2.76 us
  transfers between devices with their start and end apart: 13, of which 4 were waited for; matrix products, arithmetic and copies ran while one was open for 0% of the time, Pallas kernels for 20%

profile of v6, /device:TPU:0, one launch (start us, length us, event | category | flops | bytes accessed | tf_op | source)
XLA Modules:
  0.0 58.0 jit_solution(3766702413500826932)
XLA Ops:
  0.6 0.0 copy-start.9
  0.6 0.0 copy-start.11
  0.7 0.0 copy-start
  0.7 1.7 %copy-done = bf16[40,2,128,128]{3,2,1,0:T(8,128)(2,1)S(1)} copy-done((bf16[40,2,128,128]{3,2,1,0:T(8,128)(2,1)S(1)}, bf16[40,2,128,128]{3,2,1,0:T(8,128)(2,1)}, u32[]{:S(2)}) %copy-start) | copy-done | bytes 2621464
  2.4 0.1 shard_map.106
  2.5 0.0 copy-start.7
  2.6 0.0 copy-start.8
  2.6 3.1 %collective-permute-start.2 = (bf16[80,8,128]{2,1,0:T(8,128)(2,1)S(1)}, bf16[80,8,128]{2,1,0:T(8,128)(2,1)S(1)}, u32[]{:S(2)}, u32[]{:S(2)}) collective-permute-start(bf16[80,8,128]{2,1,0:T(8,128)(2,1)S(1)} %get-tuple-element.43), channel_id=1, source_target_pairs={{0,2},{2,0},{4,6},{6,4},{1,3},{3,1},{5,7},{7,5},{8,10},{10,8},{12,... | collective-permute-start | bytes 491528 | tf_op jit(solution)/shard_map/ppermute | solution.py:544
  5.7 0.7 %collective-permute-start.3 = (bf16[80,8,128]{2,1,0:T(8,128)(2,1)S(1)}, bf16[80,8,128]{2,1,0:T(8,128)(2,1)S(1)}, u32[]{:S(2)}, u32[]{:S(2)}) collective-permute-start(bf16[80,8,128]{2,1,0:T(8,128)(2,1)S(1)} %get-tuple-element.44), channel_id=1, source_target_pairs={{0,0},{2,4},{4,2},{6,6},{1,1},{3,5},{5,3},{7,7},{8,8},{10,12},{12,... | collective-permute-start | bytes 491528 | tf_op jit(solution)/shard_map/ppermute | solution.py:545
  6.4 0.0 copy-start.2
  6.4 1.0 %copy-done.2 = f32[2,256,256]{2,1,0:T(8,128)S(1)} copy-done((f32[2,256,256]{2,1,0:T(8,128)S(1)}, f32[2,256,256]{2,1,0:T(8,128)}, u32[]{:S(2)}) %copy-start.2) | copy-done | bytes 524312
  7.4 1.0 %copy-done.4 = f32[2,256,256]{2,1,0:T(8,128)S(1)} copy-done((f32[2,256,256]{2,1,0:T(8,128)S(1)}, f32[2,256,256]{2,1,0:T(8,128)}, u32[]{:S(2)}) %copy-start.4) | copy-done | bytes 524312
  8.4 0.3 shard_map.105
  8.8 0.0 copy-start.6
  8.8 1.5 %collective-permute-start = (f32[104,256]{1,0:T(8,128)S(1)}, f32[104,256]{1,0:T(8,128)S(1)}, u32[]{:S(2)}, u32[]{:S(2)}) collective-permute-start(f32[104,256]{1,0:T(8,128)S(1)} %get-tuple-element.41), channel_id=1, source_target_pairs={{0,8},{8,16},{16,24},{24,0},{1,9},{9,17},{17,25},{25,1},{2,10},{10... | collective-permute-start | bytes 319496 | tf_op jit(solution)/shard_map/ppermute | solution.py:535
  10.3 1.4 %collective-permute-start.1 = (f32[104,256]{1,0:T(8,128)S(1)}, f32[104,256]{1,0:T(8,128)S(1)}, u32[]{:S(2)}, u32[]{:S(2)}) collective-permute-start(f32[104,256]{1,0:T(8,128)S(1)} %get-tuple-element.42), channel_id=1, source_target_pairs={{8,0},{16,8},{24,16},{0,24},{9,1},{17,9},{25,17},{1,25},{10,2},{18... | collective-permute-start | bytes 319496 | tf_op jit(solution)/shard_map/ppermute | solution.py:536
  11.7 1.1 %shard_map.104 = (bf16[2,8,256,256]{3,2,1,0:T(8,128)(2,1)S(1)}, bf16[2,144,384]{2,1,0:T(8,128)(2,1)S(1)}) custom-call(s32[2]{0:T(128)S(1)} %copy-done.11), custom_call_target="tpu_custom_call" | custom-call | flops 100000000 | bytes 1000000 | tf_op jit(solution)/shard_map/pallas_call | solution.py:609
  12.8 0.0 collective-permute-done.2.even_ref
  12.9 0.0 collective-permute-done.3.odd_ref
  12.9 1.9 %shard_map.107 = (bf16[5,144,128]{2,1,0:T(8,128)(2,1)S(1)}, bf16[5,144,128]{2,1,0:T(8,128)(2,1)S(1)}, bf16[80,8,128]{2,1,0:T(8,128)(2,1)S(1)}, bf16[80,8,128]{2,1,0:T(8,128)(2,1)S(1)}) custom-call(bf16[80,128,128]{2,1,0:T(8,128)(2,1)S(1)} %bitcast.4, bf16[80,8,128]{2,1,0:T(8,128)(2,1)S(1)} %collective-permute-done.2.even_ref, ...), custom_call_target="tpu_custom_call" | custom-call | flops 100000000 | bytes 1000000 | tf_op jit(solution)/shard_map/pallas_call | solution.py:623
  14.8 1.6 %collective-permute-start.5 = (bf16[5,144,128]{2,1,0:T(8,128)(2,1)S(1)}, bf16[5,144,128]{2,1,0:T(8,128)(2,1)S(1)}, u32[]{:S(2)}, u32[]{:S(2)}) collective-permute-start(bf16[5,144,128]{2,1,0:T(8,128)(2,1)S(1)} %get-tuple-element.52), channel_id=1, source_target_pairs={{8,0},{16,8},{24,16},{0,24},{9,1},{17,9},{25,17},{1,25},{10,2},{18... | collective-permute-start | bytes 552968 | tf_op jit(solution)/shard_map/ppermute | solution.py:536
  16.4 0.5 collective-permute-start.4
  16.8 0.0 collective-permute-done.west_ref
  16.8 0.0 collective-permute-done.1.east_ref
  16.9 0.0 copy-done.7
  17.0 4.5 %shard_map.109 = (f32[2,128,128]{2,1,0:T(8,128)S(1)}, f32[80,16,128]{2,1,0:T(8,128)S(1)}, f32[5,2,144,128]{3,2,1,0:T(8,128)S(1)}) custom-call(bf16[80,128,128]{2,1,0:T(8,128)(2,1)S(1)} %bitcast.7, bf16[80,128,128]{2,1,0:T(8,128)(2,1)S(1)} %bitcast.5, bf16[2,8,256,256]{3,2,1,0:T(8,128)(2,1)S(1)} %get-tuple-element.39.lon_ref, ...), custom_call_target="tpu_custom_call" | custom-call | flops 10000000000 | bytes 1000000 | tf_op jit(solution)/shard_map/pallas_call | solution.py:639
  21.4 0.9 %collective-permute-done.5.east_ref = bf16[5,144,128]{2,1,0:T(8,128)(2,1)S(1)} collective-permute-done((bf16[5,144,128]{2,1,0:T(8,128)(2,1)S(1)}, bf16[5,144,128]{2,1,0:T(8,128)(2,1)S(1)}, u32[]{:S(2)}, u32[]{:S(2)}) %collective-permute-start.5) | collective-permute-done | bytes 184352 | tf_op jit(solution)/shard_map/ppermute | solution.py:536
  22.3 2.9 %collective-permute-done.4.west_ref = bf16[5,144,128]{2,1,0:T(8,128)(2,1)S(1)} collective-permute-done((bf16[5,144,128]{2,1,0:T(8,128)(2,1)S(1)}, bf16[5,144,128]{2,1,0:T(8,128)(2,1)S(1)}, u32[]{:S(2)}, u32[]{:S(2)}) %collective-permute-start.4) | collective-permute-done | bytes 184352 | tf_op jit(solution)/shard_map/ppermute | solution.py:535
  25.3 0.4 shard_map.110.mine_ref
  25.6 0.1 collective-permute-start.6
  25.7 4.2 %collective-permute-start.11 = (f32[200,256]{1,0:T(8,128)S(1)}, f32[200,256]{1,0:T(8,128)S(1)}, u32[]{:S(2)}, u32[]{:S(2)}) collective-permute-start(f32[200,256]{1,0:T(8,128)S(1)} %get-tuple-element.58), channel_id=1, source_target_pairs={{0,2},{2,4},{4,6},{6,0},{1,3},{3,5},{5,7},{7,1},{8,10},{10,12},{12... | collective-permute-start | bytes 614408 | tf_op jit(solution)/shard_map/ppermute | solution.py:535
  29.9 0.0 collective-permute-start.12
  29.9 0.0 collective-permute-done.6.other_ref
  30.0 2.1 %collective-permute-start.7 = (f32[2,24,256]{2,1,0:T(8,128)S(1)}, f32[2,24,256]{2,1,0:T(8,128)S(1)}, u32[]{:S(2)}, u32[]{:S(2)}) collective-permute-start(f32[2,24,256]{2,1,0:T(8,128)S(1)} %get-tuple-element.54), channel_id=1, source_target_pairs={{0,2},{2,4},{4,6},{6,0},{1,3},{3,5},{5,7},{7,1},{8,10},{10,12},{12... | collective-permute-start | bytes 147464 | tf_op jit(solution)/shard_map/ppermute | solution.py:535
  32.0 1.8 %collective-permute-start.8 = (f32[2,24,256]{2,1,0:T(8,128)S(1)}, f32[2,24,256]{2,1,0:T(8,128)S(1)}, u32[]{:S(2)}, u32[]{:S(2)}) collective-permute-start(f32[2,24,256]{2,1,0:T(8,128)S(1)} %get-tuple-element.55), channel_id=1, source_target_pairs={{2,0},{4,2},{6,4},{0,6},{3,1},{5,3},{7,5},{1,7},{10,8},{12,10},{14... | collective-permute-start | bytes 147464 | tf_op jit(solution)/shard_map/ppermute | solution.py:536
  33.8 7.2 %collective-permute-done.7.above_ref = f32[2,24,256]{2,1,0:T(8,128)S(1)} collective-permute-done((f32[2,24,256]{2,1,0:T(8,128)S(1)}, f32[2,24,256]{2,1,0:T(8,128)S(1)}, u32[]{:S(2)}, u32[]{:S(2)}) %collective-permute-start.7) | collective-permute-done | bytes 49184 | tf_op jit(solution)/shard_map/ppermute | solution.py:535
  41.0 0.5 collective-permute-done.8.below_ref
  41.5 0.4 shard_map.112
  41.9 0.6 %collective-permute-start.9 = (f32[48,256]{1,0:T(8,128)S(1)}, f32[48,256]{1,0:T(8,128)S(1)}, u32[]{:S(2)}, u32[]{:S(2)}) collective-permute-start(f32[48,256]{1,0:T(8,128)S(1)} %get-tuple-element.56), channel_id=1, source_target_pairs={{0,8},{8,16},{16,24},{24,0},{1,9},{9,17},{17,25},{25,1},{2,10},{10... | collective-permute-start | bytes 147464 | tf_op jit(solution)/shard_map/ppermute | solution.py:535
  42.5 2.3 %collective-permute-start.10 = (f32[48,256]{1,0:T(8,128)S(1)}, f32[48,256]{1,0:T(8,128)S(1)}, u32[]{:S(2)}, u32[]{:S(2)}) collective-permute-start(f32[48,256]{1,0:T(8,128)S(1)} %get-tuple-element.57), channel_id=1, source_target_pairs={{8,0},{16,8},{24,16},{0,24},{9,1},{17,9},{25,17},{1,25},{10,2},{18... | collective-permute-start | bytes 147464 | tf_op jit(solution)/shard_map/ppermute | solution.py:536
  44.9 1.2 %shard_map.115 = (bf16[2,8,256,256]{3,2,1,0:T(8,128)(2,1)S(1)}, bf16[2,128,432]{2,1,0:T(8,128)(2,1)S(1)}) custom-call(s32[2]{0:T(128)S(1)} %copy-done.11), custom_call_target="tpu_custom_call" | custom-call | flops 100000000 | bytes 1000000 | tf_op jit(solution)/shard_map/pallas_call | solution.py:675
  46.1 0.0 collective-permute-done.11.above_ref
  46.1 0.0 collective-permute-done.12.below_ref
  46.1 1.9 %shard_map.113 = (f32[2,384,256]{2,1,0:T(8,128)S(1)}, f32[2,48,384]{2,1,0:T(8,128)S(1)}, bf16[2,384,256]{2,1,0:T(8,128)(2,1)S(1)}, bf16[2,128,256]{2,1,0:T(8,128...) custom-call(f32[2,256,256]{2,1,0:T(8,128)S(1)} %get-tuple-element.60, ...), custom_call_target="tpu_custom_call" | custom-call | flops 100000000 | bytes 1000000 | tf_op jit(solution)/shard_map/pallas_call | solution.py:691
  48.0 0.0 collective-permute-done.9.strip_west_ref
  48.0 0.0 collective-permute-done.10.strip_east_ref
  48.0 2.8 %shard_map.114 = (f32[2,256,256]{2,1,0:T(8,128)}, f32[2,144,128]{2,1,0:T(8,128)S(1)}, f32[2,144,128]{2,1,0:T(8,128)S(1)}) custom-call(f32[48,256]{1,0:T(8,128)S(1)} %collective-permute-done.9.strip_west_ref, f32[48,256]{1,0:T(8,128)S(1)} %collective-permute-done.10.strip_east_ref, f32[2,256,256]{2,1,0:T(8,128)S(1)} %copy-done.3, ...), custom_call_target="tpu_custom_call" | custom-call | flops 100000000 | bytes 1000000 | tf_op jit(solution)/shard_map/pallas_call | solution.py:718
  50.8 7.2 %shard_map.116 = f32[80,128,128]{2,1,0:T(8,128)} custom-call(bf16[80,128,128]{2,1,0:T(8,128)(2,1)S(1)} %bitcast.8, bf16[80,128,128]{2,1,0:T(8,128)(2,1)S(1)} %bitcast.6, bf16[80,8,128]{2,1,0:T(8,128)(2,1)S(1)} %get-tuple-element.50.above_ref, bf16[80,8,128]{2,1,0:T(8,128)(2,1)S(1)} %get-tuple-element.51.below_ref, ...), custom_call_target="tpu_custom_call" | custom-call | flops 100000000 | bytes 1000000 | tf_op jit(solution)/shard_map/pallas_call | solution.py:730
  (15 shorter events, 0.1 us)
Async XLA Ops:
  0.6 5.7 %copy-start.9 = (s32[256]{0:T(256)S(1)}, s32[256]{0:T(256)}, u32[]{:S(2)}) copy-start(s32[256]{0:T(256)} %lon_index_ref.1) | copy-start | bytes 3076
  0.6 11.1 %copy-start.11 = (s32[2]{0:T(128)S(1)}, s32[2]{0:T(128)}, u32[]{:S(2)}) copy-start(s32[2]{0:T(128)} %width_ref.3) | copy-start | bytes 28
  0.7 1.8 %copy-start = (bf16[40,2,128,128]{3,2,1,0:T(8,128)(2,1)S(1)}, bf16[40,2,128,128]{3,2,1,0:T(8,128)(2,1)}, u32[]{:S(2)}) copy-start(bf16[40,2,128,128]{3,2,1,0:T(8,128)(2,1)} %param.10) | copy-start | bytes 7864324
  2.4 3.9 %copy-start.10 = (f32[256]{0:T(256)S(1)}, f32[256]{0:T(256)}, u32[]{:S(2)}) copy-start(f32[256]{0:T(256)} %lon_share_ref.1) | copy-start | bytes 3076
  2.4 10.5 %copy-start.1 = (bf16[40,2,128,128]{3,2,1,0:T(8,128)(2,1)S(1)}, bf16[40,2,128,128]{3,2,1,0:T(8,128)(2,1)}, u32[]{:S(2)}) copy-start(bf16[40,2,128,128]{3,2,1,0:T(8,128)(2,1)} %param.10) | copy-start | bytes 7864324
  2.5 14.3 %copy-start.7 = (s32[256]{0:T(256)S(1)}, s32[256]{0:T(256)}, u32[]{:S(2)}) copy-start(s32[256]{0:T(256)} %lat_index_ref.1) | copy-start | bytes 3076
  2.6 14.3 %copy-start.8 = (f32[256]{0:T(256)S(1)}, f32[256]{0:T(256)}, u32[]{:S(2)}) copy-start(f32[256]{0:T(256)} %lat_share_ref.1) | copy-start | bytes 3076
  2.6 10.3 %collective-permute-start.2 = (bf16[80,8,128]{2,1,0:T(8,128)(2,1)S(1)}, bf16[80,8,128]{2,1,0:T(8,128)(2,1)S(1)}, u32[]{:S(2)}, u32[]{:S(2)}) collective-permute-start(bf16[80,8,128]{2,1,0:T(8,128)(2,1)S(1)} %get-tuple-element.43), channel_id=1, source_target_pairs={{0,2},{2,0},{4,6},{6,4},{1,3},{3,1},{5,7},{7,5},{8,10},{10,8},{12,... | collective-permute-start | bytes 491528 | tf_op jit(solution)/shard_map/ppermute | solution.py:544
  5.7 7.2 %collective-permute-start.3 = (bf16[80,8,128]{2,1,0:T(8,128)(2,1)S(1)}, bf16[80,8,128]{2,1,0:T(8,128)(2,1)S(1)}, u32[]{:S(2)}, u32[]{:S(2)}) collective-permute-start(bf16[80,8,128]{2,1,0:T(8,128)(2,1)S(1)} %get-tuple-element.44), channel_id=1, source_target_pairs={{0,0},{2,4},{4,2},{6,6},{1,1},{3,5},{5,3},{7,7},{8,8},{10,12},{12,... | collective-permute-start | bytes 491528 | tf_op jit(solution)/shard_map/ppermute | solution.py:545
  6.4 1.0 %copy-start.2 = (f32[2,256,256]{2,1,0:T(8,128)S(1)}, f32[2,256,256]{2,1,0:T(8,128)}, u32[]{:S(2)}) copy-start(f32[2,256,256]{2,1,0:T(8,128)} %target_ref.5) | copy-start | bytes 1572868
  7.4 1.0 %copy-start.4 = (f32[2,256,256]{2,1,0:T(8,128)S(1)}, f32[2,256,256]{2,1,0:T(8,128)}, u32[]{:S(2)}) copy-start(f32[2,256,256]{2,1,0:T(8,128)} %weight_ref.5) | copy-start | bytes 1572868
  8.4 8.4 %copy-start.3 = (f32[2,256,256]{2,1,0:T(8,128)S(1)}, f32[2,256,256]{2,1,0:T(8,128)}, u32[]{:S(2)}) copy-start(f32[2,256,256]{2,1,0:T(8,128)} %target_ref.5) | copy-start | bytes 1572868
  8.4 8.4 %copy-start.5 = (f32[2,256,256]{2,1,0:T(8,128)S(1)}, f32[2,256,256]{2,1,0:T(8,128)}, u32[]{:S(2)}) copy-start(f32[2,256,256]{2,1,0:T(8,128)} %weight_ref.5) | copy-start | bytes 1572868
  8.8 8.2 %copy-start.6 = (bf16[40,2,128,128]{3,2,1,0:T(8,128)(2,1)S(1)}, bf16[40,2,128,128]{3,2,1,0:T(8,128)(2,1)}, u32[]{:S(2)}) copy-start(bf16[40,2,128,128]{3,2,1,0:T(8,128)(2,1)} %param.9) | copy-start | bytes 7864324
  8.8 8.1 %collective-permute-start = (f32[104,256]{1,0:T(8,128)S(1)}, f32[104,256]{1,0:T(8,128)S(1)}, u32[]{:S(2)}, u32[]{:S(2)}) collective-permute-start(f32[104,256]{1,0:T(8,128)S(1)} %get-tuple-element.41), channel_id=1, source_target_pairs={{0,8},{8,16},{16,24},{24,0},{1,9},{9,17},{17,25},{25,1},{2,10},{10... | collective-permute-start | bytes 319496 | tf_op jit(solution)/shard_map/ppermute | solution.py:535
  10.3 6.5 %collective-permute-start.1 = (f32[104,256]{1,0:T(8,128)S(1)}, f32[104,256]{1,0:T(8,128)S(1)}, u32[]{:S(2)}, u32[]{:S(2)}) collective-permute-start(f32[104,256]{1,0:T(8,128)S(1)} %get-tuple-element.42), channel_id=1, source_target_pairs={{8,0},{16,8},{24,16},{0,24},{9,1},{17,9},{25,17},{1,25},{10,2},{18... | collective-permute-start | bytes 319496 | tf_op jit(solution)/shard_map/ppermute | solution.py:536
  14.8 7.6 %collective-permute-start.5 = (bf16[5,144,128]{2,1,0:T(8,128)(2,1)S(1)}, bf16[5,144,128]{2,1,0:T(8,128)(2,1)S(1)}, u32[]{:S(2)}, u32[]{:S(2)}) collective-permute-start(bf16[5,144,128]{2,1,0:T(8,128)(2,1)S(1)} %get-tuple-element.52), channel_id=1, source_target_pairs={{8,0},{16,8},{24,16},{0,24},{9,1},{17,9},{25,17},{1,25},{10,2},{18... | collective-permute-start | bytes 552968 | tf_op jit(solution)/shard_map/ppermute | solution.py:536
  16.4 8.9 %collective-permute-start.4 = (bf16[5,144,128]{2,1,0:T(8,128)(2,1)S(1)}, bf16[5,144,128]{2,1,0:T(8,128)(2,1)S(1)}, u32[]{:S(2)}, u32[]{:S(2)}) collective-permute-start(bf16[5,144,128]{2,1,0:T(8,128)(2,1)S(1)} %get-tuple-element.45.order_ref), channel_id=1, source_target_pairs={{0,8},{8,16},{16,24},{24,0},{1,9},{9,17},{17,25},{25,1},{2,10},{10... | collective-permute-start | bytes 552968 | tf_op jit(solution)/shard_map/ppermute | solution.py:535
  25.6 4.3 %collective-permute-start.6 = (f32[2,144,256]{2,1,0:T(8,128)S(1)}, f32[2,144,256]{2,1,0:T(8,128)S(1)}, u32[]{:S(2)}, u32[]{:S(2)}) collective-permute-start(f32[2,144,256]{2,1,0:T(8,128)S(1)} %shard_map.110.mine_ref), channel_id=1, source_target_pairs={{0,1},{1,0},{2,3},{3,2},{4,5},{5,4},{6,7},{7,6},{8,9},{9,8},{10,11... | collective-permute-start | bytes 884744 | tf_op jit(solution)/shard_map/ppermute | solution.py:670
  25.7 20.4 %collective-permute-start.11 = (f32[200,256]{1,0:T(8,128)S(1)}, f32[200,256]{1,0:T(8,128)S(1)}, u32[]{:S(2)}, u32[]{:S(2)}) collective-permute-start(f32[200,256]{1,0:T(8,128)S(1)} %get-tuple-element.58), channel_id=1, source_target_pairs={{0,2},{2,4},{4,6},{6,0},{1,3},{3,5},{5,7},{7,1},{8,10},{10,12},{12... | collective-permute-start | bytes 614408 | tf_op jit(solution)/shard_map/ppermute | solution.py:535
  29.9 16.2 %collective-permute-start.12 = (f32[200,256]{1,0:T(8,128)S(1)}, f32[200,256]{1,0:T(8,128)S(1)}, u32[]{:S(2)}, u32[]{:S(2)}) collective-permute-start(f32[200,256]{1,0:T(8,128)S(1)} %get-tuple-element.59), channel_id=1, source_target_pairs={{2,0},{4,2},{6,4},{0,6},{3,1},{5,3},{7,5},{1,7},{10,8},{12,10},{14... | collective-permute-start | bytes 614408 | tf_op jit(solution)/shard_map/ppermute | solution.py:536
  30.0 11.0 %collective-permute-start.7 = (f32[2,24,256]{2,1,0:T(8,128)S(1)}, f32[2,24,256]{2,1,0:T(8,128)S(1)}, u32[]{:S(2)}, u32[]{:S(2)}) collective-permute-start(f32[2,24,256]{2,1,0:T(8,128)S(1)} %get-tuple-element.54), channel_id=1, source_target_pairs={{0,2},{2,4},{4,6},{6,0},{1,3},{3,5},{5,7},{7,1},{8,10},{10,12},{12... | collective-permute-start | bytes 147464 | tf_op jit(solution)/shard_map/ppermute | solution.py:535
  32.0 9.5 %collective-permute-start.8 = (f32[2,24,256]{2,1,0:T(8,128)S(1)}, f32[2,24,256]{2,1,0:T(8,128)S(1)}, u32[]{:S(2)}, u32[]{:S(2)}) collective-permute-start(f32[2,24,256]{2,1,0:T(8,128)S(1)} %get-tuple-element.55), channel_id=1, source_target_pairs={{2,0},{4,2},{6,4},{0,6},{3,1},{5,3},{7,5},{1,7},{10,8},{12,10},{14... | collective-permute-start | bytes 147464 | tf_op jit(solution)/shard_map/ppermute | solution.py:536
  41.9 6.1 %collective-permute-start.9 = (f32[48,256]{1,0:T(8,128)S(1)}, f32[48,256]{1,0:T(8,128)S(1)}, u32[]{:S(2)}, u32[]{:S(2)}) collective-permute-start(f32[48,256]{1,0:T(8,128)S(1)} %get-tuple-element.56), channel_id=1, source_target_pairs={{0,8},{8,16},{16,24},{24,0},{1,9},{9,17},{17,25},{25,1},{2,10},{10... | collective-permute-start | bytes 147464 | tf_op jit(solution)/shard_map/ppermute | solution.py:535
  42.5 5.5 %collective-permute-start.10 = (f32[48,256]{1,0:T(8,128)S(1)}, f32[48,256]{1,0:T(8,128)S(1)}, u32[]{:S(2)}, u32[]{:S(2)}) collective-permute-start(f32[48,256]{1,0:T(8,128)S(1)} %get-tuple-element.57), channel_id=1, source_target_pairs={{8,0},{16,8},{24,16},{0,24},{9,1},{17,9},{25,17},{1,25},{10,2},{18... | collective-permute-start | bytes 147464 | tf_op jit(solution)/shard_map/ppermute | solution.py:536
